TPU v7x, 256 devices: a whole 4x4x8 slice. The times are simulated.
256 devices in a mesh: dp: 64 (over z, x, core), rank: 4 (over y).
Axes of the slice: x: 4, y: 4, z: 8, core: 2. Of those that a mesh axis runs over, the one named last changes fastest.
Arguments:
- q_nope: bfloat16 [256, 2048], P('dp'), may hold values from -6 to 6
- q_rope: bfloat16 [256, 1024], P('dp'), may hold values from -40 to 40
- latent_cache: bfloat16 [256, 4096, 512], P('dp', None, 'rank'), may hold values from -6 to 6
- rope_keys: bfloat16 [256, 64, 4096], P('dp', 'rank'), may hold values from -40 to 40
- lengths: int32 [256], P('dp'), may hold values from 1 to 4096, as said below
- slot_of: int32 [256], replicated, may hold values from 0 to 255, as said below
- w_uk: bfloat16 [16, 128, 512], P(None, None, 'rank'), may hold values from -0.5 to 0.5
- w_uv: bfloat16 [16, 512, 128], P(None, 'rank'), may hold values from -1 to 1
- w_out: bfloat16 [2048, 2048], P(None, 'rank'), may hold values from -0.125 to 0.125
Outputs:
- attended: bfloat16 [256, 2048], P('dp', 'rank')
Inputs may be any that keep to these rules, and one draw needn't show every extreme that they name: Cache slot j holds lengths[j] live positions, 0 to lengths[j] - 1; some slot holds 4096. `slot_of`: each cache slot belongs to exactly one batch row.
All inputs are finite; a program needn't handle non-finite values.
Results may differ from a plain program's by a relative error of at most 0.014.
Values may be sent and summed in bfloat16 or wider, within the bound.
No kernel may reach another device: no remote copies, remote signals or barrier semaphores. Data moves between devices by JAX's collectives and lax.ppermute only.
A program may use at most 64 MiB of HBM per device.

v0:
```python
import math

import jax
import jax.numpy as jnp
from jax import lax
from jax.sharding import PartitionSpec as P

BLOCK = 512


def sent_together(arrays, axis, dim, along):
    both = jnp.concatenate(arrays, axis=along)
    filled, at, gathered = (lax.all_gather(both, axis, axis=dim, tiled=True), 0, [])
    for a in arrays:
        gathered.append(lax.slice_in_dim(filled, at, at + a.shape[along], axis=along))
        at += a.shape[along]
    return tuple(gathered)


def split_up(array, dim, count):
    before, after = (array.shape[:dim], array.shape[dim + 1 :])
    return jnp.moveaxis(array.reshape(*before, count, -1, *after), dim, 0)


def summed_on_arrival(array, axis, dim):
    blocks = split_up(array, dim, lax.axis_size(axis))
    arrived = lax.all_to_all(blocks, axis, split_axis=0, concat_axis=0, tiled=True)
    return arrived.sum(axis=0)


def joined_along(blocks, dim):
    lengths = list(blocks.shape[1:])
    lengths[dim] *= blocks.shape[0]
    return jnp.moveaxis(blocks, 0, dim).reshape(lengths)


def copy_for_each(array, axis):
    copies = jnp.broadcast_to(array, (lax.axis_size(axis), *array.shape))
    return lax.all_to_all(copies, axis, split_axis=0, concat_axis=0, tiled=True)


def collect(array, axis, dim):
    return joined_along(copy_for_each(array, axis), dim)


def over_copies(array, axis):
    everything = copy_for_each(array, axis)
    return jnp.sum(everything.astype(jnp.float32), axis=0)


def pick_rows(chooser, shard_rows):
    return jnp.dot(chooser, shard_rows, preferred_element_type=jnp.float32)


def softmax_rows(score_board, lengths):
    positions = jnp.arange(score_board.shape[2], dtype=jnp.int32)
    live_mask = positions[None, None, :] < lengths[:, None, None]
    scores = jnp.where(live_mask, score_board, -jnp.inf)
    row_max = jnp.max(scores, axis=2, keepdims=True)
    raised = jnp.exp(scores - row_max)
    return (raised / jnp.sum(raised, axis=2, keepdims=True)).astype(jnp.bfloat16)


def per_device(q_nope, q_rope, latent_cache, rope_keys, lengths, slot_of, w_uk, w_uv, w_out):
    seq_count = q_nope.shape[0]
    head_count = w_uk.shape[0]
    nope_dim = w_uk.shape[1]
    lat_part = w_uk.shape[2]
    rope_part = rope_keys.shape[1]
    rope_dim = q_rope.shape[1] // head_count
    capacity = latent_cache.shape[1]
    value_dim = w_uv.shape[2]
    seq_total = slot_of.shape[0]
    score_scale = 1.0 / math.sqrt(nope_dim + rope_dim)
    rank_pos = lax.axis_index("rank")
    data_pos = lax.axis_index("dp")
    my_slots = data_pos * seq_count + jnp.arange(seq_count, dtype=jnp.int32)
    slot_pick = (slot_of[None, :] == my_slots[:, None]).astype(jnp.bfloat16)
    my_targets = lax.dynamic_slice_in_dim(slot_of, data_pos * seq_count, seq_count)
    batch_pick = (my_targets[:, None] == jnp.arange(seq_total, dtype=jnp.int32)[None, :]).astype(
        jnp.bfloat16
    )
    shaped = q_nope.reshape(q_nope.shape[0], head_count, nope_dim)
    own_lat = (
        jnp.einsum("shn,hnl->shl", shaped, w_uk, preferred_element_type=jnp.float32)
        .astype(jnp.bfloat16)
        .reshape(seq_count, head_count * lat_part)
    )
    shaped = q_rope.reshape(q_rope.shape[0], head_count, rope_dim)
    own_rope = lax.dynamic_slice_in_dim(shaped, rank_pos * rope_part, rope_part, 2).reshape(
        seq_count, head_count * rope_part
    )
    pieces = sent_together((own_lat, own_rope), "dp", 0, 1)
    lat_sums = pick_rows(slot_pick, pieces[0])
    rope_sums = pick_rows(slot_pick, pieces[1])
    query_lat = lat_sums.astype(jnp.bfloat16).reshape(seq_count, head_count, lat_part)
    query_rope = rope_sums.astype(jnp.bfloat16).reshape(seq_count, head_count, rope_part)
    block_steps = capacity // BLOCK

    def partial_scores(block_index):
        block_start = block_index * BLOCK
        cache_block = lax.dynamic_slice_in_dim(latent_cache, block_start, BLOCK, 1)
        key_block = lax.dynamic_slice_in_dim(rope_keys, block_start, BLOCK, 2)
        lat_term = jnp.einsum(
            "shl,stl->sht", query_lat, cache_block, preferred_element_type=jnp.float32
        )
        rope_term = jnp.einsum(
            "she,set->sht", query_rope, key_block, preferred_element_type=jnp.float32
        )
        return (lat_term + rope_term) * score_scale

    head_share = head_count // lax.axis_size("rank")

    def fill_board(block_index, score_board):
        summed = summed_on_arrival(partial_scores(block_index), "rank", 1)
        return lax.dynamic_update_slice_in_dim(score_board, summed, block_index * BLOCK, 2)

    score_board = lax.fori_loop(
        0, block_steps, fill_board, jnp.zeros((seq_count, head_share, capacity), jnp.float32)
    )
    own_weights = softmax_rows(score_board, lengths)
    weights = collect(own_weights, "rank", 1)

    def add_values(block_index, running):
        block_start = block_index * BLOCK
        cache_block = lax.dynamic_slice_in_dim(latent_cache, block_start, BLOCK, 1)
        weight_block = lax.dynamic_slice_in_dim(weights, block_start, BLOCK, 2)
        return running + jnp.einsum(
            "sht,stl->shl", weight_block, cache_block, preferred_element_type=jnp.float32
        )

    latent_out = lax.fori_loop(
        0, block_steps, add_values, jnp.zeros((seq_count, head_count, lat_part), jnp.float32)
    ).astype(jnp.bfloat16)
    value_part = jnp.einsum(
        "shl,hlv->shv", latent_out, w_uv, preferred_element_type=jnp.float32
    ).reshape(seq_count, head_count * value_dim)
    head_values = (
        over_copies(value_part.astype(jnp.bfloat16), "rank")
        .astype(jnp.float32)
        .astype(jnp.bfloat16)
    )
    out_rows = jnp.dot(head_values, w_out, preferred_element_type=jnp.float32).astype(jnp.bfloat16)
    returned = pick_rows(batch_pick, collect(out_rows, "dp", 0))
    return returned.astype(jnp.bfloat16)


def solution(mesh):
    placed = (
        P("dp", None),
        P("dp", None),
        P("dp", None, "rank"),
        P("dp", "rank", None),
        P("dp"),
        P(),
        P(None, None, "rank"),
        P(None, "rank", None),
        P(None, "rank"),
    )
    return jax.shard_map(
        per_device, mesh=mesh, in_specs=placed, out_specs=P("dp", "rank"), check_vma=False
    )
```

profile of v0, /device:TPU:1, one launch (start us, length us, event | category | flops | bytes accessed | tf_op | source)
XLA Modules:
  0.0 254.4 jit_solution(13739675998776277527)
XLA Ops:
  7.7 1.3 fusion.14
  10.4 80.7 %all-gather.3.cloned.1.call-done = bf16[64,4,2304]{2,1,0:T(4,128)(2,1)} async-done(((bf16[1,4,2304]{2,1,0:T(4,128)(2,1)}), bf16[64,4,2304]{2,1,0:T(4,128)(2,1)}) %all-gather.3.cloned.1.call-update) | async-done | bytes 1179664 | tf_op jit(solution)/shard_map/all_gather | solution.py:13
  91.0 2.4 reshape.71
  94.0 90.1 %while.27 = (s32[]{:T(128)}, f32[4,4,4096]{2,1,0:T(4,128)S(1)}, bf16[4,4096,128]{2,1,0:T(8,128)(2,1)}, bf16[4,16,128]{2,1,0:T(8,128)(2,1)S(1)}, bf16[4,16,4096]{...) while((s32[]{:T(128)}, f32[4,4,4096]{2,1,0:T(4,128)S(1)}, ...), condition=%wide.region_2.0_spmd, body=%wide.region_0.0_spmd.sunk | while | flops 9527302 | bytes 2148555 | solution.py:118
  94.0 1.0 fusion.51
  95.0 1.3 fusion.52
  97.0 4.0 %all-to-all-start = ((f32[4,4,4,512]{3,2,1,0:T(4,128)}), f32[4,4,4,512]{3,2,1,0:T(4,128)S(1)}, u32[]{:S(2)}, u32[]{:S(2)}) async-start(f32[4,4,4,512]{3,2,1,0:T(4,128)} %bitcast.39), calls=%async_computation | async-start | bytes 262144 | tf_op jit(solution)/shard_map/while/body/eval_jaxpr/all_to_all | solution.py:27
  101.0 4.8 %all-to-all-done = f32[4,4,4,512]{3,2,1,0:T(4,128)S(1)} async-done(((f32[4,4,4,512]{3,2,1,0:T(4,128)}), f32[4,4,4,512]{3,2,1,0:T(4,128)S(1)}, u32[]{:S(2)}, u32[]{:S(2)}) %all-to-all-start) | async-done | bytes 131104 | tf_op jit(solution)/shard_map/while/body/eval_jaxpr/all_to_all | solution.py:27
  105.9 1.0 fusion.51
  106.9 1.3 fusion.52
  108.9 3.3 %all-to-all-start = ((f32[4,4,4,512]{3,2,1,0:T(4,128)}), f32[4,4,4,512]{3,2,1,0:T(4,128)S(1)}, u32[]{:S(2)}, u32[]{:S(2)}) async-start(f32[4,4,4,512]{3,2,1,0:T(4,128)} %bitcast.39), calls=%async_computation | async-start | bytes 262144 | tf_op jit(solution)/shard_map/while/body/eval_jaxpr/all_to_all | solution.py:27
  112.2 4.8 %all-to-all-done = f32[4,4,4,512]{3,2,1,0:T(4,128)S(1)} async-done(((f32[4,4,4,512]{3,2,1,0:T(4,128)}), f32[4,4,4,512]{3,2,1,0:T(4,128)S(1)}, u32[]{:S(2)}, u32[]{:S(2)}) %all-to-all-start) | async-done | bytes 131104 | tf_op jit(solution)/shard_map/while/body/eval_jaxpr/all_to_all | solution.py:27
  117.1 1.0 fusion.51
  118.0 1.3 fusion.52
  120.0 3.3 %all-to-all-start = ((f32[4,4,4,512]{3,2,1,0:T(4,128)}), f32[4,4,4,512]{3,2,1,0:T(4,128)S(1)}, u32[]{:S(2)}, u32[]{:S(2)}) async-start(f32[4,4,4,512]{3,2,1,0:T(4,128)} %bitcast.39), calls=%async_computation | async-start | bytes 262144 | tf_op jit(solution)/shard_map/while/body/eval_jaxpr/all_to_all | solution.py:27
  123.4 4.8 %all-to-all-done = f32[4,4,4,512]{3,2,1,0:T(4,128)S(1)} async-done(((f32[4,4,4,512]{3,2,1,0:T(4,128)}), f32[4,4,4,512]{3,2,1,0:T(4,128)S(1)}, u32[]{:S(2)}, u32[]{:S(2)}) %all-to-all-start) | async-done | bytes 131104 | tf_op jit(solution)/shard_map/while/body/eval_jaxpr/all_to_all | solution.py:27
  128.2 1.0 fusion.51
  129.2 1.3 fusion.52
  131.2 3.3 %all-to-all-start = ((f32[4,4,4,512]{3,2,1,0:T(4,128)}), f32[4,4,4,512]{3,2,1,0:T(4,128)S(1)}, u32[]{:S(2)}, u32[]{:S(2)}) async-start(f32[4,4,4,512]{3,2,1,0:T(4,128)} %bitcast.39), calls=%async_computation | async-start | bytes 262144 | tf_op jit(solution)/shard_map/while/body/eval_jaxpr/all_to_all | solution.py:27
  134.5 4.8 %all-to-all-done = f32[4,4,4,512]{3,2,1,0:T(4,128)S(1)} async-done(((f32[4,4,4,512]{3,2,1,0:T(4,128)}), f32[4,4,4,512]{3,2,1,0:T(4,128)S(1)}, u32[]{:S(2)}, u32[]{:S(2)}) %all-to-all-start) | async-done | bytes 131104 | tf_op jit(solution)/shard_map/while/body/eval_jaxpr/all_to_all | solution.py:27
  140.4 1.3 fusion.52
  142.4 3.3 %all-to-all-start = ((f32[4,4,4,512]{3,2,1,0:T(4,128)}), f32[4,4,4,512]{3,2,1,0:T(4,128)S(1)}, u32[]{:S(2)}, u32[]{:S(2)}) async-start(f32[4,4,4,512]{3,2,1,0:T(4,128)} %bitcast.39), calls=%async_computation | async-start | bytes 262144 | tf_op jit(solution)/shard_map/while/body/eval_jaxpr/all_to_all | solution.py:27
  145.7 4.8 %all-to-all-done = f32[4,4,4,512]{3,2,1,0:T(4,128)S(1)} async-done(((f32[4,4,4,512]{3,2,1,0:T(4,128)}), f32[4,4,4,512]{3,2,1,0:T(4,128)S(1)}, u32[]{:S(2)}, u32[]{:S(2)}) %all-to-all-start) | async-done | bytes 131104 | tf_op jit(solution)/shard_map/while/body/eval_jaxpr/all_to_all | solution.py:27
  150.6 1.0 fusion.51
  151.5 1.3 fusion.52
  153.6 3.3 %all-to-all-start = ((f32[4,4,4,512]{3,2,1,0:T(4,128)}), f32[4,4,4,512]{3,2,1,0:T(4,128)S(1)}, u32[]{:S(2)}, u32[]{:S(2)}) async-start(f32[4,4,4,512]{3,2,1,0:T(4,128)} %bitcast.39), calls=%async_computation | async-start | bytes 262144 | tf_op jit(solution)/shard_map/while/body/eval_jaxpr/all_to_all | solution.py:27
  156.9 4.8 %all-to-all-done = f32[4,4,4,512]{3,2,1,0:T(4,128)S(1)} async-done(((f32[4,4,4,512]{3,2,1,0:T(4,128)}), f32[4,4,4,512]{3,2,1,0:T(4,128)S(1)}, u32[]{:S(2)}, u32[]{:S(2)}) %all-to-all-start) | async-done | bytes 131104 | tf_op jit(solution)/shard_map/while/body/eval_jaxpr/all_to_all | solution.py:27
  162.7 1.3 fusion.52
  164.7 3.3 %all-to-all-start = ((f32[4,4,4,512]{3,2,1,0:T(4,128)}), f32[4,4,4,512]{3,2,1,0:T(4,128)S(1)}, u32[]{:S(2)}, u32[]{:S(2)}) async-start(f32[4,4,4,512]{3,2,1,0:T(4,128)} %bitcast.39), calls=%async_computation | async-start | bytes 262144 | tf_op jit(solution)/shard_map/while/body/eval_jaxpr/all_to_all | solution.py:27
  168.1 4.8 %all-to-all-done = f32[4,4,4,512]{3,2,1,0:T(4,128)S(1)} async-done(((f32[4,4,4,512]{3,2,1,0:T(4,128)}), f32[4,4,4,512]{3,2,1,0:T(4,128)S(1)}, u32[]{:S(2)}, u32[]{:S(2)}) %all-to-all-start) | async-done | bytes 131104 | tf_op jit(solution)/shard_map/while/body/eval_jaxpr/all_to_all | solution.py:27
  173.9 1.3 fusion.52
  175.9 3.3 %all-to-all-start = ((f32[4,4,4,512]{3,2,1,0:T(4,128)}), f32[4,4,4,512]{3,2,1,0:T(4,128)S(1)}, u32[]{:S(2)}, u32[]{:S(2)}) async-start(f32[4,4,4,512]{3,2,1,0:T(4,128)} %bitcast.39), calls=%async_computation | async-start | bytes 262144 | tf_op jit(solution)/shard_map/while/body/eval_jaxpr/all_to_all | solution.py:27
  179.2 4.8 %all-to-all-done = f32[4,4,4,512]{3,2,1,0:T(4,128)S(1)} async-done(((f32[4,4,4,512]{3,2,1,0:T(4,128)}), f32[4,4,4,512]{3,2,1,0:T(4,128)S(1)}, u32[]{:S(2)}, u32[]{:S(2)}) %all-to-all-start) | async-done | bytes 131104 | tf_op jit(solution)/shard_map/while/body/eval_jaxpr/all_to_all | solution.py:27
  184.5 1.0 broadcast_in_dim.39
  185.5 3.5 %all-to-all-start.1 = ((bf16[4,4,4,4096]{3,2,1,0:T(4,128)(2,1)}), bf16[4,4,4,4096]{3,2,1,0:T(4,128)(2,1)S(1)}, u32[]{:S(2)}, u32[]{:S(2)}) async-start(bf16[4,4,4,4096]{3,2,1,0:T(4,128)(2,1)} %broadcast_in_dim.39), calls=%async_computation.1 | async-start | bytes 1048576 | tf_op jit(solution)/shard_map/all_to_all | solution.py:39
  189.0 6.9 %all-to-all-done.1 = bf16[4,4,4,4096]{3,2,1,0:T(4,128)(2,1)S(1)} async-done(((bf16[4,4,4,4096]{3,2,1,0:T(4,128)(2,1)}), bf16[4,4,4,4096]{3,2,1,0:T(4,128)(2,1)S(1)}, u32[]{:S(2)}, u32[]{:S(2)}) %all-to-all-start.1) | async-done | bytes 524320 | tf_op jit(solution)/shard_map/all_to_all | solution.py:39
  196.3 10.4 %while.28 = (s32[]{:T(128)}, f32[4,16,128]{2,1,0:T(8,128)S(1)}, bf16[4,16,4096]{2,0,1:T(4,128)(2,1)S(1)}, bf16[4,4096,128]{2,1,0:T(8,128)(2,1)}, s32[]{:T(128)}, /*index=5*/s32[]{:T(128)}, s32[]{:T(128)}, s32[]{:T(128)}) while((s32[]{:T(128)}, f32[4,16,128]{2,1,0:T(8,128)S(1)}, bf16[4,16,4096]{2,0,1:T(4,128)(2,1)S(1)}, ...), condition=%wide.region_6.7_spmd.clone, body=%wide.region_5.6_spmd.clone.sunk | while | flops 8404999 | bytes 786581 | solution.py:132
  196.4 1.3 convolution_add_fusion.3
  197.7 1.2 convolution_add_fusion.3
  199.0 1.2 convolution_add_fusion.3
  200.3 1.2 convolution_add_fusion.3
  201.6 1.2 convolution_add_fusion.3
  202.9 1.2 convolution_add_fusion.3
  204.2 1.2 convolution_add_fusion.3
  205.5 1.2 convolution_add_fusion.3
  207.1 6.8 %all_to_all.25 = bf16[4,4,2048]{2,1,0:T(4,128)(2,1)S(1)} all-to-all(bf16[4,4,2048]{2,1,0:T(4,128)(2,1)S(1)} %broadcast_in_dim.40), channel_id=1, replica_groups=mesh['dp'=64,'rank'=4] {'rank'}, dimensions={0} | all-to-all | bytes 131072 | tf_op jit(solution)/shard_map/all_to_all | solution.py:39
  215.1 18.5 %all-to-all-start.3 = ((bf16[64,4,512]{2,1,0:T(4,128)(2,1)}), bf16[64,4,512]{2,1,0:T(4,128)(2,1)S(1)}, u32[]{:S(2)}, u32[]{:S(2)}) async-start(bf16[64,4,512]{2,1,0:T(4,128)(2,1)} %broadcast_in_dim.41), calls=%async_computation.3 | async-start | bytes 524288 | tf_op jit(solution)/shard_map/all_to_all | solution.py:39
  233.8 13.0 %all-to-all-done.3 = bf16[64,4,512]{2,1,0:T(4,128)(2,1)S(1)} async-done(((bf16[64,4,512]{2,1,0:T(4,128)(2,1)}), bf16[64,4,512]{2,1,0:T(4,128)(2,1)S(1)}, u32[]{:S(2)}, u32[]{:S(2)}) %all-to-all-start.3) | async-done | bytes 262176 | tf_op jit(solution)/shard_map/all_to_all | solution.py:39
  (75 shorter events, 15.5 us)
Async XLA Ops:
  6.5 207.4 %copy-start = (bf16[2048,512]{1,0:T(8,128)(2,1)S(1)}, bf16[2048,512]{1,0:T(8,128)(2,1)}, u32[]{:S(2)}) copy-start(bf16[2048,512]{1,0:T(8,128)(2,1)} %param.21) | copy-start | bytes 6291460
  6.5 86.8 %copy-start.2 = (s32[256]{0:T(256)S(1)}, s32[256]{0:T(256)}, u32[]{:S(2)}) copy-start(s32[256]{0:T(256)} %param.18) | copy-start | bytes 3076
  6.5 84.5 %all-gather.3.cloned.1.call-start = ((), (), s32[]{:S(2)}) async-start(), calls=%async_computation.4 | async-start | bytes 1198080 | tf_op jit(solution)/shard_map/all_gather | solution.py:13
  97.0 8.8 %all-to-all-start = ((f32[4,4,4,512]{3,2,1,0:T(4,128)}), f32[4,4,4,512]{3,2,1,0:T(4,128)S(1)}, u32[]{:S(2)}, u32[]{:S(2)}) async-start(f32[4,4,4,512]{3,2,1,0:T(4,128)} %bitcast.39), calls=%async_computation | async-start | bytes 262144 | tf_op jit(solution)/shard_map/while/body/eval_jaxpr/all_to_all | solution.py:27
  108.9 8.1 %all-to-all-start = ((f32[4,4,4,512]{3,2,1,0:T(4,128)}), f32[4,4,4,512]{3,2,1,0:T(4,128)S(1)}, u32[]{:S(2)}, u32[]{:S(2)}) async-start(f32[4,4,4,512]{3,2,1,0:T(4,128)} %bitcast.39), calls=%async_computation | async-start | bytes 262144 | tf_op jit(solution)/shard_map/while/body/eval_jaxpr/all_to_all | solution.py:27
  120.0 8.1 %all-to-all-start = ((f32[4,4,4,512]{3,2,1,0:T(4,128)}), f32[4,4,4,512]{3,2,1,0:T(4,128)S(1)}, u32[]{:S(2)}, u32[]{:S(2)}) async-start(f32[4,4,4,512]{3,2,1,0:T(4,128)} %bitcast.39), calls=%async_computation | async-start | bytes 262144 | tf_op jit(solution)/shard_map/while/body/eval_jaxpr/all_to_all | solution.py:27
  131.2 8.1 %all-to-all-start = ((f32[4,4,4,512]{3,2,1,0:T(4,128)}), f32[4,4,4,512]{3,2,1,0:T(4,128)S(1)}, u32[]{:S(2)}, u32[]{:S(2)}) async-start(f32[4,4,4,512]{3,2,1,0:T(4,128)} %bitcast.39), calls=%async_computation | async-start | bytes 262144 | tf_op jit(solution)/shard_map/while/body/eval_jaxpr/all_to_all | solution.py:27
  142.4 8.1 %all-to-all-start = ((f32[4,4,4,512]{3,2,1,0:T(4,128)}), f32[4,4,4,512]{3,2,1,0:T(4,128)S(1)}, u32[]{:S(2)}, u32[]{:S(2)}) async-start(f32[4,4,4,512]{3,2,1,0:T(4,128)} %bitcast.39), calls=%async_computation | async-start | bytes 262144 | tf_op jit(solution)/shard_map/while/body/eval_jaxpr/all_to_all | solution.py:27
  153.6 8.1 %all-to-all-start = ((f32[4,4,4,512]{3,2,1,0:T(4,128)}), f32[4,4,4,512]{3,2,1,0:T(4,128)S(1)}, u32[]{:S(2)}, u32[]{:S(2)}) async-start(f32[4,4,4,512]{3,2,1,0:T(4,128)} %bitcast.39), calls=%async_computation | async-start | bytes 262144 | tf_op jit(solution)/shard_map/while/body/eval_jaxpr/all_to_all | solution.py:27
  164.7 8.1 %all-to-all-start = ((f32[4,4,4,512]{3,2,1,0:T(4,128)}), f32[4,4,4,512]{3,2,1,0:T(4,128)S(1)}, u32[]{:S(2)}, u32[]{:S(2)}) async-start(f32[4,4,4,512]{3,2,1,0:T(4,128)} %bitcast.39), calls=%async_computation | async-start | bytes 262144 | tf_op jit(solution)/shard_map/while/body/eval_jaxpr/all_to_all | solution.py:27
  175.9 8.1 %all-to-all-start = ((f32[4,4,4,512]{3,2,1,0:T(4,128)}), f32[4,4,4,512]{3,2,1,0:T(4,128)S(1)}, u32[]{:S(2)}, u32[]{:S(2)}) async-start(f32[4,4,4,512]{3,2,1,0:T(4,128)} %bitcast.39), calls=%async_computation | async-start | bytes 262144 | tf_op jit(solution)/shard_map/while/body/eval_jaxpr/all_to_all | solution.py:27
  185.5 10.4 %all-to-all-start.1 = ((bf16[4,4,4,4096]{3,2,1,0:T(4,128)(2,1)}), bf16[4,4,4,4096]{3,2,1,0:T(4,128)(2,1)S(1)}, u32[]{:S(2)}, u32[]{:S(2)}) async-start(bf16[4,4,4,4096]{3,2,1,0:T(4,128)(2,1)} %broadcast_in_dim.39), calls=%async_computation.1 | async-start | bytes 1048576 | tf_op jit(solution)/shard_map/all_to_all | solution.py:39
  196.3 10.5 %copy-start.1 = (bf16[16,128,128]{2,1,0:T(8,128)(2,1)S(1)}, bf16[16,128,128]{2,1,0:T(8,128)(2,1)}, u32[]{:S(2)}) copy-start(bf16[16,128,128]{2,1,0:T(8,128)(2,1)} %param.20) | copy-start | bytes 1572868
  215.1 31.6 %all-to-all-start.3 = ((bf16[64,4,512]{2,1,0:T(4,128)(2,1)}), bf16[64,4,512]{2,1,0:T(4,128)(2,1)S(1)}, u32[]{:S(2)}, u32[]{:S(2)}) async-start(bf16[64,4,512]{2,1,0:T(4,128)(2,1)} %broadcast_in_dim.41), calls=%async_computation.3 | async-start | bytes 524288 | tf_op jit(solution)/shard_map/all_to_all | solution.py:39
Sparse Core Ops, SparseCore 0:
  10.0 80.9 all-gather.2
where the time goes:
time: 257 us; the launch traced here: 254 us
  waiting for transfers between devices  139 us (54%)
  starting transfers between devices  49.3 us (19%)
  matrix products  31.1 us (12%)
  between operations  13.5 us (5%)
  local copies, waits for them, and re-layouts  12 us (5%)
  blocking collectives  6.84 us (3%)
    all_gather x1, waiting for transfers between devices, sent_together(): lax.all_gather(both, axis, axis=dim, tiled=True)  80.7 us
    all_to_all x8, waiting for transfers between devices, summed_on_arrival(): lax.all_to_all(blocks, axis, split_axis=0, concat_axis=0, tiled=True)  38.4 us
    all_to_all x8, starting transfers between devices, summed_on_arrival(): lax.all_to_all(blocks, axis, split_axis=0, concat_axis=0, tiled=True)  27.3 us
    all_to_all x2, starting transfers between devices, copy_for_each(): return lax.all_to_all(copies, axis, split_axis=0, concat_axis=0, tiled=True)  22 us
    all_to_all x2, waiting for transfers between devices, copy_for_each(): return lax.all_to_all(copies, axis, split_axis=0, concat_axis=0, tiled=True)  19.9 us
    dot_general x8, matrix products, partial_scores(): jnp.einsum('shl,stl->sht', query_lat, cache_block, preferred_element_type...  10.3 us
    dot_general x8, matrix products, add_values(): jnp.einsum('sht,stl->shl', weight_block, cache_block, preferred_element_t...  9.92 us
    dot_general x8, matrix products, partial_scores(): jnp.einsum('she,set->sht', query_rope, key_block, preferred_element_type=...  7.73 us
  transfers between devices with their start and end apart: 11, of which 11 were waited for; matrix products, arithmetic and copies ran while one was open for 0% of the time, Pallas kernels for 0%

commit v1 on v0

v1 whole, which is shorter than its diff:
```python
import math

import jax
import jax.numpy as jnp
from jax import lax
from jax.sharding import PartitionSpec as P

NZ, NX, NC = 8, 4, 2


def dp_groups():
    z_groups = [[z * NX * NC + p for z in range(NZ)] for p in range(NX * NC)]
    x_groups = [[(z * NX + x) * NC + c for x in range(NX)] for z in range(NZ) for c in range(NC)]
    c_groups = [[i * NC + c for c in range(NC)] for i in range(NZ * NX)]
    return z_groups, x_groups, c_groups


def shifted(array, axis, groups, step):
    pairs = [(g[i], g[(i + step) % len(g)]) for g in groups for i in range(len(g))]
    return lax.ppermute(array, axis, pairs)


def from_ranks(arrays):
    count = lax.axis_size("rank")
    return [
        shifted(a, "rank", [list(range(count))], k) for k, a in enumerate(arrays, start=1)
    ]


def per_device(q_nope, q_rope, latent_cache, rope_keys, lengths, slot_of, w_uk, w_uv, w_out):
    f32, bf16 = jnp.float32, jnp.bfloat16
    seqs = q_nope.shape[0]
    heads, nope_dim, lat_part = w_uk.shape
    rope_part = rope_keys.shape[1]
    rope_dim = q_rope.shape[1] // heads
    capacity = latent_cache.shape[1]
    value_dim = w_uv.shape[2]
    seq_total = slot_of.shape[0]
    ranks = lax.axis_size("rank")
    group = heads // ranks
    scale = 1.0 / math.sqrt(nope_dim + rope_dim)
    z_groups, x_groups, c_groups = dp_groups()
    rank_pos = lax.axis_index("rank")
    dp_pos = lax.axis_index("dp")
    c_pos = dp_pos % NC
    x_pos = dp_pos // NC % NX
    z_pos = dp_pos // (NC * NX)

    own_lat = jnp.einsum(
        "shn,hnl->shl", q_nope.reshape(seqs, heads, nope_dim), w_uk, preferred_element_type=f32
    ).astype(bf16).reshape(seqs, heads * lat_part)
    own_rope = lax.dynamic_slice_in_dim(
        q_rope.reshape(seqs, heads, rope_dim), rank_pos * rope_part, rope_part, 2
    ).reshape(seqs, heads * rope_part)
    rows = jnp.concatenate([own_lat, own_rope], axis=1)

    over_x = [rows] + [shifted(rows, "dp", x_groups, k) for k in range(1, NX)]
    over_x = jnp.concatenate(over_x, axis=0)
    plane = jnp.concatenate([over_x, shifted(over_x, "dp", c_groups, 1)], axis=0)
    at = jnp.arange(plane.shape[0], dtype=jnp.int32)
    from_c = (c_pos + at // (NX * seqs)) % NC
    from_x = (x_pos - at // seqs % NX) % NX
    row_of = ((z_pos * NX + from_x) * NC + from_c) * seqs + at % seqs
    slot_here = jnp.sum(
        jnp.where(
            row_of[:, None] == jnp.arange(seq_total, dtype=jnp.int32)[None, :], slot_of[None, :], 0
        ),
        axis=1,
    )
    wanted = jnp.arange(NZ * seqs, dtype=jnp.int32)
    wanted = ((wanted // seqs * NX + x_pos) * NC + c_pos) * seqs + wanted % seqs
    pick = (wanted[:, None] == slot_here[None, :]).astype(bf16)
    picked = jnp.dot(pick, plane, preferred_element_type=f32).astype(bf16)
    arrived = lax.all_to_all(
        picked.reshape(NZ, seqs, -1), "dp", 0, 0, axis_index_groups=z_groups, tiled=True
    )
    query = arrived.astype(f32).sum(axis=0).astype(bf16)
    query_lat = query[:, : heads * lat_part].reshape(seqs, ranks, group, lat_part)
    query_rope = query[:, heads * lat_part :].reshape(seqs, ranks, group, rope_part)

    turned_lat = jnp.roll(query_lat, -rank_pos, axis=1).reshape(seqs, heads, lat_part)
    turned_rope = jnp.roll(query_rope, -rank_pos, axis=1).reshape(seqs, heads, rope_part)
    scores = (
        jnp.einsum("shl,stl->sht", turned_lat, latent_cache, preferred_element_type=f32)
        + jnp.einsum("she,set->sht", turned_rope, rope_keys, preferred_element_type=f32)
    ) * scale
    scores = scores.reshape(seqs, ranks, group, capacity)
    own = scores[:, 0]
    for part in from_ranks([scores[:, k] for k in range(1, ranks)]):
        own = own + part
    positions = jnp.arange(capacity, dtype=jnp.int32)
    own = jnp.where(positions[None, None, :] < lengths[:, None, None], own, -jnp.inf)
    raised = jnp.exp(own - jnp.max(own, axis=2, keepdims=True))
    weights = (raised / jnp.sum(raised, axis=2, keepdims=True)).astype(bf16)

    gathered = [weights] + from_ranks([weights] * (ranks - 1))
    gathered = jnp.concatenate(gathered[::-1], axis=1)
    latent_out = jnp.einsum(
        "sht,stl->shl", gathered, latent_cache, preferred_element_type=f32
    ).astype(bf16)
    latent_out = jnp.roll(
        latent_out.reshape(seqs, ranks, group, lat_part), rank_pos + 1, axis=1
    ).reshape(seqs, heads, lat_part)
    value_part = jnp.einsum(
        "shl,hlv->shv", latent_out, w_uv, preferred_element_type=f32
    ).astype(bf16).reshape(seqs, heads * value_dim)
    total = value_part.astype(f32)
    for part in from_ranks([value_part] * (ranks - 1)):
        total = total + part.astype(f32)
    out_rows = jnp.dot(total.astype(bf16), w_out, preferred_element_type=f32).astype(bf16)

    copies = jnp.broadcast_to(out_rows, (lax.axis_size("dp"), *out_rows.shape))
    everyone = lax.all_to_all(copies, "dp", 0, 0, tiled=True).reshape(seq_total, -1)
    targets = lax.dynamic_slice_in_dim(slot_of, dp_pos * seqs, seqs)
    back = (targets[:, None] == jnp.arange(seq_total, dtype=jnp.int32)[None, :]).astype(bf16)
    return jnp.dot(back, everyone, preferred_element_type=f32).astype(bf16)


def solution(mesh):
    placed = (
        P("dp", None),
        P("dp", None),
        P("dp", None, "rank"),
        P("dp", "rank", None),
        P("dp"),
        P(),
        P(None, None, "rank"),
        P(None, "rank", None),
        P(None, "rank"),
    )
    return jax.shard_map(
        per_device, mesh=mesh, in_specs=placed, out_specs=P("dp", "rank"), check_vma=False
    )
```

time: 257 us -> 97.4 us (0.38)
  waiting for transfers between devices: 139 us -> 41.1 us
  matrix products: 31.1 us -> 11.6 us
  between operations: 13.5 us -> 0.15 us
  starting transfers between devices: 49.3 us -> 37.9 us
  local copies, waits for them, and re-layouts: 12 us -> 4.54 us
  blocking collectives: 6.84 us -> 0 us
    all_gather x1 -> x0, waiting for transfers between devices: 80.7 us -> none  [sent_together(): lax.all_gather(both, axis, axis=dim, tiled=True)]
    all_to_all x10 -> x2, waiting for transfers between devices: 58.3 us -> 21.4 us  [the longest x1 13 us: per_device(): lax.all_to_all(copies, 'dp', 0, 0, tiled=True).reshape(seq_total, -1)]
    all_to_all x10 -> x2, starting transfers between devices: 49.3 us -> 17.2 us  [the longest x1 9.03 us: per_device(): lax.all_to_all(copies, 'dp', 0, 0, tiled=True).reshape(seq_total, -1)]
    ppermute x0 -> x13, starting transfers between devices: none -> 20.6 us  [shifted(): return lax.ppermute(array, axis, pairs)]
    ppermute x0 -> x13, waiting for transfers between devices: none -> 19.7 us  [shifted(): return lax.ppermute(array, axis, pairs)]
    dot_general x30 -> x8, matrix products: 31.1 us -> 11.6 us  [the longest x1 3.38 us: per_device(): jnp.einsum('shl,stl->sht', turned_lat, latent_cache, preferred_element_ty...]
    all_to_all x1 -> x0, blocking collectives: 6.84 us -> none  [copy_for_each(): return lax.all_to_all(copies, axis, split_axis=0, concat_axis=0, tiled=True)]
    reshape x20 -> x7, local copies, waits for them, and re-layouts: 6.85 us -> 3.44 us  [the longest x1 1.53 us: per_device(): scores = scores.reshape(seqs, ranks, group, capacity)]
  transfers between devices with their start and end apart: 11 -> 15, of which waited for: 11 -> 13; matrix products, arithmetic and copies ran while one was open for 0% -> 1% of each run, Pallas kernels for 0% -> 0%
where the time goes in v1:
time: 97.4 us; the launch traced here: 96.9 us
  waiting for transfers between devices  41.1 us (42%)
  starting transfers between devices  37.9 us (39%)
  matrix products  11.6 us (12%)
  local copies, waits for them, and re-layouts  4.54 us (5%)
  other arithmetic  1.71 us (2%)
    ppermute x13, starting transfers between devices, shifted(): return lax.ppermute(array, axis, pairs)  20.6 us
    ppermute x13, waiting for transfers between devices, shifted(): return lax.ppermute(array, axis, pairs)  19.7 us
    all_to_all x1, waiting for transfers between devices, per_device(): lax.all_to_all(copies, 'dp', 0, 0, tiled=True).reshape(seq_total, -1)  13 us
    all_to_all x1, starting transfers between devices, per_device(): lax.all_to_all(copies, 'dp', 0, 0, tiled=True).reshape(seq_total, -1)  9.03 us
    all_to_all x1, waiting for transfers between devices, per_device(): lax.all_to_all(picked.reshape(NZ, seqs, -1), 'dp', 0, 0, axis_index_group...  8.37 us
    all_to_all x1, starting transfers between devices, per_device(): lax.all_to_all(picked.reshape(NZ, seqs, -1), 'dp', 0, 0, axis_index_group...  8.19 us
    dot_general x1, matrix products, per_device(): jnp.einsum('shl,stl->sht', turned_lat, latent_cache, preferred_element_ty...  3.38 us
    dot_general x1, matrix products, per_device(): jnp.einsum('sht,stl->shl', gathered, latent_cache, preferred_element_type...  2.97 us
  transfers between devices with their start and end apart: 15, of which 13 were waited for; matrix products, arithmetic and copies ran while one was open for 1% of the time, Pallas kernels for 0%

profile of v1, /device:TPU:1, one launch (start us, length us, event | category | flops | bytes accessed | tf_op | source)
XLA Modules:
  0.0 96.9 jit_solution(12136163564614931430)
XLA Ops:
  0.0 0.9 reshape.148
  0.9 0.1 constant_dynamic-slice_fusion
  1.0 0.1 reshape.149
  1.1 1.3 %fusion.5 = bf16[4,2048]{1,0:T(4,128)(2,1)S(1)} fusion(bf16[16,128,128]{2,1,0:T(8,128)(2,1)} %param.17, bf16[4,2048]{1,0:T(4,128)(2,1)} %param.11), kind=kOutput, calls=%fused_computation.10 | convolution fusion | flops 2105344 | bytes 557056 | tf_op jit(solution)/shard_map/shn,hnl->shl/dot_general | solution.py:49
  2.4 2.1 %collective-permute-start = (bf16[4,2304]{1,0:T(4,128)(2,1)S(1)}, bf16[4,2304]{1,0:T(4,128)(2,1)S(1)}, u32[]{:S(2)}, u32[]{:S(2)}) collective-permute-start(bf16[4,2304]{1,0:T(4,128)(2,1)S(1)} %pad_maximum_fusion.1), channel_id=1, source_target_pairs={{0,8},{8,16},{16,24},{24,0},{4,12},{12,20},{20,28},{28,4},{32,40},... | collective-permute-start | bytes 55304 | tf_op jit(solution)/shard_map/ppermute | solution.py:20
  4.5 2.5 %collective-permute-start.1 = (bf16[4,2304]{1,0:T(4,128)(2,1)S(1)}, bf16[4,2304]{1,0:T(4,128)(2,1)S(1)}, u32[]{:S(2)}, u32[]{:S(2)}) collective-permute-start(bf16[4,2304]{1,0:T(4,128)(2,1)S(1)} %pad_maximum_fusion.1), channel_id=1, source_target_pairs={{0,16},{8,24},{16,0},{24,8},{4,20},{12,28},{20,4},{28,12},{32,48},... | collective-permute-start | bytes 55304 | tf_op jit(solution)/shard_map/ppermute | solution.py:20
  7.0 1.2 %collective-permute-start.2 = (bf16[4,2304]{1,0:T(4,128)(2,1)S(1)}, bf16[4,2304]{1,0:T(4,128)(2,1)S(1)}, u32[]{:S(2)}, u32[]{:S(2)}) collective-permute-start(bf16[4,2304]{1,0:T(4,128)(2,1)S(1)} %pad_maximum_fusion.1), channel_id=1, source_target_pairs={{0,24},{8,0},{16,8},{24,16},{4,28},{12,4},{20,12},{28,20},{32,56},... | collective-permute-start | bytes 55304 | tf_op jit(solution)/shard_map/ppermute | solution.py:20
  8.2 0.5 collective-permute-done.1
  8.7 1.2 %collective-permute-done.2 = bf16[4,2304]{1,0:T(4,128)(2,1)S(1)} collective-permute-done((bf16[4,2304]{1,0:T(4,128)(2,1)S(1)}, bf16[4,2304]{1,0:T(4,128)(2,1)S(1)}, u32[]{:S(2)}, u32[]{:S(2)}) %collective-permute-start.2) | collective-permute-done | bytes 18464 | tf_op jit(solution)/shard_map/ppermute | solution.py:20
  9.9 2.2 %collective-permute-start.3 = (bf16[16,2304]{1,0:T(8,128)(2,1)S(1)}, bf16[16,2304]{1,0:T(8,128)(2,1)S(1)}, u32[]{:S(2)}, u32[]{:S(2)}) collective-permute-start(bf16[16,2304]{1,0:T(8,128)(2,1)S(1)} %pad_maximum_fusion), channel_id=1, source_target_pairs={{0,4},{4,0},{8,12},{12,8},{16,20},{20,16},{24,28},{28,24},{32,36},... | collective-permute-start | bytes 221192 | tf_op jit(solution)/shard_map/ppermute | solution.py:20
  12.1 0.9 select_reduce_fusion
  13.0 0.1 concatenate.22
  13.1 0.2 convolution_convert_fusion
  13.3 0.7 reshape.150
  14.1 8.2 %all-to-all-start = ((bf16[8,4,2304]{2,1,0:T(4,128)(2,1)}), bf16[8,4,2304]{2,1,0:T(4,128)(2,1)S(1)}, u32[]{:S(2)}, u32[]{:S(2)}) async-start(bf16[8,4,2304]{2,1,0:T(4,128)(2,1)} %reshape.150), calls=%async_computation | async-start | bytes 294912 | tf_op jit(solution)/shard_map/all_to_all | solution.py:74
  22.2 8.4 %all-to-all-done = bf16[8,4,2304]{2,1,0:T(4,128)(2,1)S(1)} async-done(((bf16[8,4,2304]{2,1,0:T(4,128)(2,1)}), bf16[8,4,2304]{2,1,0:T(4,128)(2,1)S(1)}, u32[]{:S(2)}, u32[]{:S(2)}) %all-to-all-start) | async-done | bytes 147488 | tf_op jit(solution)/shard_map/all_to_all | solution.py:74
  30.6 0.1 reduce_sum.31
  30.7 0.1 reshape.153
  30.9 3.4 %fusion.38 = f32[4,16,4096]{2,1,0:T(8,128)S(1)} fusion(bf16[4,16,128]{2,1,0:T(8,128)(2,1)S(1)} %bitcast.52, bf16[4,4096,128]{2,1,0:T(8,128)(2,1)} %param.13), kind=kOutput, calls=%fused_computation.81 | convolution fusion | flops 67108864 | bytes 5259264 | tf_op jit(solution)/shard_map/shl,stl->sht/dot_general | solution.py:84
  34.3 1.3 %fusion.1 = f32[4,16,4096]{2,1,0:T(8,128)} fusion(f32[4,16,4096]{2,1,0:T(8,128)S(1)} %fusion.38, bf16[4,16,16]{2,1,0:T(8,128)(2,1)S(1)} %bitcast.53, bf16[4,16,4096]{2,1,0:T(8,128)(2,1)S(1)} %copy-done.1), kind=kOutput, calls=%fused_computation.2 | convolution fusion | flops 8912896 | bytes 2623488 | tf_op jit(solution)/shard_map/she,set->sht/dot_general | solution.py:85
  35.6 1.5 %reshape.155 = f32[4,4,4,4096]{3,2,1,0:T(4,128)S(1)} reshape(f32[4,16,4096]{2,1,0:T(8,128)} %fusion.1) | data formatting | bytes 2097152 | tf_op jit(solution)/shard_map/reshape | solution.py:87
  37.2 1.4 %collective-permute-start.4 = (f32[4,4,4096]{2,1,0:T(4,128)S(1)}, f32[4,4,4096]{2,1,0:T(4,128)S(1)}, u32[]{:S(2)}, u32[]{:S(2)}) collective-permute-start(f32[4,4,4096]{2,1,0:T(4,128)S(1)} %get-tuple-element.6), channel_id=1, source_target_pairs={{0,1},{1,2},{2,3},{3,0},{4,5},{5,6},{6,7},{7,4},{8,9},{9,10},{10,1... | collective-permute-start | bytes 786440 | tf_op jit(solution)/shard_map/ppermute | solution.py:20
  38.5 2.6 %collective-permute-start.5 = (f32[4,4,4096]{2,1,0:T(4,128)S(1)}, f32[4,4,4096]{2,1,0:T(4,128)S(1)}, u32[]{:S(2)}, u32[]{:S(2)}) collective-permute-start(f32[4,4,4096]{2,1,0:T(4,128)S(1)} %get-tuple-element.7), channel_id=1, source_target_pairs={{0,2},{1,3},{2,0},{3,1},{4,6},{5,7},{6,4},{7,5},{8,10},{9,11},{10,... | collective-permute-start | bytes 786440 | tf_op jit(solution)/shard_map/ppermute | solution.py:20
  41.2 1.1 %collective-permute-start.6 = (f32[4,4,4096]{2,1,0:T(4,128)S(1)}, f32[4,4,4096]{2,1,0:T(4,128)S(1)}, u32[]{:S(2)}, u32[]{:S(2)}) collective-permute-start(f32[4,4,4096]{2,1,0:T(4,128)S(1)} %get-tuple-element.8), channel_id=1, source_target_pairs={{0,3},{1,0},{2,1},{3,2},{4,7},{5,4},{6,5},{7,6},{8,11},{9,8},{10,9... | collective-permute-start | bytes 786440 | tf_op jit(solution)/shard_map/ppermute | solution.py:20
  42.2 0.1 iota_compare_fusion
  42.3 2.1 %collective-permute-done.4 = f32[4,4,4096]{2,1,0:T(4,128)S(1)} collective-permute-done((f32[4,4,4096]{2,1,0:T(4,128)S(1)}, f32[4,4,4096]{2,1,0:T(4,128)S(1)}, u32[]{:S(2)}, u32[]{:S(2)}) %collective-permute-start.4) | collective-permute-done | bytes 262176 | tf_op jit(solution)/shard_map/ppermute | solution.py:20
  44.4 6.7 %collective-permute-done.5 = f32[4,4,4096]{2,1,0:T(4,128)S(1)} collective-permute-done((f32[4,4,4096]{2,1,0:T(4,128)S(1)}, f32[4,4,4096]{2,1,0:T(4,128)S(1)}, u32[]{:S(2)}, u32[]{:S(2)}) %collective-permute-start.5) | collective-permute-done | bytes 262176 | tf_op jit(solution)/shard_map/ppermute | solution.py:20
  51.2 0.4 fusion.36
  51.6 0.1 divide_convert_fusion
  51.7 3.5 %collective-permute-start.7 = (bf16[4,4,4096]{2,1,0:T(4,128)(2,1)S(1)}, bf16[4,4,4096]{2,1,0:T(4,128)(2,1)S(1)}, u32[]{:S(2)}, u32[]{:S(2)}) collective-permute-start(bf16[4,4,4096]{2,1,0:T(4,128)(2,1)S(1)} %divide_convert_fusion), channel_id=1, source_target_pairs={{0,3},{1,0},{2,1},{3,2},{4,7},{5,4},{6,5},{7,6},{8,11},{9,8},{10,9... | collective-permute-start | bytes 393224 | tf_op jit(solution)/shard_map/ppermute | solution.py:20
  55.2 1.0 %collective-permute-start.8 = (bf16[4,4,4096]{2,1,0:T(4,128)(2,1)S(1)}, bf16[4,4,4096]{2,1,0:T(4,128)(2,1)S(1)}, u32[]{:S(2)}, u32[]{:S(2)}) collective-permute-start(bf16[4,4,4096]{2,1,0:T(4,128)(2,1)S(1)} %divide_convert_fusion), channel_id=1, source_target_pairs={{0,2},{1,3},{2,0},{3,1},{4,6},{5,7},{6,4},{7,5},{8,10},{9,11},{10,... | collective-permute-start | bytes 393224 | tf_op jit(solution)/shard_map/ppermute | solution.py:20
  56.2 2.8 %collective-permute-done.7 = bf16[4,4,4096]{2,1,0:T(4,128)(2,1)S(1)} collective-permute-done((bf16[4,4,4096]{2,1,0:T(4,128)(2,1)S(1)}, bf16[4,4,4096]{2,1,0:T(4,128)(2,1)S(1)}, u32[]{:S(2)}, u32[]{:S(2)}) %collective-permute-start.7) | collective-permute-done | bytes 131104 | tf_op jit(solution)/shard_map/ppermute | solution.py:20
  59.0 1.6 %collective-permute-done.8 = bf16[4,4,4096]{2,1,0:T(4,128)(2,1)S(1)} collective-permute-done((bf16[4,4,4096]{2,1,0:T(4,128)(2,1)S(1)}, bf16[4,4,4096]{2,1,0:T(4,128)(2,1)S(1)}, u32[]{:S(2)}, u32[]{:S(2)}) %collective-permute-start.8) | collective-permute-done | bytes 131104 | tf_op jit(solution)/shard_map/ppermute | solution.py:20
  60.6 3.4 %collective-permute-done.9 = bf16[4,4,4096]{2,1,0:T(4,128)(2,1)S(1)} collective-permute-done((bf16[4,4,4096]{2,1,0:T(4,128)(2,1)S(1)}, bf16[4,4,4096]{2,1,0:T(4,128)(2,1)S(1)}, u32[]{:S(2)}, u32[]{:S(2)}) %collective-permute-start.9) | collective-permute-done | bytes 131104 | tf_op jit(solution)/shard_map/ppermute | solution.py:20
  63.9 3.0 %convolution_convert_fusion.1 = bf16[4,16,128]{2,1,0:T(8,128)(2,1)S(1)} fusion(bf16[4,4096,128]{2,1,0:T(8,128)(2,1)} %param.13, bf16[4,4,4096]{2,1,0:T(4,128)(2,1)S(1)} %divide_convert_fusion, bf16[4,4,4096]{2,1,0:T(4,128)(2,1)S(1)} %collective-permute-done.9, bf16[4,4,4096]{2,1,0:T(4,128)(2,1)S(1)} %collective-permute-done.8, ...), kind=kOutput, calls=%fused_computation.6 | convolution fusion | flops 69214208 | bytes 4734976 | tf_op jit(solution)/shard_map/sht,stl->shl/dot_general | solution.py:98
  67.0 1.3 %fusion.4 = bf16[4,2048]{1,0:T(4,128)(2,1)S(1)} fusion(bf16[4,16,128]{2,0,1:T(4,128)(2,1)S(1)} %bitcast.54, bf16[16,128,128]{2,1,0:T(8,128)(2,1)} %param.18), kind=kOutput, calls=%fused_computation.8 | convolution fusion | flops 2105344 | bytes 557056 | tf_op jit(solution)/shard_map/shl,hlv->shv/dot_general | solution.py:104
  68.3 1.2 %collective-permute-start.11 = (bf16[4,2048]{1,0:T(4,128)(2,1)S(1)}, bf16[4,2048]{1,0:T(4,128)(2,1)S(1)}, u32[]{:S(2)}, u32[]{:S(2)}) collective-permute-start(bf16[4,2048]{1,0:T(4,128)(2,1)S(1)} %fusion.4), channel_id=1, source_target_pairs={{0,2},{1,3},{2,0},{3,1},{4,6},{5,7},{6,4},{7,5},{8,10},{9,11},{10,... | collective-permute-start | bytes 49160 | tf_op jit(solution)/shard_map/ppermute | solution.py:20
  69.5 2.0 %collective-permute-start.12 = (bf16[4,2048]{1,0:T(4,128)(2,1)S(1)}, bf16[4,2048]{1,0:T(4,128)(2,1)S(1)}, u32[]{:S(2)}, u32[]{:S(2)}) collective-permute-start(bf16[4,2048]{1,0:T(4,128)(2,1)S(1)} %fusion.4), channel_id=1, source_target_pairs={{0,3},{1,0},{2,1},{3,2},{4,7},{5,4},{6,5},{7,6},{8,11},{9,8},{10,9... | collective-permute-start | bytes 49160 | tf_op jit(solution)/shard_map/ppermute | solution.py:20
  71.5 0.6 collective-permute-done.10
  72.1 0.4 collective-permute-done.11
  72.4 0.4 collective-permute-done.12
  72.8 0.4 convolution_convert_fusion.5
  73.2 0.8 broadcast_in_dim.42
  74.0 9.0 %all-to-all-start.1 = ((bf16[64,4,512]{2,1,0:T(4,128)(2,1)}), bf16[64,4,512]{2,1,0:T(4,128)(2,1)S(1)}, u32[]{:S(2)}, u32[]{:S(2)}) async-start(bf16[64,4,512]{2,1,0:T(4,128)(2,1)} %broadcast_in_dim.42), calls=%async_computation.1 | async-start | bytes 524288 | tf_op jit(solution)/shard_map/all_to_all | solution.py:113
  83.0 0.1 dynamic_slice.13
  83.1 13.0 %all-to-all-done.1 = bf16[64,4,512]{2,1,0:T(4,128)(2,1)S(1)} async-done(((bf16[64,4,512]{2,1,0:T(4,128)(2,1)}), bf16[64,4,512]{2,1,0:T(4,128)(2,1)S(1)}, u32[]{:S(2)}, u32[]{:S(2)}) %all-to-all-start.1) | async-done | bytes 262176 | tf_op jit(solution)/shard_map/all_to_all | solution.py:113
  96.1 0.1 reshape.159
  96.2 0.8 convolution_convert_fusion.4
  (24 shorter events, 0.4 us)
Async XLA Ops:
  0.0 72.8 %copy-start = (bf16[2048,512]{1,0:T(8,128)(2,1)S(1)}, bf16[2048,512]{1,0:T(8,128)(2,1)}, u32[]{:S(2)}) copy-start(bf16[2048,512]{1,0:T(8,128)(2,1)} %param.19) | copy-start | bytes 6291460
  0.0 34.3 %copy-start.1 = (bf16[4,16,4096]{2,1,0:T(8,128)(2,1)S(1)}, bf16[4,16,4096]{2,1,0:T(8,128)(2,1)}, u32[]{:S(2)}) copy-start(bf16[4,16,4096]{2,1,0:T(8,128)(2,1)} %param.14) | copy-start | bytes 1572868
  2.4 5.7 %collective-permute-start = (bf16[4,2304]{1,0:T(4,128)(2,1)S(1)}, bf16[4,2304]{1,0:T(4,128)(2,1)S(1)}, u32[]{:S(2)}, u32[]{:S(2)}) collective-permute-start(bf16[4,2304]{1,0:T(4,128)(2,1)S(1)} %pad_maximum_fusion.1), channel_id=1, source_target_pairs={{0,8},{8,16},{16,24},{24,0},{4,12},{12,20},{20,28},{28,4},{32,40},... | collective-permute-start | bytes 55304 | tf_op jit(solution)/shard_map/ppermute | solution.py:20
  4.5 4.1 %collective-permute-start.1 = (bf16[4,2304]{1,0:T(4,128)(2,1)S(1)}, bf16[4,2304]{1,0:T(4,128)(2,1)S(1)}, u32[]{:S(2)}, u32[]{:S(2)}) collective-permute-start(bf16[4,2304]{1,0:T(4,128)(2,1)S(1)} %pad_maximum_fusion.1), channel_id=1, source_target_pairs={{0,16},{8,24},{16,0},{24,8},{4,20},{12,28},{20,4},{28,12},{32,48},... | collective-permute-start | bytes 55304 | tf_op jit(solution)/shard_map/ppermute | solution.py:20
  7.0 2.9 %collective-permute-start.2 = (bf16[4,2304]{1,0:T(4,128)(2,1)S(1)}, bf16[4,2304]{1,0:T(4,128)(2,1)S(1)}, u32[]{:S(2)}, u32[]{:S(2)}) collective-permute-start(bf16[4,2304]{1,0:T(4,128)(2,1)S(1)} %pad_maximum_fusion.1), channel_id=1, source_target_pairs={{0,24},{8,0},{16,8},{24,16},{4,28},{12,4},{20,12},{28,20},{32,56},... | collective-permute-start | bytes 55304 | tf_op jit(solution)/shard_map/ppermute | solution.py:20
  9.9 3.1 %collective-permute-start.3 = (bf16[16,2304]{1,0:T(8,128)(2,1)S(1)}, bf16[16,2304]{1,0:T(8,128)(2,1)S(1)}, u32[]{:S(2)}, u32[]{:S(2)}) collective-permute-start(bf16[16,2304]{1,0:T(8,128)(2,1)S(1)} %pad_maximum_fusion), channel_id=1, source_target_pairs={{0,4},{4,0},{8,12},{12,8},{16,20},{20,16},{24,28},{28,24},{32,36},... | collective-permute-start | bytes 221192 | tf_op jit(solution)/shard_map/ppermute | solution.py:20
  14.1 16.6 %all-to-all-start = ((bf16[8,4,2304]{2,1,0:T(4,128)(2,1)}), bf16[8,4,2304]{2,1,0:T(4,128)(2,1)S(1)}, u32[]{:S(2)}, u32[]{:S(2)}) async-start(bf16[8,4,2304]{2,1,0:T(4,128)(2,1)} %reshape.150), calls=%async_computation | async-start | bytes 294912 | tf_op jit(solution)/shard_map/all_to_all | solution.py:74
  34.3 7.9 %copy-start.3 = (s32[4]{0:T(128)S(1)}, s32[4]{0:T(128)}, u32[]{:S(2)}) copy-start(s32[4]{0:T(128)} %param.15) | copy-start | bytes 52
  37.2 7.3 %collective-permute-start.4 = (f32[4,4,4096]{2,1,0:T(4,128)S(1)}, f32[4,4,4096]{2,1,0:T(4,128)S(1)}, u32[]{:S(2)}, u32[]{:S(2)}) collective-permute-start(f32[4,4,4096]{2,1,0:T(4,128)S(1)} %get-tuple-element.6), channel_id=1, source_target_pairs={{0,1},{1,2},{2,3},{3,0},{4,5},{5,6},{6,7},{7,4},{8,9},{9,10},{10,1... | collective-permute-start | bytes 786440 | tf_op jit(solution)/shard_map/ppermute | solution.py:20
  38.5 12.6 %collective-permute-start.5 = (f32[4,4,4096]{2,1,0:T(4,128)S(1)}, f32[4,4,4096]{2,1,0:T(4,128)S(1)}, u32[]{:S(2)}, u32[]{:S(2)}) collective-permute-start(f32[4,4,4096]{2,1,0:T(4,128)S(1)} %get-tuple-element.7), channel_id=1, source_target_pairs={{0,2},{1,3},{2,0},{3,1},{4,6},{5,7},{6,4},{7,5},{8,10},{9,11},{10,... | collective-permute-start | bytes 786440 | tf_op jit(solution)/shard_map/ppermute | solution.py:20
  41.2 10.0 %collective-permute-start.6 = (f32[4,4,4096]{2,1,0:T(4,128)S(1)}, f32[4,4,4096]{2,1,0:T(4,128)S(1)}, u32[]{:S(2)}, u32[]{:S(2)}) collective-permute-start(f32[4,4,4096]{2,1,0:T(4,128)S(1)} %get-tuple-element.8), channel_id=1, source_target_pairs={{0,3},{1,0},{2,1},{3,2},{4,7},{5,4},{6,5},{7,6},{8,11},{9,8},{10,9... | collective-permute-start | bytes 786440 | tf_op jit(solution)/shard_map/ppermute | solution.py:20
  51.7 7.3 %collective-permute-start.7 = (bf16[4,4,4096]{2,1,0:T(4,128)(2,1)S(1)}, bf16[4,4,4096]{2,1,0:T(4,128)(2,1)S(1)}, u32[]{:S(2)}, u32[]{:S(2)}) collective-permute-start(bf16[4,4,4096]{2,1,0:T(4,128)(2,1)S(1)} %divide_convert_fusion), channel_id=1, source_target_pairs={{0,3},{1,0},{2,1},{3,2},{4,7},{5,4},{6,5},{7,6},{8,11},{9,8},{10,9... | collective-permute-start | bytes 393224 | tf_op jit(solution)/shard_map/ppermute | solution.py:20
  55.2 5.4 %collective-permute-start.8 = (bf16[4,4,4096]{2,1,0:T(4,128)(2,1)S(1)}, bf16[4,4,4096]{2,1,0:T(4,128)(2,1)S(1)}, u32[]{:S(2)}, u32[]{:S(2)}) collective-permute-start(bf16[4,4,4096]{2,1,0:T(4,128)(2,1)S(1)} %divide_convert_fusion), channel_id=1, source_target_pairs={{0,2},{1,3},{2,0},{3,1},{4,6},{5,7},{6,4},{7,5},{8,10},{9,11},{10,... | collective-permute-start | bytes 393224 | tf_op jit(solution)/shard_map/ppermute | solution.py:20
  56.2 7.7 %collective-permute-start.9 = (bf16[4,4,4096]{2,1,0:T(4,128)(2,1)S(1)}, bf16[4,4,4096]{2,1,0:T(4,128)(2,1)S(1)}, u32[]{:S(2)}, u32[]{:S(2)}) collective-permute-start(bf16[4,4,4096]{2,1,0:T(4,128)(2,1)S(1)} %divide_convert_fusion), channel_id=1, source_target_pairs={{0,1},{1,2},{2,3},{3,0},{4,5},{5,6},{6,7},{7,4},{8,9},{9,10},{10,1... | collective-permute-start | bytes 393224 | tf_op jit(solution)/shard_map/ppermute | solution.py:20
  56.2 26.8 %copy-start.2 = (s32[256]{0:T(256)S(1)}, s32[256]{0:T(256)}, u32[]{:S(2)}) copy-start(s32[256]{0:T(256)} %param.16) | copy-start | bytes 3076
  68.2 3.8 %collective-permute-start.10 = (bf16[4,2048]{1,0:T(4,128)(2,1)S(1)}, bf16[4,2048]{1,0:T(4,128)(2,1)S(1)}, u32[]{:S(2)}, u32[]{:S(2)}) collective-permute-start(bf16[4,2048]{1,0:T(4,128)(2,1)S(1)} %fusion.4), channel_id=1, source_target_pairs={{0,1},{1,2},{2,3},{3,0},{4,5},{5,6},{6,7},{7,4},{8,9},{9,10},{10,1... | collective-permute-start | bytes 49160 | tf_op jit(solution)/shard_map/ppermute | solution.py:20
  68.3 4.2 %collective-permute-start.11 = (bf16[4,2048]{1,0:T(4,128)(2,1)S(1)}, bf16[4,2048]{1,0:T(4,128)(2,1)S(1)}, u32[]{:S(2)}, u32[]{:S(2)}) collective-permute-start(bf16[4,2048]{1,0:T(4,128)(2,1)S(1)} %fusion.4), channel_id=1, source_target_pairs={{0,2},{1,3},{2,0},{3,1},{4,6},{5,7},{6,4},{7,5},{8,10},{9,11},{10,... | collective-permute-start | bytes 49160 | tf_op jit(solution)/shard_map/ppermute | solution.py:20
  69.5 3.3 %collective-permute-start.12 = (bf16[4,2048]{1,0:T(4,128)(2,1)S(1)}, bf16[4,2048]{1,0:T(4,128)(2,1)S(1)}, u32[]{:S(2)}, u32[]{:S(2)}) collective-permute-start(bf16[4,2048]{1,0:T(4,128)(2,1)S(1)} %fusion.4), channel_id=1, source_target_pairs={{0,3},{1,0},{2,1},{3,2},{4,7},{5,4},{6,5},{7,6},{8,11},{9,8},{10,9... | collective-permute-start | bytes 49160 | tf_op jit(solution)/shard_map/ppermute | solution.py:20
  74.0 22.1 %all-to-all-start.1 = ((bf16[64,4,512]{2,1,0:T(4,128)(2,1)}), bf16[64,4,512]{2,1,0:T(4,128)(2,1)S(1)}, u32[]{:S(2)}, u32[]{:S(2)}) async-start(bf16[64,4,512]{2,1,0:T(4,128)(2,1)} %broadcast_in_dim.42), calls=%async_computation.1 | async-start | bytes 524288 | tf_op jit(solution)/shard_map/all_to_all | solution.py:113

commit v2 on v1

v2 whole, which is shorter than its diff:
```python
import math

import jax
import jax.numpy as jnp
from jax import lax
from jax.experimental import pallas as pl
from jax.experimental.pallas import tpu as pltpu
from jax.sharding import PartitionSpec as P

NZ, NX, NC = 8, 4, 2


def dp_groups():
    z_groups = [[z * NX * NC + p for z in range(NZ)] for p in range(NX * NC)]
    x_groups = [[(z * NX + x) * NC + c for x in range(NX)] for z in range(NZ) for c in range(NC)]
    c_groups = [[i * NC + c for c in range(NC)] for i in range(NZ * NX)]
    return z_groups, x_groups, c_groups


def shifted(array, axis, groups, step):
    pairs = [(g[i], g[(i + step) % len(g)]) for g in groups for i in range(len(g))]
    return lax.ppermute(array, axis, pairs)


def from_ranks(arrays):
    count = lax.axis_size("rank")
    return [
        shifted(a, "rank", [list(range(count))], k) for k, a in enumerate(arrays, start=1)
    ]


F32, BF16 = jnp.float32, jnp.bfloat16
BLOCK = 1024
SMALL = pltpu.CompilerParams(vmem_limit_bytes=16 << 20)


def vmem():
    return pl.BlockSpec(memory_space=pltpu.VMEM)


def dot(a, b):
    return jnp.dot(a, b, preferred_element_type=F32)


def iota(shape, dim):
    return lax.broadcasted_iota(jnp.int32, shape, dim)


def fetch(after, *arrays):
    def body(*refs):
        refs[-1][...] = jnp.zeros(refs[-1].shape, F32)

    return pl.pallas_call(
        body,
        out_shape=jax.ShapeDtypeStruct((8, 128), F32),
        in_specs=[vmem()] * (1 + len(arrays)),
        out_specs=vmem(),
        compiler_params=SMALL,
    )(after, *arrays)


def pick_rows(near, far, slot_here, seqs, token):
    rows, width = near.shape

    def body(near_ref, far_ref, slot_ref, token_ref, out_ref):
        dp = lax.axis_index("dp")
        i = iota((NZ * seqs, 2 * rows), 0)
        wanted = (i // seqs * (NX * NC) + dp % (NX * NC)) * seqs + i % seqs
        pick = jnp.where(slot_ref[...] == wanted, 1.0, 0.0).astype(BF16)
        got = dot(pick[:, :rows], near_ref[...]) + dot(pick[:, rows:], far_ref[...])
        got = got.astype(BF16)
        for z in range(NZ):
            out_ref[z] = got[z * seqs : (z + 1) * seqs]

    return pl.pallas_call(
        body,
        out_shape=jax.ShapeDtypeStruct((NZ, seqs, width), BF16),
        in_specs=[vmem()] * 4,
        out_specs=vmem(),
        compiler_params=SMALL,
    )(near, far, slot_here, token)


def partial_scores(arrived, w_uk, latent_cache, rope_keys, scale):
    seqs, capacity, lat_part = latent_cache.shape
    heads, nope_dim, _ = w_uk.shape
    rope_part = rope_keys.shape[1]
    nope_width = heads * nope_dim
    rope_dim = arrived.shape[2] // heads - nope_dim
    ranks = lax.axis_size("rank")
    group = heads // ranks
    steps = capacity // BLOCK

    def body(arrived_ref, w_ref, cache, keys, *rest):
        outs, (lat_rows,) = rest[:ranks], rest[ranks:]
        rank = lax.axis_index("rank")
        query = arrived_ref[0].astype(F32)
        for z in range(1, NZ):
            query = query + arrived_ref[z].astype(F32)
        for h in range(heads):
            turned = (h // group - rank + ranks) % ranks * group + h % group
            lat_rows[pl.ds(pl.multiple_of(turned * seqs, seqs), seqs), :] = dot(
                query[:, h * nope_dim : (h + 1) * nope_dim].astype(BF16), w_ref[h]
            )
        rope_width = heads * rope_dim
        i, j = iota((rope_width, 128), 0), iota((rope_width, 128), 1)
        fold = (i % rope_dim - rank * rope_part == j) & (j < rope_part)
        fold = jnp.where(fold, 1.0, 0.0).astype(BF16)
        t = iota((heads, rope_width), 0)
        own_head = (t // group + rank) % ranks * group + t % group
        mine = own_head == iota((heads, rope_width), 1) // rope_dim
        for s in range(seqs):
            lat = lat_rows[pl.ds(s, heads, stride=seqs), :].astype(BF16)
            flat = jnp.broadcast_to(query[s : s + 1, nope_width:], (heads, rope_width))
            spread = jnp.where(mine, flat, 0.0).astype(BF16)
            rope = dot(spread, fold).astype(BF16)[:, :rope_part]
            for b in range(steps):
                at = pl.ds(b * BLOCK, BLOCK)
                part = lax.dot_general(
                    lat, cache[s, at, :], (((1,), (1,)), ((), ())), preferred_element_type=F32
                )
                part = (part + dot(rope, keys[s, :, at])) * scale
                for k in range(ranks):
                    outs[k][s * group : (s + 1) * group, at] = part[k * group : (k + 1) * group]

    return pl.pallas_call(
        body,
        out_shape=[jax.ShapeDtypeStruct((seqs * group, capacity), F32)] * ranks,
        in_specs=[vmem()] * 4,
        out_specs=[vmem()] * ranks,
        compiler_params=SMALL,
        scratch_shapes=[pltpu.VMEM((heads * seqs, lat_part), F32)],
    )(arrived, w_uk, latent_cache, rope_keys)


def softmax(parts, live):
    rows, capacity = parts[0].shape

    def body(*refs):
        *part_refs, live_ref, out_ref = refs
        total = part_refs[0][...]
        for ref in part_refs[1:]:
            total = total + ref[...]
        total = jnp.where(iota((rows, capacity), 1) < live_ref[...], total, -jnp.inf)
        raised = jnp.exp(total - jnp.max(total, axis=1, keepdims=True))
        out_ref[...] = (raised / jnp.sum(raised, axis=1, keepdims=True)).astype(BF16)

    return pl.pallas_call(
        body,
        out_shape=jax.ShapeDtypeStruct((rows, capacity), BF16),
        in_specs=[vmem()] * (len(parts) + 1),
        out_specs=vmem(),
        compiler_params=SMALL,
    )(*parts, live)


def head_part(weights, latent_cache, w_uv):
    seqs, capacity, lat_part = latent_cache.shape
    heads, _, value_dim = w_uv.shape
    ranks = len(weights)
    group = heads // ranks
    rows = seqs * group
    steps = capacity // BLOCK

    def body(*refs):
        weight_refs = refs[:ranks]
        cache, w_ref, out_ref, lat_rows = refs[ranks:]
        rank = lax.axis_index("rank")
        for s in range(seqs):
            total = jnp.zeros((ranks * rows, lat_part), F32)
            for b in range(steps):
                at = pl.ds(b * BLOCK, BLOCK)
                block = jnp.concatenate([ref[:, at] for ref in weight_refs], axis=0)
                total = total + dot(block, cache[s, at, :])
            lat_rows[s * ranks * rows : (s + 1) * ranks * rows, :] = total
        for k in range(ranks):
            for i in range(group):
                at = pl.ds(k * rows + i, seqs, stride=ranks * rows + group)
                lat = lat_rows[at, :].astype(BF16)
                head = (rank - k + ranks) % ranks * group + i
                out_ref[:, pl.ds(pl.multiple_of(head * value_dim, value_dim), value_dim)] = dot(
                    lat, w_ref[head]
                ).astype(BF16)

    return pl.pallas_call(
        body,
        out_shape=jax.ShapeDtypeStruct((seqs, heads * value_dim), BF16),
        in_specs=[vmem()] * (ranks + 2),
        out_specs=vmem(),
        compiler_params=SMALL,
        scratch_shapes=[pltpu.VMEM((seqs * ranks * rows, lat_part), F32)],
    )(*weights, latent_cache, w_uv)


def project(parts, w_out, copies):
    seqs = parts[0].shape[0]
    width = w_out.shape[1]

    def body(*refs):
        *part_refs, w_ref, out_ref = refs
        total = part_refs[0][...].astype(F32)
        for ref in part_refs[1:]:
            total = total + ref[...].astype(F32)
        out = dot(total.astype(BF16), w_ref[...]).astype(BF16)
        for d in range(copies):
            out_ref[d] = out

    return pl.pallas_call(
        body,
        out_shape=jax.ShapeDtypeStruct((copies, seqs, width), BF16),
        in_specs=[vmem()] * (len(parts) + 1),
        out_specs=vmem(),
        compiler_params=SMALL,
    )(*parts, w_out)


def bring_back(everyone, targets):
    devices, seqs, width = everyone.shape

    def body(all_ref, target_ref, out_ref):
        row = iota((seqs, width), 0)
        wanted = [jnp.broadcast_to(target_ref[j : j + 1, :], (seqs, width)) for j in range(seqs)]
        lines = [jnp.zeros((seqs, width), F32) for _ in range(seqs)]
        for d in range(devices):
            block = all_ref[d].astype(F32)
            for j in range(seqs):
                lines[j] = jnp.where(wanted[j] == row + d * seqs, block, lines[j])
        for j in range(seqs):
            mine = wanted[j] % seqs == row
            line = jnp.sum(jnp.where(mine, lines[j], 0.0), axis=0, keepdims=True)
            out_ref[j : j + 1, :] = line.astype(BF16)

    return pl.pallas_call(
        body,
        out_shape=jax.ShapeDtypeStruct((seqs, width), BF16),
        in_specs=[vmem()] * 2,
        out_specs=vmem(),
        compiler_params=SMALL,
    )(everyone, targets)


def per_device(q_nope, q_rope, latent_cache, rope_keys, lengths, slot_of, w_uk, w_uv, w_out):
    seqs = q_nope.shape[0]
    heads, nope_dim, _ = w_uk.shape
    scale = 1.0 / math.sqrt(nope_dim + q_rope.shape[1] // heads)
    seq_total = slot_of.shape[0]
    ranks = lax.axis_size("rank")
    z_groups, x_groups, c_groups = dp_groups()

    dp_pos = lax.axis_index("dp")
    plane_rows = 2 * NX * seqs
    at = jnp.arange(plane_rows, dtype=jnp.int32)
    from_c = (dp_pos % NC + at // (NX * seqs)) % NC
    from_x = (dp_pos // NC % NX + NX - at // seqs % NX) % NX
    row_of = ((dp_pos // (NC * NX) * NX + from_x) * NC + from_c) * seqs + at % seqs
    slot_here = jnp.sum(
        jnp.where(
            row_of[:, None] == jnp.arange(seq_total, dtype=jnp.int32)[None, :], slot_of[None, :], 0
        ),
        axis=1,
    ).reshape(1, plane_rows)

    live = jnp.repeat(lengths, heads // ranks).reshape(-1, 1)
    targets = lax.dynamic_slice_in_dim(slot_of, dp_pos * seqs, seqs).reshape(seqs, 1)

    rows = jnp.concatenate([q_nope, q_rope], axis=1)
    near = [rows] + [shifted(rows, "dp", x_groups, k) for k in range(1, NX)]
    near = jnp.concatenate(near, axis=0)
    far = shifted(near, "dp", c_groups, 1)
    token = fetch(rows, latent_cache, rope_keys, w_uk, live, targets)
    picked = pick_rows(near, far, slot_here, seqs, token)
    arrived = lax.all_to_all(picked, "dp", 0, 0, axis_index_groups=z_groups, tiled=True)

    own, *others = partial_scores(arrived, w_uk, latent_cache, rope_keys, scale)
    weights = softmax([own] + from_ranks(others), live)
    gathered = [weights] + from_ranks([weights] * (ranks - 1))
    value_part = head_part(gathered, latent_cache, w_uv)
    parts = [value_part] + from_ranks([value_part] * (ranks - 1))
    copies = project(parts, w_out, lax.axis_size("dp"))
    everyone = lax.all_to_all(copies, "dp", 0, 0, tiled=True)
    return bring_back(everyone, targets)


def solution(mesh):
    placed = (
        P("dp", None),
        P("dp", None),
        P("dp", None, "rank"),
        P("dp", "rank", None),
        P("dp"),
        P(),
        P(None, None, "rank"),
        P(None, "rank", None),
        P(None, "rank"),
    )
    return jax.shard_map(
        per_device, mesh=mesh, in_specs=placed, out_specs=P("dp", "rank"), check_vma=False
    )
```

time: 97.4 us -> 90.8 us (0.932)
  blocking collectives: 0 us -> 39.4 us
  waiting for transfers between devices: 41.1 us -> 20.6 us
  starting transfers between devices: 37.9 us -> 17.5 us
  matrix products: 11.6 us -> 0 us
  Pallas kernels: 0 us -> 5.16 us
  local copies, waits for them, and re-layouts: 4.54 us -> 7.39 us
  other arithmetic: 1.71 us -> 0.26 us
    all_to_all x0 -> x2, blocking collectives: none -> 39.4 us  [the longest x1 22 us: per_device(): everyone = lax.all_to_all(copies, 'dp', 0, 0, tiled=True)]
    all_to_all x2 -> x0, waiting for transfers between devices: 21.4 us -> none  [the longest x1 13 us: per_device(): lax.all_to_all(copies, 'dp', 0, 0, tiled=True).reshape(seq_total, -1)]
    all_to_all x2 -> x0, starting transfers between devices: 17.2 us -> none  [the longest x1 9.03 us: per_device(): lax.all_to_all(copies, 'dp', 0, 0, tiled=True).reshape(seq_total, -1)]
    dot_general x8 -> x0, matrix products: 11.6 us -> none  [the longest x1 3.38 us: per_device(): jnp.einsum('shl,stl->sht', turned_lat, latent_cache, preferred_element_ty...]
    pallas_call x0 -> x7, Pallas kernels: none -> 5.16 us  [the longest x1 2.28 us: partial_scores(): pl.pallas_call(body, out_shape=[jax.ShapeDtypeStruct((seqs * group, capac...]
    unnamed x8 -> x19, local copies, waits for them, and re-layouts: 0.02 us -> 5.03 us
    ppermute x13, starting transfers between devices: 20.6 us -> 17.5 us  [shifted(): return lax.ppermute(array, axis, pairs)]
    reshape x7 -> x2, local copies, waits for them, and re-layouts: 3.44 us -> 0.84 us  [per_device(): lax.dynamic_slice_in_dim(slot_of, dp_pos * seqs, seqs).reshape(seqs, 1)]
  transfers between devices with their start and end apart: 15 -> 13, of which waited for: 13 -> 9; matrix products, arithmetic and copies ran while one was open for 1% -> 2% of each run, Pallas kernels for 0% -> 0%
where the time goes in v2:
time: 90.8 us; the launch traced here: 90.5 us
  blocking collectives  39.4 us (43%)
  waiting for transfers between devices  20.6 us (23%)
  starting transfers between devices  17.5 us (19%)
  local copies, waits for them, and re-layouts  7.39 us (8%)
  Pallas kernels  5.16 us (6%)
    all_to_all x1, blocking collectives, per_device(): everyone = lax.all_to_all(copies, 'dp', 0, 0, tiled=True)  22 us
    ppermute x13, waiting for transfers between devices, shifted(): return lax.ppermute(array, axis, pairs)  20.6 us
    ppermute x13, starting transfers between devices, shifted(): return lax.ppermute(array, axis, pairs)  17.5 us
    all_to_all x1, blocking collectives, per_device(): lax.all_to_all(picked, 'dp', 0, 0, axis_index_groups=z_groups, tiled=True)  17.4 us
    unnamed x19, local copies, waits for them, and re-layouts  5.03 us
    pallas_call x1, Pallas kernels, partial_scores(): pl.pallas_call(body, out_shape=[jax.ShapeDtypeStruct((seqs * group, capac...  2.28 us
  transfers between devices with their start and end apart: 13, of which 9 were waited for; matrix products, arithmetic and copies ran while one was open for 2% of the time, Pallas kernels for 0%

profile of v2, /device:TPU:1, one launch (start us, length us, event | category | flops | bytes accessed | tf_op | source)
XLA Modules:
  0.0 90.5 jit_solution(13956662415643694685)
XLA Ops:
  0.0 0.7 constant_dynamic-update-slice_fusion.1
  0.7 0.7 constant_dynamic-update-slice_fusion.refs_0_
  1.4 3.3 %collective-permute-start.2 = (bf16[4,3072]{1,0:T(4,128)(2,1)S(1)}, bf16[4,3072]{1,0:T(4,128)(2,1)S(1)}, u32[]{:S(2)}, u32[]{:S(2)}) collective-permute-start(bf16[4,3072]{1,0:T(4,128)(2,1)S(1)} %constant_dynamic-update-slice_fusion.refs_0_), channel_id=1, source_target_pairs={{0,24},{8,0},{16,8},{24,16},{4,28},{12,4},{20,12},{28,20},{32,56},... | collective-permute-start | bytes 73736 | tf_op jit(solution)/shard_map/ppermute | solution.py:22
  4.7 0.5 collective-permute-start.1
  5.3 0.6 collective-permute-start
  5.9 0.8 dynamic-slice_bitcast_fusion
  6.6 0.1 copy.15.refs_5_.target_ref
  6.7 0.7 broadcast_in_dim.20
  7.5 0.1 reshape_reshape.4.refs_4_
  7.5 2.2 %copy-done = bf16[4,4096,128]{2,1,0:T(8,128)(2,1)S(1)} copy-done((bf16[4,4096,128]{2,1,0:T(8,128)(2,1)S(1)}, bf16[4,4096,128]{2,1,0:T(8,128)(2,1)}, u32[]{:S(2)}) %copy-start) | copy-done | bytes 4194328
  9.7 1.0 %copy-done.3 = bf16[4,16,4096]{2,1,0:T(8,128)(2,1)S(1)} copy-done((bf16[4,16,4096]{2,1,0:T(8,128)(2,1)S(1)}, bf16[4,16,4096]{2,1,0:T(8,128)(2,1)}, u32[]{:S(2)}) %copy-start.3) | copy-done | bytes 524312
  10.8 1.0 %copy-done.5 = bf16[16,128,128]{2,1,0:T(8,128)(2,1)S(1)} copy-done((bf16[16,128,128]{2,1,0:T(8,128)(2,1)S(1)}, bf16[16,128,128]{2,1,0:T(8,128)(2,1)}, u32[]{:S(2)}) %copy-start.5) | copy-done | bytes 524312
  11.8 0.0 copy-start.7
  11.8 0.0 collective-permute-done.2
  11.8 0.0 collective-permute-done.1
  11.9 0.0 collective-permute-done
  11.9 0.1 pad_maximum_fusion.near_ref
  11.9 1.6 %collective-permute-start.3 = (bf16[16,3072]{1,0:T(8,128)(2,1)S(1)}, bf16[16,3072]{1,0:T(8,128)(2,1)S(1)}, u32[]{:S(2)}, u32[]{:S(2)}) collective-permute-start(bf16[16,3072]{1,0:T(8,128)(2,1)S(1)} %pad_maximum_fusion.near_ref), channel_id=1, source_target_pairs={{0,4},{4,0},{8,12},{12,8},{16,20},{20,16},{24,28},{28,24},{32,36},... | collective-permute-start | bytes 294920 | tf_op jit(solution)/shard_map/ppermute | solution.py:22
  13.5 0.0 copy-done.8
  13.5 0.2 select_reduce_fusion
  13.7 0.8 collective-permute-done.3.far_ref
  14.5 0.3 shard_map.92
  14.8 17.4 %all_to_all.10.arrived_ref = bf16[8,4,3072]{2,1,0:T(4,128)(2,1)S(1)} all-to-all(bf16[8,4,3072]{2,1,0:T(4,128)(2,1)S(1)} %shard_map.92), channel_id=1, replica_groups={{0,32,64,96,128,160,192,224},{4,36,68,100,132,164,196,228},{8,40,72,104..., dimensions={0} | all-to-all | bytes 393216 | tf_op jit(solution)/shard_map/all_to_all | solution.py:272
  32.2 0.0 copy-done.4
  32.2 2.3 %shard_map.93 = (f32[16,4096]{1,0:T(8,128)S(1)}, f32[16,4096]{1,0:T(8,128)S(1)}, f32[16,4096]{1,0:T(8,128)S(1)}, f32[16,4096]{1,0:T(8,128)S(1)}) custom-call(bf16[8,4,3072]{2,1,0:T(4,128)(2,1)S(1)} %all_to_all.10.arrived_ref, bf16[16,128,128]{2,1,0:T(8,128)(2,1)S(1)} %copy-done.6, bf16[4,4096,128]{2,1,0:T(8,128)(2,1)S(1)} %copy-done.1, ...), custom_call_target="tpu_custom_call" | custom-call | tf_op jit(solution)/shard_map/pallas_call | solution.py:126
  34.5 1.4 %collective-permute-start.4 = (f32[16,4096]{1,0:T(8,128)S(1)}, f32[16,4096]{1,0:T(8,128)S(1)}, u32[]{:S(2)}, u32[]{:S(2)}) collective-permute-start(f32[16,4096]{1,0:T(8,128)S(1)} %get-tuple-element.10), channel_id=1, source_target_pairs={{0,1},{1,2},{2,3},{3,0},{4,5},{5,6},{6,7},{7,4},{8,9},{9,10},{10,1... | collective-permute-start | bytes 786440 | tf_op jit(solution)/shard_map/ppermute | solution.py:22
  35.9 2.6 %collective-permute-start.5 = (f32[16,4096]{1,0:T(8,128)S(1)}, f32[16,4096]{1,0:T(8,128)S(1)}, u32[]{:S(2)}, u32[]{:S(2)}) collective-permute-start(f32[16,4096]{1,0:T(8,128)S(1)} %get-tuple-element.11), channel_id=1, source_target_pairs={{0,2},{1,3},{2,0},{3,1},{4,6},{5,7},{6,4},{7,5},{8,10},{9,11},{10,... | collective-permute-start | bytes 786440 | tf_op jit(solution)/shard_map/ppermute | solution.py:22
  38.5 1.1 %collective-permute-start.6 = (f32[16,4096]{1,0:T(8,128)S(1)}, f32[16,4096]{1,0:T(8,128)S(1)}, u32[]{:S(2)}, u32[]{:S(2)}) collective-permute-start(f32[16,4096]{1,0:T(8,128)S(1)} %get-tuple-element.12), channel_id=1, source_target_pairs={{0,3},{1,0},{2,1},{3,2},{4,7},{5,4},{6,5},{7,6},{8,11},{9,8},{10,9... | collective-permute-start | bytes 786440 | tf_op jit(solution)/shard_map/ppermute | solution.py:22
  39.6 2.2 %collective-permute-done.4.refs_1_ = f32[16,4096]{1,0:T(8,128)S(1)} collective-permute-done((f32[16,4096]{1,0:T(8,128)S(1)}, f32[16,4096]{1,0:T(8,128)S(1)}, u32[]{:S(2)}, u32[]{:S(2)}) %collective-permute-start.4) | collective-permute-done | bytes 262176 | tf_op jit(solution)/shard_map/ppermute | solution.py:22
  41.8 6.7 %collective-permute-done.5.refs_2_ = f32[16,4096]{1,0:T(8,128)S(1)} collective-permute-done((f32[16,4096]{1,0:T(8,128)S(1)}, f32[16,4096]{1,0:T(8,128)S(1)}, u32[]{:S(2)}, u32[]{:S(2)}) %collective-permute-start.5) | collective-permute-done | bytes 262176 | tf_op jit(solution)/shard_map/ppermute | solution.py:22
  48.5 0.0 collective-permute-done.6.refs_3_
  48.6 0.3 shard_map.94.refs_0_
  48.9 3.5 %collective-permute-start.9 = (bf16[16,4096]{1,0:T(8,128)(2,1)S(1)}, bf16[16,4096]{1,0:T(8,128)(2,1)S(1)}, u32[]{:S(2)}, u32[]{:S(2)}) collective-permute-start(bf16[16,4096]{1,0:T(8,128)(2,1)S(1)} %shard_map.94.refs_0_), channel_id=1, source_target_pairs={{0,3},{1,0},{2,1},{3,2},{4,7},{5,4},{6,5},{7,6},{8,11},{9,8},{10,9... | collective-permute-start | bytes 393224 | tf_op jit(solution)/shard_map/ppermute | solution.py:22
  52.4 1.0 %collective-permute-start.8 = (bf16[16,4096]{1,0:T(8,128)(2,1)S(1)}, bf16[16,4096]{1,0:T(8,128)(2,1)S(1)}, u32[]{:S(2)}, u32[]{:S(2)}) collective-permute-start(bf16[16,4096]{1,0:T(8,128)(2,1)S(1)} %shard_map.94.refs_0_), channel_id=1, source_target_pairs={{0,2},{1,3},{2,0},{3,1},{4,6},{5,7},{6,4},{7,5},{8,10},{9,11},{10,... | collective-permute-start | bytes 393224 | tf_op jit(solution)/shard_map/ppermute | solution.py:22
  53.4 0.0 collective-permute-start.7
  53.4 2.9 %collective-permute-done.9.refs_3_ = bf16[16,4096]{1,0:T(8,128)(2,1)S(1)} collective-permute-done((bf16[16,4096]{1,0:T(8,128)(2,1)S(1)}, bf16[16,4096]{1,0:T(8,128)(2,1)S(1)}, u32[]{:S(2)}, u32[]{:S(2)}) %collective-permute-start.9) | collective-permute-done | bytes 131104 | tf_op jit(solution)/shard_map/ppermute | solution.py:22
  56.2 1.6 %collective-permute-done.8.refs_2_ = bf16[16,4096]{1,0:T(8,128)(2,1)S(1)} collective-permute-done((bf16[16,4096]{1,0:T(8,128)(2,1)S(1)}, bf16[16,4096]{1,0:T(8,128)(2,1)S(1)}, u32[]{:S(2)}, u32[]{:S(2)}) %collective-permute-start.8) | collective-permute-done | bytes 131104 | tf_op jit(solution)/shard_map/ppermute | solution.py:22
  57.8 3.4 %collective-permute-done.7.refs_1_ = bf16[16,4096]{1,0:T(8,128)(2,1)S(1)} collective-permute-done((bf16[16,4096]{1,0:T(8,128)(2,1)S(1)}, bf16[16,4096]{1,0:T(8,128)(2,1)S(1)}, u32[]{:S(2)}, u32[]{:S(2)}) %collective-permute-start.7) | collective-permute-done | bytes 131104 | tf_op jit(solution)/shard_map/ppermute | solution.py:22
  61.2 1.0 %shard_map.95.refs_0_ = bf16[4,2048]{1,0:T(4,128)(2,1)S(1)} custom-call(bf16[16,4096]{1,0:T(8,128)(2,1)S(1)} %shard_map.94.refs_0_, bf16[16,4096]{1,0:T(8,128)(2,1)S(1)} %collective-permute-done.7.refs_1_, bf16[16,4096]{1,0:T(8,128)(2,1)S(1)} %collective-permute-done.8.refs_2_, bf16[16,4096]{1,0:T(8,128)(2,1)S(1)} %collective-permute-done.9.refs_3_, ...), custom_call_target="tpu_custom_call" | custom-call | tf_op jit(solution)/shard_map/pallas_call | solution.py:185
  62.1 0.1 collective-permute-start.12
  62.2 1.1 %collective-permute-start.11 = (bf16[4,2048]{1,0:T(4,128)(2,1)S(1)}, bf16[4,2048]{1,0:T(4,128)(2,1)S(1)}, u32[]{:S(2)}, u32[]{:S(2)}) collective-permute-start(bf16[4,2048]{1,0:T(4,128)(2,1)S(1)} %shard_map.95.refs_0_), channel_id=1, source_target_pairs={{0,2},{1,3},{2,0},{3,1},{4,6},{5,7},{6,4},{7,5},{8,10},{9,11},{10,... | collective-permute-start | bytes 49160 | tf_op jit(solution)/shard_map/ppermute | solution.py:22
  63.4 0.8 collective-permute-start.10
  64.1 0.7 collective-permute-done.12.refs_3_
  64.8 1.6 %collective-permute-done.11.refs_2_ = bf16[4,2048]{1,0:T(4,128)(2,1)S(1)} collective-permute-done((bf16[4,2048]{1,0:T(4,128)(2,1)S(1)}, bf16[4,2048]{1,0:T(4,128)(2,1)S(1)}, u32[]{:S(2)}, u32[]{:S(2)}) %collective-permute-start.11) | collective-permute-done | bytes 16416 | tf_op jit(solution)/shard_map/ppermute | solution.py:22
  66.4 0.8 collective-permute-done.10.refs_1_
  67.2 0.4 shard_map.96
  67.6 22.0 %all_to_all.11.all_ref = bf16[64,4,512]{2,1,0:T(4,128)(2,1)S(1)} all-to-all(bf16[64,4,512]{2,1,0:T(4,128)(2,1)S(1)} %shard_map.96), channel_id=1, replica_groups=mesh['dp'=64,'rank'=4] {'dp'}, dimensions={0} | all-to-all | bytes 524288 | tf_op jit(solution)/shard_map/all_to_all | solution.py:280
  89.6 0.9 shard_map.97
  (14 shorter events, 0.0 us)
Async XLA Ops:
  0.0 13.5 %copy-start.8 = (s32[256]{0:T(256)S(1)}, s32[256]{0:T(256)}, u32[]{:S(2)}) copy-start(s32[256]{0:T(256)} %param.14) | copy-start | bytes 3076
  1.4 10.4 %collective-permute-start.2 = (bf16[4,3072]{1,0:T(4,128)(2,1)S(1)}, bf16[4,3072]{1,0:T(4,128)(2,1)S(1)}, u32[]{:S(2)}, u32[]{:S(2)}) collective-permute-start(bf16[4,3072]{1,0:T(4,128)(2,1)S(1)} %constant_dynamic-update-slice_fusion.refs_0_), channel_id=1, source_target_pairs={{0,24},{8,0},{16,8},{24,16},{4,28},{12,4},{20,12},{28,20},{32,56},... | collective-permute-start | bytes 73736 | tf_op jit(solution)/shard_map/ppermute | solution.py:22
  4.7 7.1 %collective-permute-start.1 = (bf16[4,3072]{1,0:T(4,128)(2,1)S(1)}, bf16[4,3072]{1,0:T(4,128)(2,1)S(1)}, u32[]{:S(2)}, u32[]{:S(2)}) collective-permute-start(bf16[4,3072]{1,0:T(4,128)(2,1)S(1)} %constant_dynamic-update-slice_fusion.refs_0_), channel_id=1, source_target_pairs={{0,16},{8,24},{16,0},{24,8},{4,20},{12,28},{20,4},{28,12},{32,48},... | collective-permute-start | bytes 73736 | tf_op jit(solution)/shard_map/ppermute | solution.py:22
  5.3 6.6 %collective-permute-start = (bf16[4,3072]{1,0:T(4,128)(2,1)S(1)}, bf16[4,3072]{1,0:T(4,128)(2,1)S(1)}, u32[]{:S(2)}, u32[]{:S(2)}) collective-permute-start(bf16[4,3072]{1,0:T(4,128)(2,1)S(1)} %constant_dynamic-update-slice_fusion.refs_0_), channel_id=1, source_target_pairs={{0,8},{8,16},{16,24},{24,0},{4,12},{12,20},{20,28},{28,4},{32,40},... | collective-permute-start | bytes 73736 | tf_op jit(solution)/shard_map/ppermute | solution.py:22
  7.5 2.2 %copy-start = (bf16[4,4096,128]{2,1,0:T(8,128)(2,1)S(1)}, bf16[4,4096,128]{2,1,0:T(8,128)(2,1)}, u32[]{:S(2)}) copy-start(bf16[4,4096,128]{2,1,0:T(8,128)(2,1)} %refs_4_.2) | copy-start | bytes 12582916
  9.7 1.0 %copy-start.3 = (bf16[4,16,4096]{2,1,0:T(8,128)(2,1)S(1)}, bf16[4,16,4096]{2,1,0:T(8,128)(2,1)}, u32[]{:S(2)}) copy-start(bf16[4,16,4096]{2,1,0:T(8,128)(2,1)} %keys.1) | copy-start | bytes 1572868
  10.8 1.0 %copy-start.5 = (bf16[16,128,128]{2,1,0:T(8,128)(2,1)S(1)}, bf16[16,128,128]{2,1,0:T(8,128)(2,1)}, u32[]{:S(2)}) copy-start(bf16[16,128,128]{2,1,0:T(8,128)(2,1)} %w_ref.1) | copy-start | bytes 1572868
  11.8 20.4 %copy-start.1 = (bf16[4,4096,128]{2,1,0:T(8,128)(2,1)S(1)}, bf16[4,4096,128]{2,1,0:T(8,128)(2,1)}, u32[]{:S(2)}) copy-start(bf16[4,4096,128]{2,1,0:T(8,128)(2,1)} %refs_4_.2) | copy-start | bytes 12582916
  11.8 20.4 %copy-start.4 = (bf16[4,16,4096]{2,1,0:T(8,128)(2,1)S(1)}, bf16[4,16,4096]{2,1,0:T(8,128)(2,1)}, u32[]{:S(2)}) copy-start(bf16[4,16,4096]{2,1,0:T(8,128)(2,1)} %keys.1) | copy-start | bytes 1572868
  11.8 20.4 %copy-start.6 = (bf16[16,128,128]{2,1,0:T(8,128)(2,1)S(1)}, bf16[16,128,128]{2,1,0:T(8,128)(2,1)}, u32[]{:S(2)}) copy-start(bf16[16,128,128]{2,1,0:T(8,128)(2,1)} %w_ref.1) | copy-start | bytes 1572868
  11.8 49.3 %copy-start.7 = (bf16[16,128,128]{2,1,0:T(8,128)(2,1)S(1)}, bf16[16,128,128]{2,1,0:T(8,128)(2,1)}, u32[]{:S(2)}) copy-start(bf16[16,128,128]{2,1,0:T(8,128)(2,1)} %refs_5_.1) | copy-start | bytes 1572868
  11.9 2.5 %collective-permute-start.3 = (bf16[16,3072]{1,0:T(8,128)(2,1)S(1)}, bf16[16,3072]{1,0:T(8,128)(2,1)S(1)}, u32[]{:S(2)}, u32[]{:S(2)}) collective-permute-start(bf16[16,3072]{1,0:T(8,128)(2,1)S(1)} %pad_maximum_fusion.near_ref), channel_id=1, source_target_pairs={{0,4},{4,0},{8,12},{12,8},{16,20},{20,16},{24,28},{28,24},{32,36},... | collective-permute-start | bytes 294920 | tf_op jit(solution)/shard_map/ppermute | solution.py:22
  34.5 32.7 %copy-start.2 = (bf16[2048,512]{1,0:T(8,128)(2,1)S(1)}, bf16[2048,512]{1,0:T(8,128)(2,1)}, u32[]{:S(2)}) copy-start(bf16[2048,512]{1,0:T(8,128)(2,1)} %refs_4_.3) | copy-start | bytes 6291460
  34.5 7.3 %collective-permute-start.4 = (f32[16,4096]{1,0:T(8,128)S(1)}, f32[16,4096]{1,0:T(8,128)S(1)}, u32[]{:S(2)}, u32[]{:S(2)}) collective-permute-start(f32[16,4096]{1,0:T(8,128)S(1)} %get-tuple-element.10), channel_id=1, source_target_pairs={{0,1},{1,2},{2,3},{3,0},{4,5},{5,6},{6,7},{7,4},{8,9},{9,10},{10,1... | collective-permute-start | bytes 786440 | tf_op jit(solution)/shard_map/ppermute | solution.py:22
  35.9 12.7 %collective-permute-start.5 = (f32[16,4096]{1,0:T(8,128)S(1)}, f32[16,4096]{1,0:T(8,128)S(1)}, u32[]{:S(2)}, u32[]{:S(2)}) collective-permute-start(f32[16,4096]{1,0:T(8,128)S(1)} %get-tuple-element.11), channel_id=1, source_target_pairs={{0,2},{1,3},{2,0},{3,1},{4,6},{5,7},{6,4},{7,5},{8,10},{9,11},{10,... | collective-permute-start | bytes 786440 | tf_op jit(solution)/shard_map/ppermute | solution.py:22
  38.5 10.1 %collective-permute-start.6 = (f32[16,4096]{1,0:T(8,128)S(1)}, f32[16,4096]{1,0:T(8,128)S(1)}, u32[]{:S(2)}, u32[]{:S(2)}) collective-permute-start(f32[16,4096]{1,0:T(8,128)S(1)} %get-tuple-element.12), channel_id=1, source_target_pairs={{0,3},{1,0},{2,1},{3,2},{4,7},{5,4},{6,5},{7,6},{8,11},{9,8},{10,9... | collective-permute-start | bytes 786440 | tf_op jit(solution)/shard_map/ppermute | solution.py:22
  48.9 7.3 %collective-permute-start.9 = (bf16[16,4096]{1,0:T(8,128)(2,1)S(1)}, bf16[16,4096]{1,0:T(8,128)(2,1)S(1)}, u32[]{:S(2)}, u32[]{:S(2)}) collective-permute-start(bf16[16,4096]{1,0:T(8,128)(2,1)S(1)} %shard_map.94.refs_0_), channel_id=1, source_target_pairs={{0,3},{1,0},{2,1},{3,2},{4,7},{5,4},{6,5},{7,6},{8,11},{9,8},{10,9... | collective-permute-start | bytes 393224 | tf_op jit(solution)/shard_map/ppermute | solution.py:22
  52.4 5.4 %collective-permute-start.8 = (bf16[16,4096]{1,0:T(8,128)(2,1)S(1)}, bf16[16,4096]{1,0:T(8,128)(2,1)S(1)}, u32[]{:S(2)}, u32[]{:S(2)}) collective-permute-start(bf16[16,4096]{1,0:T(8,128)(2,1)S(1)} %shard_map.94.refs_0_), channel_id=1, source_target_pairs={{0,2},{1,3},{2,0},{3,1},{4,6},{5,7},{6,4},{7,5},{8,10},{9,11},{10,... | collective-permute-start | bytes 393224 | tf_op jit(solution)/shard_map/ppermute | solution.py:22
  53.4 7.8 %collective-permute-start.7 = (bf16[16,4096]{1,0:T(8,128)(2,1)S(1)}, bf16[16,4096]{1,0:T(8,128)(2,1)S(1)}, u32[]{:S(2)}, u32[]{:S(2)}) collective-permute-start(bf16[16,4096]{1,0:T(8,128)(2,1)S(1)} %shard_map.94.refs_0_), channel_id=1, source_target_pairs={{0,1},{1,2},{2,3},{3,0},{4,5},{5,6},{6,7},{7,4},{8,9},{9,10},{10,1... | collective-permute-start | bytes 393224 | tf_op jit(solution)/shard_map/ppermute | solution.py:22
  62.1 2.6 %collective-permute-start.12 = (bf16[4,2048]{1,0:T(4,128)(2,1)S(1)}, bf16[4,2048]{1,0:T(4,128)(2,1)S(1)}, u32[]{:S(2)}, u32[]{:S(2)}) collective-permute-start(bf16[4,2048]{1,0:T(4,128)(2,1)S(1)} %shard_map.95.refs_0_), channel_id=1, source_target_pairs={{0,3},{1,0},{2,1},{3,2},{4,7},{5,4},{6,5},{7,6},{8,11},{9,8},{10,9... | collective-permute-start | bytes 49160 | tf_op jit(solution)/shard_map/ppermute | solution.py:22
  62.2 4.2 %collective-permute-start.11 = (bf16[4,2048]{1,0:T(4,128)(2,1)S(1)}, bf16[4,2048]{1,0:T(4,128)(2,1)S(1)}, u32[]{:S(2)}, u32[]{:S(2)}) collective-permute-start(bf16[4,2048]{1,0:T(4,128)(2,1)S(1)} %shard_map.95.refs_0_), channel_id=1, source_target_pairs={{0,2},{1,3},{2,0},{3,1},{4,6},{5,7},{6,4},{7,5},{8,10},{9,11},{10,... | collective-permute-start | bytes 49160 | tf_op jit(solution)/shard_map/ppermute | solution.py:22
  63.4 3.8 %collective-permute-start.10 = (bf16[4,2048]{1,0:T(4,128)(2,1)S(1)}, bf16[4,2048]{1,0:T(4,128)(2,1)S(1)}, u32[]{:S(2)}, u32[]{:S(2)}) collective-permute-start(bf16[4,2048]{1,0:T(4,128)(2,1)S(1)} %shard_map.95.refs_0_), channel_id=1, source_target_pairs={{0,1},{1,2},{2,3},{3,0},{4,5},{5,6},{6,7},{7,4},{8,9},{9,10},{10,1... | collective-permute-start | bytes 49160 | tf_op jit(solution)/shard_map/ppermute | solution.py:22

commit v3 on v2

--- a/solution.py
+++ b/solution.py
@@ -30,14 +30,25 @@
 
 
 F32, BF16 = jnp.float32, jnp.bfloat16
-BLOCK = 1024
-SMALL = pltpu.CompilerParams(vmem_limit_bytes=16 << 20)
+BLOCK = 512
+SIZES = (9216, 10240, 12288)
+SMALL = pltpu.CompilerParams(vmem_limit_bytes=8 << 20)
+SCORES = pltpu.CompilerParams(vmem_limit_bytes=8 << 20)
+LARGE = pltpu.CompilerParams(vmem_limit_bytes=40 << 20)
 
 
 def vmem():
     return pl.BlockSpec(memory_space=pltpu.VMEM)
 
 
+def smem():
+    return pl.BlockSpec(memory_space=pltpu.SMEM)
+
+
+def hbm():
+    return pl.BlockSpec(memory_space=pltpu.HBM)
+
+
 def dot(a, b):
     return jnp.dot(a, b, preferred_element_type=F32)
 
@@ -46,23 +57,35 @@
     return lax.broadcasted_iota(jnp.int32, shape, dim)
 
 
-def fetch(after, *arrays):
-    def body(*refs):
-        refs[-1][...] = jnp.zeros(refs[-1].shape, F32)
-
-    return pl.pallas_call(
-        body,
-        out_shape=jax.ShapeDtypeStruct((8, 128), F32),
-        in_specs=[vmem()] * (1 + len(arrays)),
-        out_specs=vmem(),
-        compiler_params=SMALL,
-    )(after, *arrays)
-
-
-def pick_rows(near, far, slot_here, seqs, token):
+def join(q_nope, q_rope):
+    seqs, nope_width = q_nope.shape
+    width = nope_width + q_rope.shape[1]
+
+    def body(nope_ref, rope_ref, out_ref, sems):
+        copies = [
+            pltpu.make_async_copy(nope_ref, out_ref.at[:, :nope_width], sems.at[0]),
+            pltpu.make_async_copy(rope_ref, out_ref.at[:, nope_width:], sems.at[1]),
+        ]
+        for copy in copies:
+            copy.start()
+        for copy in copies:
+            copy.wait()
+
+    return pl.pallas_call(
+        body,
+        out_shape=jax.ShapeDtypeStruct((seqs, width), BF16),
+        in_specs=[hbm()] * 2,
+        out_specs=vmem(),
+        scratch_shapes=[pltpu.SemaphoreType.DMA((2,))],
+        compiler_params=LARGE,
+    )(q_nope, q_rope)
+
+
+def pick_rows(near, far, slot_here, seqs, ready):
     rows, width = near.shape
 
-    def body(near_ref, far_ref, slot_ref, token_ref, out_ref):
+    def body(near_ref, far_ref, slot_ref, *rest):
+        out_ref = rest[-1]
         dp = lax.axis_index("dp")
         i = iota((NZ * seqs, 2 * rows), 0)
         wanted = (i // seqs * (NX * NC) + dp % (NX * NC)) * seqs + i % seqs
@@ -75,13 +98,17 @@
     return pl.pallas_call(
         body,
         out_shape=jax.ShapeDtypeStruct((NZ, seqs, width), BF16),
-        in_specs=[vmem()] * 4,
+        in_specs=[vmem()] * (3 + len(ready)),
         out_specs=vmem(),
         compiler_params=SMALL,
-    )(near, far, slot_here, token)
-
-
-def partial_scores(arrived, w_uk, latent_cache, rope_keys, scale):
+    )(near, far, slot_here, *ready)
+
+
+def live_rows(bounds_ref, pos, slot):
+    return (pos >= bounds_ref[slot : slot + 1, :1]) & (pos < bounds_ref[8 + slot : 9 + slot, :1])
+
+
+def partial_scores(arrived, lengths, w_uk, latent_cache, rope_keys, packed, scale):
     seqs, capacity, lat_part = latent_cache.shape
     heads, nope_dim, _ = w_uk.shape
     rope_part = rope_keys.shape[1]
@@ -89,11 +116,41 @@
     rope_dim = arrived.shape[2] // heads - nope_dim
     ranks = lax.axis_size("rank")
     group = heads // ranks
-    steps = capacity // BLOCK
-
-    def body(arrived_ref, w_ref, cache, keys, *rest):
-        outs, (lat_rows,) = rest[:ranks], rest[ranks:]
+    blocks, half = packed // BLOCK, packed // BLOCK // 2
+
+    def body(arrived_ref, len_ref, w_ref, cache_ref, keys_ref, *rest):
+        outs, rest = rest[:ranks], rest[ranks:]
+        bounds_ref, cache, keys, lat_rows, lat_slots, rope_slots, sems, key_sems = rest
         rank = lax.axis_index("rank")
+        counts = [(len_ref[s] + BLOCK - 1) // BLOCK for s in range(seqs)]
+        starts = [jnp.int32(0)]
+        for s in range(seqs):
+            starts.append(starts[-1] + counts[s])
+        slots, copies = [], []
+        for b in range(blocks):
+            slot = jnp.int32(0)
+            start = jnp.int32(0)
+            for s in range(1, seqs):
+                slot = jnp.where(b >= starts[s], s, slot)
+                start = jnp.where(b >= starts[s], starts[s], start)
+            block = jnp.minimum(b - start, capacity // BLOCK - 1)
+            source = pl.ds(pl.multiple_of(block * BLOCK, BLOCK), BLOCK)
+            at = pl.ds(b * BLOCK, BLOCK)
+            copies.append(
+                (
+                    pltpu.make_async_copy(cache_ref.at[slot, source], cache.at[at], sems.at[b]),
+                    pltpu.make_async_copy(
+                        keys_ref.at[slot, :, source], keys.at[:, at], key_sems.at[b]
+                    ),
+                )
+            )
+            for copy in copies[-1]:
+                copy.start()
+            slots.append(slot)
+        for s in range(seqs):
+            first = starts[s] * BLOCK
+            bounds_ref[s : s + 1, :] = jnp.full((1, 128), first, jnp.int32)
+            bounds_ref[8 + s : 9 + s, :] = jnp.full((1, 128), first + len_ref[s], jnp.int32)
         query = arrived_ref[0].astype(F32)
         for z in range(1, NZ):
             query = query + arrived_ref[z].astype(F32)
@@ -110,73 +167,107 @@
         own_head = (t // group + rank) % ranks * group + t % group
         mine = own_head == iota((heads, rope_width), 1) // rope_dim
         for s in range(seqs):
-            lat = lat_rows[pl.ds(s, heads, stride=seqs), :].astype(BF16)
+            lat_slots[s] = lat_rows[pl.ds(s, heads, stride=seqs), :].astype(BF16)
             flat = jnp.broadcast_to(query[s : s + 1, nope_width:], (heads, rope_width))
-            spread = jnp.where(mine, flat, 0.0).astype(BF16)
-            rope = dot(spread, fold).astype(BF16)[:, :rope_part]
-            for b in range(steps):
-                at = pl.ds(b * BLOCK, BLOCK)
-                part = lax.dot_general(
-                    lat, cache[s, at, :], (((1,), (1,)), ((), ())), preferred_element_type=F32
-                )
-                part = (part + dot(rope, keys[s, :, at])) * scale
-                for k in range(ranks):
-                    outs[k][s * group : (s + 1) * group, at] = part[k * group : (k + 1) * group]
-
-    return pl.pallas_call(
-        body,
-        out_shape=[jax.ShapeDtypeStruct((seqs * group, capacity), F32)] * ranks,
-        in_specs=[vmem()] * 4,
-        out_specs=[vmem()] * ranks,
-        compiler_params=SMALL,
-        scratch_shapes=[pltpu.VMEM((heads * seqs, lat_part), F32)],
-    )(arrived, w_uk, latent_cache, rope_keys)
-
-
-def softmax(parts, live):
-    rows, capacity = parts[0].shape
+            rope_slots[s] = dot(jnp.where(mine, flat, 0.0).astype(BF16), fold).astype(BF16)
+        for b in range(blocks):
+            for copy in copies[b]:
+                copy.wait()
+            at = pl.ds(b * BLOCK, BLOCK)
+            part = lax.dot_general(
+                lat_slots[slots[b]],
+                cache[at, :],
+                (((1,), (1,)), ((), ())),
+                preferred_element_type=F32,
+            )
+            part = (part + dot(rope_slots[slots[b]][:, :rope_part], keys[:, at])) * scale
+            row, to = b // half * group, pl.ds(b % half * BLOCK, BLOCK)
+            for k in range(ranks):
+                outs[k][row : row + group, to] = part[k * group : (k + 1) * group]
+
+    return pl.pallas_call(
+        body,
+        out_shape=[jax.ShapeDtypeStruct((2 * group, packed // 2), F32)] * ranks
+        + [
+            jax.ShapeDtypeStruct((16, 128), jnp.int32),
+            jax.ShapeDtypeStruct((packed, lat_part), BF16),
+        ],
+        in_specs=[vmem(), smem(), vmem(), hbm(), hbm()],
+        out_specs=[vmem()] * (ranks + 2),
+        compiler_params=SCORES,
+        scratch_shapes=[
+            pltpu.VMEM((rope_part, packed), BF16),
+            pltpu.VMEM((heads * seqs, lat_part), F32),
+            pltpu.VMEM((seqs, heads, lat_part), BF16),
+            pltpu.VMEM((seqs, heads, 128), BF16),
+            pltpu.SemaphoreType.DMA((blocks,)),
+            pltpu.SemaphoreType.DMA((blocks,)),
+        ],
+    )(arrived, lengths, w_uk, latent_cache, rope_keys)
+
+
+def softmax(parts, bounds, seqs):
+    rows, width = parts[0].shape
 
     def body(*refs):
-        *part_refs, live_ref, out_ref = refs
+        *part_refs, bounds_ref, out_ref = refs
         total = part_refs[0][...]
         for ref in part_refs[1:]:
             total = total + ref[...]
-        total = jnp.where(iota((rows, capacity), 1) < live_ref[...], total, -jnp.inf)
-        raised = jnp.exp(total - jnp.max(total, axis=1, keepdims=True))
-        out_ref[...] = (raised / jnp.sum(raised, axis=1, keepdims=True)).astype(BF16)
-
-    return pl.pallas_call(
-        body,
-        out_shape=jax.ShapeDtypeStruct((rows, capacity), BF16),
+        pos = iota((rows, width), 1) + iota((rows, width), 0) // (rows // 2) * width
+        live = [live_rows(bounds_ref, pos, s) for s in range(seqs)]
+        top = jnp.full((rows, width), jnp.inf, F32)
+        for s in range(seqs):
+            most = jnp.max(jnp.where(live[s], total, -jnp.inf), axis=1, keepdims=True)
+            most = jnp.maximum(most, jnp.concatenate([most[rows // 2 :], most[: rows // 2]], axis=0))
+            top = jnp.where(live[s], most, top)
+        raised = jnp.exp(jnp.where(top < jnp.inf, total - top, -jnp.inf))
+        below = jnp.ones((rows, width), F32)
+        for s in range(seqs):
+            sums = jnp.sum(jnp.where(live[s], raised, 0.0), axis=1, keepdims=True)
+            sums = sums + jnp.concatenate([sums[rows // 2 :], sums[: rows // 2]], axis=0)
+            below = jnp.where(live[s], sums, below)
+        out_ref[...] = (raised / below).astype(BF16)
+
+    return pl.pallas_call(
+        body,
+        out_shape=jax.ShapeDtypeStruct((rows, width), BF16),
         in_specs=[vmem()] * (len(parts) + 1),
         out_specs=vmem(),
         compiler_params=SMALL,
-    )(*parts, live)
-
-
-def head_part(weights, latent_cache, w_uv):
-    seqs, capacity, lat_part = latent_cache.shape
+    )(*parts, bounds)
+
+
+def head_part(weights, bounds, cache, w_uv, seqs):
+    packed, lat_part = cache.shape
     heads, _, value_dim = w_uv.shape
     ranks = len(weights)
     group = heads // ranks
-    rows = seqs * group
-    steps = capacity // BLOCK
+    blocks, half = packed // BLOCK, packed // BLOCK // 2
 
     def body(*refs):
         weight_refs = refs[:ranks]
-        cache, w_ref, out_ref, lat_rows = refs[ranks:]
+        bounds_ref, cache_ref, w_ref, out_ref, lat_rows = refs[ranks:]
         rank = lax.axis_index("rank")
-        for s in range(seqs):
-            total = jnp.zeros((ranks * rows, lat_part), F32)
-            for b in range(steps):
-                at = pl.ds(b * BLOCK, BLOCK)
-                block = jnp.concatenate([ref[:, at] for ref in weight_refs], axis=0)
-                total = total + dot(block, cache[s, at, :])
-            lat_rows[s * ranks * rows : (s + 1) * ranks * rows, :] = total
+        total = jnp.zeros((seqs * heads, lat_part), F32)
+        for b in range(blocks):
+            row, source = b // half * group, pl.ds(b % half * BLOCK, BLOCK)
+            block = jnp.concatenate(
+                [ref[:, source].astype(F32)[row : row + group] for ref in weight_refs], axis=0
+            )
+            pos = iota((heads, BLOCK), 1) + b * BLOCK
+            block = jnp.concatenate(
+                [
+                    jnp.where(live_rows(bounds_ref, pos, s), block, 0.0).astype(BF16)
+                    for s in range(seqs)
+                ],
+                axis=0,
+            )
+            total = total + dot(block, cache_ref[pl.ds(b * BLOCK, BLOCK), :])
+        lat_rows[...] = total
         for k in range(ranks):
             for i in range(group):
-                at = pl.ds(k * rows + i, seqs, stride=ranks * rows + group)
-                lat = lat_rows[at, :].astype(BF16)
+                lat = lat_rows[pl.ds(k * group + i, seqs, stride=heads), :].astype(BF16)
                 head = (rank - k + ranks) % ranks * group + i
                 out_ref[:, pl.ds(pl.multiple_of(head * value_dim, value_dim), value_dim)] = dot(
                     lat, w_ref[head]
@@ -185,11 +276,11 @@
     return pl.pallas_call(
         body,
         out_shape=jax.ShapeDtypeStruct((seqs, heads * value_dim), BF16),
-        in_specs=[vmem()] * (ranks + 2),
+        in_specs=[vmem()] * (ranks + 3),
         out_specs=vmem(),
         compiler_params=SMALL,
-        scratch_shapes=[pltpu.VMEM((seqs * ranks * rows, lat_part), F32)],
-    )(*weights, latent_cache, w_uv)
+        scratch_shapes=[pltpu.VMEM((seqs * heads, lat_part), F32)],
+    )(*weights, bounds, cache, w_uv)
 
 
 def project(parts, w_out, copies):
@@ -260,21 +351,40 @@
         axis=1,
     ).reshape(1, plane_rows)
 
-    live = jnp.repeat(lengths, heads // ranks).reshape(-1, 1)
     targets = lax.dynamic_slice_in_dim(slot_of, dp_pos * seqs, seqs).reshape(seqs, 1)
 
-    rows = jnp.concatenate([q_nope, q_rope], axis=1)
+    sizes = [n for n in SIZES if n < seqs * latent_cache.shape[1]] + [seqs * latent_cache.shape[1]]
+    needed = jnp.sum((lengths + BLOCK - 1) // BLOCK) * BLOCK
+    which = sum((needed > n).astype(jnp.int32) for n in sizes[:-1])
+
+    rows = join(q_nope, q_rope)
     near = [rows] + [shifted(rows, "dp", x_groups, k) for k in range(1, NX)]
     near = jnp.concatenate(near, axis=0)
     far = shifted(near, "dp", c_groups, 1)
-    token = fetch(rows, latent_cache, rope_keys, w_uk, live, targets)
-    picked = pick_rows(near, far, slot_here, seqs, token)
+    picked = pick_rows(near, far, slot_here, seqs, (targets, which.reshape(1, 1)))
     arrived = lax.all_to_all(picked, "dp", 0, 0, axis_index_groups=z_groups, tiled=True)
 
-    own, *others = partial_scores(arrived, w_uk, latent_cache, rope_keys, scale)
-    weights = softmax([own] + from_ranks(others), live)
-    gathered = [weights] + from_ranks([weights] * (ranks - 1))
-    value_part = head_part(gathered, latent_cache, w_uv)
+    def attend(packed):
+        def branch(arrived, lengths, w_uk, latent_cache, rope_keys, w_uv):
+            own, *others, bounds, cache = partial_scores(
+                arrived, lengths, w_uk, latent_cache, rope_keys, packed, scale
+            )
+            weights = softmax([own] + from_ranks(others), bounds, seqs)
+            gathered = [weights] + from_ranks([weights] * (ranks - 1))
+            return head_part(gathered, bounds, cache, w_uv, seqs)
+
+        return branch
+
+    value_part = lax.switch(
+        which,
+        [attend(n) for n in sizes],
+        arrived,
+        lengths,
+        w_uk,
+        latent_cache,
+        rope_keys,
+        w_uv,
+    )
     parts = [value_part] + from_ranks([value_part] * (ranks - 1))
     copies = project(parts, w_out, lax.axis_size("dp"))
     everyone = lax.all_to_all(copies, "dp", 0, 0, tiled=True)

time: 90.8 us -> 86 us (0.947)
  blocking collectives: 39.4 us -> 23.5 us
  starting transfers between devices: 17.5 us -> 25.3 us
  local copies, waits for them, and re-layouts: 7.39 us -> 2.26 us
  Pallas kernels: 5.16 us -> 9.48 us
  other arithmetic: 0.26 us -> 2.24 us
  waiting for transfers between devices: 20.6 us -> 21.8 us
    all_to_all x1 -> x0, blocking collectives: 17.4 us -> none  [per_device(): lax.all_to_all(picked, 'dp', 0, 0, axis_index_groups=z_groups, tiled=True)]
    all_to_all x0 -> x1, waiting for transfers between devices: none -> 9.46 us  [per_device(): lax.all_to_all(picked, 'dp', 0, 0, axis_index_groups=z_groups, tiled=True)]
    ppermute x13, waiting for transfers between devices: 20.6 us -> 12.4 us  [shifted(): return lax.ppermute(array, axis, pairs)]
    all_to_all x0 -> x1, starting transfers between devices: none -> 8.19 us  [per_device(): lax.all_to_all(picked, 'dp', 0, 0, axis_index_groups=z_groups, tiled=True)]
    pallas_call x3, Pallas kernels: 2.59 us -> 6.4 us  [the longest x1 5.7 us: partial_scores(): pl.pallas_call(body, out_shape=[jax.ShapeDtypeStruct((2 * group, packed /...]
    unnamed x19 -> x6, local copies, waits for them, and re-layouts: 5.03 us -> 1.42 us
    all_to_all x1, blocking collectives: 22 us -> 23.5 us  [per_device(): everyone = lax.all_to_all(copies, 'dp', 0, 0, tiled=True)]
    reduce_sum x0 -> x1, other arithmetic: none -> 1.3 us  [per_device(): needed = jnp.sum((lengths + BLOCK - 1) // BLOCK) * BLOCK]
  transfers between devices with their start and end apart: 13 -> 14, of which waited for: 9 -> 13; matrix products, arithmetic and copies ran while one was open for 2% -> 4% of each run, Pallas kernels for 0% -> 0%
where the time goes in v3:
time: 86 us; the launch traced here: 85.8 us
  starting transfers between devices  25.3 us (29%)
  blocking collectives  23.5 us (27%)
  waiting for transfers between devices  21.8 us (25%)
  Pallas kernels  9.48 us (11%)
  local copies, waits for them, and re-layouts  2.26 us (3%)
  other arithmetic  2.24 us (3%)
    all_to_all x1, blocking collectives, per_device(): everyone = lax.all_to_all(copies, 'dp', 0, 0, tiled=True)  23.5 us
    ppermute x13, starting transfers between devices, shifted(): return lax.ppermute(array, axis, pairs)  17.1 us
    ppermute x13, waiting for transfers between devices, shifted(): return lax.ppermute(array, axis, pairs)  12.4 us
    all_to_all x1, waiting for transfers between devices, per_device(): lax.all_to_all(picked, 'dp', 0, 0, axis_index_groups=z_groups, tiled=True)  9.46 us
    all_to_all x1, starting transfers between devices, per_device(): lax.all_to_all(picked, 'dp', 0, 0, axis_index_groups=z_groups, tiled=True)  8.19 us
    pallas_call x1, Pallas kernels, partial_scores(): pl.pallas_call(body, out_shape=[jax.ShapeDtypeStruct((2 * group, packed /...  5.7 us
  transfers between devices with their start and end apart: 14, of which 13 were waited for; matrix products, arithmetic and copies ran while one was open for 4% of the time, Pallas kernels for 0%

profile of v3, /device:TPU:1, one launch (start us, length us, event | category | flops | bytes accessed | tf_op | source)
XLA Modules:
  0.0 85.8 jit_solution(8154374523554043463)
XLA Ops:
  0.0 0.0 copy-start.1
  0.0 0.7 copy-done.1
  0.7 0.0 copy-start.2
  0.7 0.7 copy-done.2
  1.5 3.4 %collective-permute-start.26 = (bf16[4,3072]{1,0:T(4,128)(2,1)S(1)}, bf16[4,3072]{1,0:T(4,128)(2,1)S(1)}, u32[]{:S(2)}, u32[]{:S(2)}) collective-permute-start(bf16[4,3072]{1,0:T(4,128)(2,1)S(1)} %shard_map.91), channel_id=1, source_target_pairs={{0,24},{8,0},{16,8},{24,16},{4,28},{12,4},{20,12},{28,20},{32,56},... | collective-permute-start | bytes 73736 | tf_op jit(solution)/shard_map/ppermute | solution.py:22
  4.8 0.5 collective-permute-start.25
  5.3 0.6 collective-permute-start.24
  6.0 1.3 %fusion.10 = s32[]{:T(128)} fusion(s32[4]{0:T(128)} %param.17), kind=kLoop, calls=%fused_computation.35 | loop fusion | flops 67 | bytes 20 | tf_op jit(solution)/shard_map/reduce_sum | solution.py:357
  7.3 0.8 dynamic-slice_bitcast_fusion
  8.7 0.1 copy.12.rest_0_.target_ref
  8.8 0.0 collective-permute-done.26
  8.8 0.2 collective-permute-done.25
  9.0 0.3 collective-permute-done.24
  9.3 0.1 pad_maximum_fusion.near_ref
  9.3 2.4 %collective-permute-start.27 = (bf16[16,3072]{1,0:T(8,128)(2,1)S(1)}, bf16[16,3072]{1,0:T(8,128)(2,1)S(1)}, u32[]{:S(2)}, u32[]{:S(2)}) collective-permute-start(bf16[16,3072]{1,0:T(8,128)(2,1)S(1)} %pad_maximum_fusion.near_ref), channel_id=1, source_target_pairs={{0,4},{4,0},{8,12},{12,8},{16,20},{20,16},{24,28},{28,24},{32,36},... | collective-permute-start | bytes 294920 | tf_op jit(solution)/shard_map/ppermute | solution.py:22
  11.8 0.9 select_reduce_fusion
  12.6 0.1 collective-permute-done.27.far_ref
  12.7 1.0 %shard_map.92 = bf16[8,4,3072]{2,1,0:T(4,128)(2,1)} custom-call(bf16[16,3072]{1,0:T(8,128)(2,1)S(1)} %pad_maximum_fusion.near_ref, bf16[16,3072]{1,0:T(8,128)(2,1)S(1)} %collective-permute-done.27.far_ref, s32[1,32]{1,0:T(1,128)S(1)} %bitcast.4, s32[4,1]{1,0:T(4,128)S(1)} %copy.12.rest_0_.target_ref, s32[1,1]{1,0:T(1,128)} %bitcast.2.rest_1_), custom_call_target="tpu_custom_call" | custom-call | tf_op jit(solution)/shard_map/pallas_call | solution.py:98
  13.7 8.2 %all-to-all-start = ((bf16[8,4,3072]{2,1,0:T(4,128)(2,1)}), bf16[8,4,3072]{2,1,0:T(4,128)(2,1)S(1)}, u32[]{:S(2)}, u32[]{:S(2)}) async-start(bf16[8,4,3072]{2,1,0:T(4,128)(2,1)} %shard_map.92), calls=%async_computation | async-start | bytes 393216 | tf_op jit(solution)/shard_map/all_to_all | solution.py:365
  21.9 9.5 %all-to-all-done = bf16[8,4,3072]{2,1,0:T(4,128)(2,1)S(1)} async-done(((bf16[8,4,3072]{2,1,0:T(4,128)(2,1)}), bf16[8,4,3072]{2,1,0:T(4,128)(2,1)S(1)}, u32[]{:S(2)}, u32[]{:S(2)}) %all-to-all-start) | async-done | bytes 196640 | tf_op jit(solution)/shard_map/all_to_all | solution.py:365
  31.4 0.0 copy-start
  31.4 24.5 %conditional.1 = (bf16[4,2048]{1,0:T(4,128)(2,1)S(1)}) conditional(s32[]{:T(128)} %clamp.3, (bf16[8,4,3072]{2,1,0:T(4,128)(2,1)S(1)}, s32[4]{0:T(128)}, bf16[16,128,128]{2,1,0:T(8,128)(2,1)}, bf16[4,4096,128]{2,1,0:T(8,128)(2,1)}, bf16[4,16,4096]{2,1,0:T(8,128)(2,1)}, ...), branch_computations={%region_2.3_spmd, %region_3.4_spmd, %region_4.5_spmd, %region_5.6_... | conditional | bytes 6816020 | solution.py:378
  31.4 5.7 %branch_0_fun.3 = (f32[8,4608]{1,0:T(8,128)S(1)}, f32[8,4608]{1,0:T(8,128)S(1)}, f32[8,4608]{1,0:T(8,128)S(1)}, f32[8,4608]{1,0:T(8,128)S(1)}, s32[16,128]{1,0:T(8,128)S(1)}, /*index=5*/bf16[9216,128]{1,0:T(8,128)(2,1)S(1)}) custom-call(bf16[8,4,3072]{2,1,0:T(4,128)(2,1)S(1)} %get-tuple-element.56.arrived_ref, s32[4]{0:T(128)} %get-tuple-element.58.len_ref, ...), custom_call_target="tpu_custom_call" | custom-call | tf_op jit(solution)/shard_map/cond/branch_0_fun/pallas_call | solution.py:188
  37.1 1.4 %collective-permute-start = (f32[8,4608]{1,0:T(8,128)S(1)}, f32[8,4608]{1,0:T(8,128)S(1)}, u32[]{:S(2)}, u32[]{:S(2)}) collective-permute-start(f32[8,4608]{1,0:T(8,128)S(1)} %get-tuple-element.64), channel_id=1, source_target_pairs={{0,1},{1,2},{2,3},{3,0},{4,5},{5,6},{6,7},{7,4},{8,9},{9,10},{10,1... | collective-permute-start | bytes 442376 | tf_op jit(solution)/shard_map/cond/branch_0_fun/ppermute | solution.py:22
  38.4 2.6 %collective-permute-start.1 = (f32[8,4608]{1,0:T(8,128)S(1)}, f32[8,4608]{1,0:T(8,128)S(1)}, u32[]{:S(2)}, u32[]{:S(2)}) collective-permute-start(f32[8,4608]{1,0:T(8,128)S(1)} %get-tuple-element.65), channel_id=1, source_target_pairs={{0,2},{1,3},{2,0},{3,1},{4,6},{5,7},{6,4},{7,5},{8,10},{9,11},{10,... | collective-permute-start | bytes 442376 | tf_op jit(solution)/shard_map/cond/branch_0_fun/ppermute | solution.py:22
  41.1 1.1 %collective-permute-start.2 = (f32[8,4608]{1,0:T(8,128)S(1)}, f32[8,4608]{1,0:T(8,128)S(1)}, u32[]{:S(2)}, u32[]{:S(2)}) collective-permute-start(f32[8,4608]{1,0:T(8,128)S(1)} %get-tuple-element.66), channel_id=1, source_target_pairs={{0,3},{1,0},{2,1},{3,2},{4,7},{5,4},{6,5},{7,6},{8,11},{9,8},{10,9... | collective-permute-start | bytes 442376 | tf_op jit(solution)/shard_map/cond/branch_0_fun/ppermute | solution.py:22
  42.1 0.3 collective-permute-done.refs_1_
  42.4 3.5 %collective-permute-done.1.refs_2_ = f32[8,4608]{1,0:T(8,128)S(1)} collective-permute-done((f32[8,4608]{1,0:T(8,128)S(1)}, f32[8,4608]{1,0:T(8,128)S(1)}, u32[]{:S(2)}, u32[]{:S(2)}) %collective-permute-start.1) | collective-permute-done | bytes 147488 | tf_op jit(solution)/shard_map/cond/branch_0_fun/ppermute | solution.py:22
  45.9 0.5 collective-permute-done.2.refs_3_
  46.4 0.7 branch_0_fun.4.refs_0_
  47.0 2.2 %collective-permute-start.5 = (bf16[8,4608]{1,0:T(8,128)(2,1)S(1)}, bf16[8,4608]{1,0:T(8,128)(2,1)S(1)}, u32[]{:S(2)}, u32[]{:S(2)}) collective-permute-start(bf16[8,4608]{1,0:T(8,128)(2,1)S(1)} %branch_0_fun.4.refs_0_), channel_id=1, source_target_pairs={{0,3},{1,0},{2,1},{3,2},{4,7},{5,4},{6,5},{7,6},{8,11},{9,8},{10,9... | collective-permute-start | bytes 221192 | tf_op jit(solution)/shard_map/cond/branch_0_fun/ppermute | solution.py:22
  49.3 0.1 collective-permute-start.4
  49.4 0.7 collective-permute-start.3
  50.1 0.6 collective-permute-done.5.refs_3_
  50.7 3.4 %collective-permute-done.4.refs_2_ = bf16[8,4608]{1,0:T(8,128)(2,1)S(1)} collective-permute-done((bf16[8,4608]{1,0:T(8,128)(2,1)S(1)}, bf16[8,4608]{1,0:T(8,128)(2,1)S(1)}, u32[]{:S(2)}, u32[]{:S(2)}) %collective-permute-start.4) | collective-permute-done | bytes 73760 | tf_op jit(solution)/shard_map/cond/branch_0_fun/ppermute | solution.py:22
  54.1 0.5 collective-permute-done.3.refs_1_
  54.6 0.0 copy-done.3
  54.6 0.8 branch_0_fun.5
  55.9 0.5 collective-permute-start.30
  56.4 0.8 collective-permute-start.29
  57.2 0.8 collective-permute-start.28
  58.0 0.6 collective-permute-done.30.refs_3_
  58.6 1.9 %collective-permute-done.29.refs_2_ = bf16[4,2048]{1,0:T(4,128)(2,1)S(1)} collective-permute-done((bf16[4,2048]{1,0:T(4,128)(2,1)S(1)}, bf16[4,2048]{1,0:T(4,128)(2,1)S(1)}, u32[]{:S(2)}, u32[]{:S(2)}) %collective-permute-start.29) | collective-permute-done | bytes 16416 | tf_op jit(solution)/shard_map/ppermute | solution.py:22
  60.5 0.5 collective-permute-done.28.refs_1_
  61.0 0.0 copy-done
  61.0 0.4 shard_map.93
  61.4 23.5 %all_to_all.10.all_ref = bf16[64,4,512]{2,1,0:T(4,128)(2,1)S(1)} all-to-all(bf16[64,4,512]{2,1,0:T(4,128)(2,1)S(1)} %shard_map.93), channel_id=1, replica_groups=mesh['dp'=64,'rank'=4] {'dp'}, dimensions={0} | all-to-all | bytes 524288 | tf_op jit(solution)/shard_map/all_to_all | solution.py:390
  84.9 0.9 %shard_map.94 = bf16[4,512]{1,0:T(4,128)(2,1)} custom-call(bf16[64,4,512]{2,1,0:T(4,128)(2,1)S(1)} %all_to_all.10.all_ref, s32[4,1]{1,0:T(4,128)S(1)} %copy.12.rest_0_.target_ref), custom_call_target="tpu_custom_call" | custom-call | tf_op jit(solution)/shard_map/pallas_call | solution.py:324
  (3 shorter events, 0.0 us)
Async XLA Ops:
  0.0 0.7 copy-start.1
  0.7 0.7 copy-start.2
  1.5 7.3 %collective-permute-start.26 = (bf16[4,3072]{1,0:T(4,128)(2,1)S(1)}, bf16[4,3072]{1,0:T(4,128)(2,1)S(1)}, u32[]{:S(2)}, u32[]{:S(2)}) collective-permute-start(bf16[4,3072]{1,0:T(4,128)(2,1)S(1)} %shard_map.91), channel_id=1, source_target_pairs={{0,24},{8,0},{16,8},{24,16},{4,28},{12,4},{20,12},{28,20},{32,56},... | collective-permute-start | bytes 73736 | tf_op jit(solution)/shard_map/ppermute | solution.py:22
  4.8 4.2 %collective-permute-start.25 = (bf16[4,3072]{1,0:T(4,128)(2,1)S(1)}, bf16[4,3072]{1,0:T(4,128)(2,1)S(1)}, u32[]{:S(2)}, u32[]{:S(2)}) collective-permute-start(bf16[4,3072]{1,0:T(4,128)(2,1)S(1)} %shard_map.91), channel_id=1, source_target_pairs={{0,16},{8,24},{16,0},{24,8},{4,20},{12,28},{20,4},{28,12},{32,48},... | collective-permute-start | bytes 73736 | tf_op jit(solution)/shard_map/ppermute | solution.py:22
  5.3 3.9 %collective-permute-start.24 = (bf16[4,3072]{1,0:T(4,128)(2,1)S(1)}, bf16[4,3072]{1,0:T(4,128)(2,1)S(1)}, u32[]{:S(2)}, u32[]{:S(2)}) collective-permute-start(bf16[4,3072]{1,0:T(4,128)(2,1)S(1)} %shard_map.91), channel_id=1, source_target_pairs={{0,8},{8,16},{16,24},{24,0},{4,12},{12,20},{20,28},{28,4},{32,40},... | collective-permute-start | bytes 73736 | tf_op jit(solution)/shard_map/ppermute | solution.py:22
  9.3 3.4 %collective-permute-start.27 = (bf16[16,3072]{1,0:T(8,128)(2,1)S(1)}, bf16[16,3072]{1,0:T(8,128)(2,1)S(1)}, u32[]{:S(2)}, u32[]{:S(2)}) collective-permute-start(bf16[16,3072]{1,0:T(8,128)(2,1)S(1)} %pad_maximum_fusion.near_ref), channel_id=1, source_target_pairs={{0,4},{4,0},{8,12},{12,8},{16,20},{20,16},{24,28},{28,24},{32,36},... | collective-permute-start | bytes 294920 | tf_op jit(solution)/shard_map/ppermute | solution.py:22
  13.7 17.7 %all-to-all-start = ((bf16[8,4,3072]{2,1,0:T(4,128)(2,1)}), bf16[8,4,3072]{2,1,0:T(4,128)(2,1)S(1)}, u32[]{:S(2)}, u32[]{:S(2)}) async-start(bf16[8,4,3072]{2,1,0:T(4,128)(2,1)} %shard_map.92), calls=%async_computation | async-start | bytes 393216 | tf_op jit(solution)/shard_map/all_to_all | solution.py:365
  31.4 29.7 %copy-start = (bf16[2048,512]{1,0:T(8,128)(2,1)S(1)}, bf16[2048,512]{1,0:T(8,128)(2,1)}, u32[]{:S(2)}) copy-start(bf16[2048,512]{1,0:T(8,128)(2,1)} %refs_4_.1) | copy-start | bytes 6291460
  31.4 23.2 %copy-start.3 = (bf16[16,128,128]{2,1,0:T(8,128)(2,1)S(1)}, bf16[16,128,128]{2,1,0:T(8,128)(2,1)}, u32[]{:S(2)}) copy-start(bf16[16,128,128]{2,1,0:T(8,128)(2,1)} %get-tuple-element.69.refs_6_) | copy-start | bytes 1572868 | tf_op jit(solution)/shard_map/cond
  37.1 5.3 %collective-permute-start = (f32[8,4608]{1,0:T(8,128)S(1)}, f32[8,4608]{1,0:T(8,128)S(1)}, u32[]{:S(2)}, u32[]{:S(2)}) collective-permute-start(f32[8,4608]{1,0:T(8,128)S(1)} %get-tuple-element.64), channel_id=1, source_target_pairs={{0,1},{1,2},{2,3},{3,0},{4,5},{5,6},{6,7},{7,4},{8,9},{9,10},{10,1... | collective-permute-start | bytes 442376 | tf_op jit(solution)/shard_map/cond/branch_0_fun/ppermute | solution.py:22
  38.4 7.5 %collective-permute-start.1 = (f32[8,4608]{1,0:T(8,128)S(1)}, f32[8,4608]{1,0:T(8,128)S(1)}, u32[]{:S(2)}, u32[]{:S(2)}) collective-permute-start(f32[8,4608]{1,0:T(8,128)S(1)} %get-tuple-element.65), channel_id=1, source_target_pairs={{0,2},{1,3},{2,0},{3,1},{4,6},{5,7},{6,4},{7,5},{8,10},{9,11},{10,... | collective-permute-start | bytes 442376 | tf_op jit(solution)/shard_map/cond/branch_0_fun/ppermute | solution.py:22
  41.1 5.3 %collective-permute-start.2 = (f32[8,4608]{1,0:T(8,128)S(1)}, f32[8,4608]{1,0:T(8,128)S(1)}, u32[]{:S(2)}, u32[]{:S(2)}) collective-permute-start(f32[8,4608]{1,0:T(8,128)S(1)} %get-tuple-element.66), channel_id=1, source_target_pairs={{0,3},{1,0},{2,1},{3,2},{4,7},{5,4},{6,5},{7,6},{8,11},{9,8},{10,9... | collective-permute-start | bytes 442376 | tf_op jit(solution)/shard_map/cond/branch_0_fun/ppermute | solution.py:22
  47.0 3.7 %collective-permute-start.5 = (bf16[8,4608]{1,0:T(8,128)(2,1)S(1)}, bf16[8,4608]{1,0:T(8,128)(2,1)S(1)}, u32[]{:S(2)}, u32[]{:S(2)}) collective-permute-start(bf16[8,4608]{1,0:T(8,128)(2,1)S(1)} %branch_0_fun.4.refs_0_), channel_id=1, source_target_pairs={{0,3},{1,0},{2,1},{3,2},{4,7},{5,4},{6,5},{7,6},{8,11},{9,8},{10,9... | collective-permute-start | bytes 221192 | tf_op jit(solution)/shard_map/cond/branch_0_fun/ppermute | solution.py:22
  49.3 4.8 %collective-permute-start.4 = (bf16[8,4608]{1,0:T(8,128)(2,1)S(1)}, bf16[8,4608]{1,0:T(8,128)(2,1)S(1)}, u32[]{:S(2)}, u32[]{:S(2)}) collective-permute-start(bf16[8,4608]{1,0:T(8,128)(2,1)S(1)} %branch_0_fun.4.refs_0_), channel_id=1, source_target_pairs={{0,2},{1,3},{2,0},{3,1},{4,6},{5,7},{6,4},{7,5},{8,10},{9,11},{10,... | collective-permute-start | bytes 221192 | tf_op jit(solution)/shard_map/cond/branch_0_fun/ppermute | solution.py:22
  49.4 5.2 %collective-permute-start.3 = (bf16[8,4608]{1,0:T(8,128)(2,1)S(1)}, bf16[8,4608]{1,0:T(8,128)(2,1)S(1)}, u32[]{:S(2)}, u32[]{:S(2)}) collective-permute-start(bf16[8,4608]{1,0:T(8,128)(2,1)S(1)} %branch_0_fun.4.refs_0_), channel_id=1, source_target_pairs={{0,1},{1,2},{2,3},{3,0},{4,5},{5,6},{6,7},{7,4},{8,9},{9,10},{10,1... | collective-permute-start | bytes 221192 | tf_op jit(solution)/shard_map/cond/branch_0_fun/ppermute | solution.py:22
  55.9 2.7 %collective-permute-start.30 = (bf16[4,2048]{1,0:T(4,128)(2,1)S(1)}, bf16[4,2048]{1,0:T(4,128)(2,1)S(1)}, u32[]{:S(2)}, u32[]{:S(2)}) collective-permute-start(bf16[4,2048]{1,0:T(4,128)(2,1)S(1)} %get-tuple-element.106.refs_0_), channel_id=1, source_target_pairs={{0,3},{1,0},{2,1},{3,2},{4,7},{5,4},{6,5},{7,6},{8,11},{9,8},{10,9... | collective-permute-start | bytes 49160 | tf_op jit(solution)/shard_map/ppermute | solution.py:22
  56.4 4.1 %collective-permute-start.29 = (bf16[4,2048]{1,0:T(4,128)(2,1)S(1)}, bf16[4,2048]{1,0:T(4,128)(2,1)S(1)}, u32[]{:S(2)}, u32[]{:S(2)}) collective-permute-start(bf16[4,2048]{1,0:T(4,128)(2,1)S(1)} %get-tuple-element.106.refs_0_), channel_id=1, source_target_pairs={{0,2},{1,3},{2,0},{3,1},{4,6},{5,7},{6,4},{7,5},{8,10},{9,11},{10,... | collective-permute-start | bytes 49160 | tf_op jit(solution)/shard_map/ppermute | solution.py:22
  57.2 3.8 %collective-permute-start.28 = (bf16[4,2048]{1,0:T(4,128)(2,1)S(1)}, bf16[4,2048]{1,0:T(4,128)(2,1)S(1)}, u32[]{:S(2)}, u32[]{:S(2)}) collective-permute-start(bf16[4,2048]{1,0:T(4,128)(2,1)S(1)} %get-tuple-element.106.refs_0_), channel_id=1, source_target_pairs={{0,1},{1,2},{2,3},{3,0},{4,5},{5,6},{6,7},{7,4},{8,9},{9,10},{10,1... | collective-permute-start | bytes 49160 | tf_op jit(solution)/shard_map/ppermute | solution.py:22

commit v4 on v3

--- a/solution.py
+++ b/solution.py
@@ -31,10 +31,11 @@
 
 F32, BF16 = jnp.float32, jnp.bfloat16
 BLOCK = 512
+CHUNK = 4
 SIZES = (9216, 10240, 12288)
 SMALL = pltpu.CompilerParams(vmem_limit_bytes=8 << 20)
-SCORES = pltpu.CompilerParams(vmem_limit_bytes=8 << 20)
-LARGE = pltpu.CompilerParams(vmem_limit_bytes=40 << 20)
+LARGE = pltpu.CompilerParams(vmem_limit_bytes=60 << 20)
+HALF = pltpu.CompilerParams(vmem_limit_bytes=40 << 20)
 
 
 def vmem():
@@ -77,15 +78,14 @@
         in_specs=[hbm()] * 2,
         out_specs=vmem(),
         scratch_shapes=[pltpu.SemaphoreType.DMA((2,))],
-        compiler_params=LARGE,
+        compiler_params=HALF,
     )(q_nope, q_rope)
 
 
-def pick_rows(near, far, slot_here, seqs, ready):
+def pick_rows(near, far, slot_here, seqs):
     rows, width = near.shape
 
-    def body(near_ref, far_ref, slot_ref, *rest):
-        out_ref = rest[-1]
+    def body(near_ref, far_ref, slot_ref, out_ref):
         dp = lax.axis_index("dp")
         i = iota((NZ * seqs, 2 * rows), 0)
         wanted = (i // seqs * (NX * NC) + dp % (NX * NC)) * seqs + i % seqs
@@ -98,35 +98,24 @@
     return pl.pallas_call(
         body,
         out_shape=jax.ShapeDtypeStruct((NZ, seqs, width), BF16),
-        in_specs=[vmem()] * (3 + len(ready)),
-        out_specs=vmem(),
-        compiler_params=SMALL,
-    )(near, far, slot_here, *ready)
-
-
-def live_rows(bounds_ref, pos, slot):
-    return (pos >= bounds_ref[slot : slot + 1, :1]) & (pos < bounds_ref[8 + slot : 9 + slot, :1])
-
-
-def partial_scores(arrived, lengths, w_uk, latent_cache, rope_keys, packed, scale):
+        in_specs=[vmem()] * 3,
+        out_specs=vmem(),
+        compiler_params=SMALL,
+    )(near, far, slot_here)
+
+
+def pack_live(lengths, latent_cache, rope_keys, ready):
     seqs, capacity, lat_part = latent_cache.shape
-    heads, nope_dim, _ = w_uk.shape
     rope_part = rope_keys.shape[1]
-    nope_width = heads * nope_dim
-    rope_dim = arrived.shape[2] // heads - nope_dim
-    ranks = lax.axis_size("rank")
-    group = heads // ranks
-    blocks, half = packed // BLOCK, packed // BLOCK // 2
-
-    def body(arrived_ref, len_ref, w_ref, cache_ref, keys_ref, *rest):
-        outs, rest = rest[:ranks], rest[ranks:]
-        bounds_ref, cache, keys, lat_rows, lat_slots, rope_slots, sems, key_sems = rest
-        rank = lax.axis_index("rank")
-        counts = [(len_ref[s] + BLOCK - 1) // BLOCK for s in range(seqs)]
+    packed = seqs * capacity
+    blocks = packed // BLOCK
+
+    def body(len_ref, cache_ref, keys_ref, *rest):
+        cache, keys, bounds_ref, sems = rest[-4:]
         starts = [jnp.int32(0)]
         for s in range(seqs):
-            starts.append(starts[-1] + counts[s])
-        slots, copies = [], []
+            starts.append(starts[-1] + (len_ref[s] + BLOCK - 1) // BLOCK)
+        copies = []
         for b in range(blocks):
             slot = jnp.int32(0)
             start = jnp.int32(0)
@@ -136,21 +125,43 @@
             block = jnp.minimum(b - start, capacity // BLOCK - 1)
             source = pl.ds(pl.multiple_of(block * BLOCK, BLOCK), BLOCK)
             at = pl.ds(b * BLOCK, BLOCK)
-            copies.append(
-                (
-                    pltpu.make_async_copy(cache_ref.at[slot, source], cache.at[at], sems.at[b]),
-                    pltpu.make_async_copy(
-                        keys_ref.at[slot, :, source], keys.at[:, at], key_sems.at[b]
-                    ),
-                )
-            )
-            for copy in copies[-1]:
-                copy.start()
-            slots.append(slot)
+            copies += [
+                pltpu.make_async_copy(cache_ref.at[slot, source], cache.at[at], sems.at[0, b]),
+                pltpu.make_async_copy(keys_ref.at[slot, :, source], keys.at[:, at], sems.at[1, b]),
+            ]
+            copies[-2].start()
+            copies[-1].start()
         for s in range(seqs):
             first = starts[s] * BLOCK
             bounds_ref[s : s + 1, :] = jnp.full((1, 128), first, jnp.int32)
             bounds_ref[8 + s : 9 + s, :] = jnp.full((1, 128), first + len_ref[s], jnp.int32)
+        for copy in copies:
+            copy.wait()
+
+    return pl.pallas_call(
+        body,
+        out_shape=[
+            jax.ShapeDtypeStruct((packed, lat_part), BF16),
+            jax.ShapeDtypeStruct((rope_part, packed), BF16),
+            jax.ShapeDtypeStruct((16, 128), jnp.int32),
+        ],
+        in_specs=[smem(), hbm(), hbm()] + [hbm()] * len(ready),
+        out_specs=[vmem()] * 3,
+        compiler_params=LARGE,
+        scratch_shapes=[pltpu.SemaphoreType.DMA((2, blocks))],
+    )(lengths, latent_cache, rope_keys, *ready)
+
+
+def absorb(arrived, w_uk, rope_part):
+    _, seqs, width = arrived.shape
+    heads, nope_dim, lat_part = w_uk.shape
+    nope_width = heads * nope_dim
+    rope_dim = width // heads - nope_dim
+    ranks = lax.axis_size("rank")
+    group = heads // ranks
+
+    def body(arrived_ref, w_ref, lat_ref, rope_ref, lat_rows):
+        rank = lax.axis_index("rank")
         query = arrived_ref[0].astype(F32)
         for z in range(1, NZ):
             query = query + arrived_ref[z].astype(F32)
@@ -167,20 +178,63 @@
         own_head = (t // group + rank) % ranks * group + t % group
         mine = own_head == iota((heads, rope_width), 1) // rope_dim
         for s in range(seqs):
-            lat_slots[s] = lat_rows[pl.ds(s, heads, stride=seqs), :].astype(BF16)
+            rows = slice(s * heads, (s + 1) * heads)
+            lat_ref[rows, :] = lat_rows[pl.ds(s, heads, stride=seqs), :].astype(BF16)
             flat = jnp.broadcast_to(query[s : s + 1, nope_width:], (heads, rope_width))
-            rope_slots[s] = dot(jnp.where(mine, flat, 0.0).astype(BF16), fold).astype(BF16)
+            rope_ref[rows, :] = dot(jnp.where(mine, flat, 0.0).astype(BF16), fold).astype(BF16)
+
+    return pl.pallas_call(
+        body,
+        out_shape=[
+            jax.ShapeDtypeStruct((seqs * heads, lat_part), BF16),
+            jax.ShapeDtypeStruct((seqs * heads, 128), BF16),
+        ],
+        in_specs=[vmem()] * 2,
+        out_specs=[vmem()] * 2,
+        compiler_params=SMALL,
+        scratch_shapes=[pltpu.VMEM((heads * seqs, lat_part), F32)],
+    )(arrived, w_uk)
+
+
+def live_rows(bounds_ref, pos, slot):
+    return (pos >= bounds_ref[slot : slot + 1, :1]) & (pos < bounds_ref[8 + slot : 9 + slot, :1])
+
+
+def partial_scores(query_lat, query_rope, bounds, cache, keys, packed, seqs, scale):
+    heads, lat_part = query_lat.shape[0] // seqs, query_lat.shape[1]
+    rope_part = keys.shape[0]
+    ranks = lax.axis_size("rank")
+    group = heads // ranks
+    blocks, half = packed // BLOCK, packed // BLOCK // 2
+    chunks = [(b, min(b + CHUNK, blocks)) for b in range(0, blocks, CHUNK)]
+
+    def body(lat_ref, rope_ref, bounds_ref, cache_hbm, keys_hbm, *rest):
+        outs, (cache_ref, keys_ref, sems) = rest[:ranks], rest[ranks:]
+        copies = []
+        for i, (first, end) in enumerate(chunks):
+            at = pl.ds(first * BLOCK, (end - first) * BLOCK)
+            copies += [
+                pltpu.make_async_copy(cache_hbm.at[at], cache_ref.at[at], sems.at[0, i]),
+                pltpu.make_async_copy(keys_hbm.at[:, at], keys_ref.at[:, at], sems.at[1, i]),
+            ]
+            copies[-2].start()
+            copies[-1].start()
+        lat, rope = lat_ref[...], rope_ref[:, :rope_part]
         for b in range(blocks):
-            for copy in copies[b]:
-                copy.wait()
+            if b % CHUNK == 0:
+                copies[b // CHUNK * 2].wait()
+                copies[b // CHUNK * 2 + 1].wait()
             at = pl.ds(b * BLOCK, BLOCK)
-            part = lax.dot_general(
-                lat_slots[slots[b]],
-                cache[at, :],
-                (((1,), (1,)), ((), ())),
-                preferred_element_type=F32,
+            every = lax.dot_general(
+                lat, cache_ref[at, :], (((1,), (1,)), ((), ())), preferred_element_type=F32
             )
-            part = (part + dot(rope_slots[slots[b]][:, :rope_part], keys[:, at])) * scale
+            every = every + dot(rope, keys_ref[:, at])
+            pos = iota((heads, BLOCK), 1) + b * BLOCK
+            part = every[:heads]
+            for s in range(1, seqs):
+                rows = every[s * heads : (s + 1) * heads]
+                part = jnp.where(pos >= bounds_ref[s : s + 1, :1], rows, part)
+            part = part * scale
             row, to = b // half * group, pl.ds(b % half * BLOCK, BLOCK)
             for k in range(ranks):
                 outs[k][row : row + group, to] = part[k * group : (k + 1) * group]
@@ -188,22 +242,15 @@
     return pl.pallas_call(
         body,
         out_shape=[jax.ShapeDtypeStruct((2 * group, packed // 2), F32)] * ranks
-        + [
-            jax.ShapeDtypeStruct((16, 128), jnp.int32),
-            jax.ShapeDtypeStruct((packed, lat_part), BF16),
-        ],
-        in_specs=[vmem(), smem(), vmem(), hbm(), hbm()],
-        out_specs=[vmem()] * (ranks + 2),
-        compiler_params=SCORES,
+        + [jax.ShapeDtypeStruct((packed, lat_part), BF16)],
+        in_specs=[vmem()] * 3 + [hbm()] * 2,
+        out_specs=[vmem()] * (ranks + 1),
+        compiler_params=SMALL,
         scratch_shapes=[
             pltpu.VMEM((rope_part, packed), BF16),
-            pltpu.VMEM((heads * seqs, lat_part), F32),
-            pltpu.VMEM((seqs, heads, lat_part), BF16),
-            pltpu.VMEM((seqs, heads, 128), BF16),
-            pltpu.SemaphoreType.DMA((blocks,)),
-            pltpu.SemaphoreType.DMA((blocks,)),
+            pltpu.SemaphoreType.DMA((2, len(chunks))),
         ],
-    )(arrived, lengths, w_uk, latent_cache, rope_keys)
+    )(query_lat, query_rope, bounds, cache, keys)
 
 
 def softmax(parts, bounds, seqs):
@@ -238,9 +285,8 @@
     )(*parts, bounds)
 
 
-def head_part(weights, bounds, cache, w_uv, seqs):
-    packed, lat_part = cache.shape
-    heads, _, value_dim = w_uv.shape
+def head_part(weights, bounds, cache, w_uv, packed, seqs):
+    heads, lat_part, value_dim = w_uv.shape
     ranks = len(weights)
     group = heads // ranks
     blocks, half = packed // BLOCK, packed // BLOCK // 2
@@ -361,29 +407,27 @@
     near = [rows] + [shifted(rows, "dp", x_groups, k) for k in range(1, NX)]
     near = jnp.concatenate(near, axis=0)
     far = shifted(near, "dp", c_groups, 1)
-    picked = pick_rows(near, far, slot_here, seqs, (targets, which.reshape(1, 1)))
+    picked = pick_rows(near, far, slot_here, seqs)
+    cache, keys, bounds = pack_live(
+        lengths, latent_cache, rope_keys, (picked, targets, which.reshape(1, 1))
+    )
     arrived = lax.all_to_all(picked, "dp", 0, 0, axis_index_groups=z_groups, tiled=True)
 
+    query_lat, query_rope = absorb(arrived, w_uk, rope_keys.shape[1])
+
     def attend(packed):
-        def branch(arrived, lengths, w_uk, latent_cache, rope_keys, w_uv):
-            own, *others, bounds, cache = partial_scores(
-                arrived, lengths, w_uk, latent_cache, rope_keys, packed, scale
+        def branch(query_lat, query_rope, bounds, cache, keys, w_uv):
+            own, *others, held = partial_scores(
+                query_lat, query_rope, bounds, cache, keys, packed, seqs, scale
             )
             weights = softmax([own] + from_ranks(others), bounds, seqs)
             gathered = [weights] + from_ranks([weights] * (ranks - 1))
-            return head_part(gathered, bounds, cache, w_uv, seqs)
+            return head_part(gathered, bounds, held, w_uv, packed, seqs)
 
         return branch
 
     value_part = lax.switch(
-        which,
-        [attend(n) for n in sizes],
-        arrived,
-        lengths,
-        w_uk,
-        latent_cache,
-        rope_keys,
-        w_uv,
+        which, [attend(n) for n in sizes], query_lat, query_rope, bounds, cache, keys, w_uv
     )
     parts = [value_part] + from_ranks([value_part] * (ranks - 1))
     copies = project(parts, w_out, lax.axis_size("dp"))

time: 86 us -> 88.3 us (1.027)
  waiting for transfers between devices: 21.8 us -> 16.5 us
  Pallas kernels: 9.48 us -> 14.5 us
  blocking collectives: 23.5 us -> 25.2 us
    all_to_all x1, waiting for transfers between devices: 9.46 us -> 0.01 us  [per_device(): lax.all_to_all(picked, 'dp', 0, 0, axis_index_groups=z_groups, tiled=True)]
    pallas_call x0 -> x2, Pallas kernels: none -> 7.67 us  [the longest x1 7.23 us: pack_live(): pl.pallas_call(body, out_shape=[jax.ShapeDtypeStruct((packed, lat_part),...]
    ppermute x13, waiting for transfers between devices: 12.4 us -> 16.5 us  [shifted(): return lax.ppermute(array, axis, pairs)]
    pallas_call x1, Pallas kernels: 5.7 us -> 3.03 us  [partial_scores(): pl.pallas_call(body, out_shape=[jax.ShapeDtypeStruct((2 * group, packed /...]
    all_to_all x1, blocking collectives: 23.5 us -> 25.2 us  [per_device(): everyone = lax.all_to_all(copies, 'dp', 0, 0, tiled=True)]
  transfers between devices with their start and end apart: 14 -> 14, of which waited for: 13 -> 11; matrix products, arithmetic and copies ran while one was open for 4% -> 4% of each run, Pallas kernels for 0% -> 8%
where the time goes in v4:
time: 88.3 us; the launch traced here: 88 us
  starting transfers between devices  25.3 us (29%)
  blocking collectives  25.2 us (29%)
  waiting for transfers between devices  16.5 us (19%)
  Pallas kernels  14.5 us (16%)
  local copies, waits for them, and re-layouts  2.92 us (3%)
  other arithmetic  2.24 us (3%)
    all_to_all x1, blocking collectives, per_device(): everyone = lax.all_to_all(copies, 'dp', 0, 0, tiled=True)  25.2 us
    ppermute x13, starting transfers between devices, shifted(): return lax.ppermute(array, axis, pairs)  17.2 us
    ppermute x13, waiting for transfers between devices, shifted(): return lax.ppermute(array, axis, pairs)  16.5 us
    all_to_all x1, starting transfers between devices, per_device(): lax.all_to_all(picked, 'dp', 0, 0, axis_index_groups=z_groups, tiled=True)  8.18 us
    pallas_call x1, Pallas kernels, pack_live(): pl.pallas_call(body, out_shape=[jax.ShapeDtypeStruct((packed, lat_part),...  7.23 us
    pallas_call x1, Pallas kernels, partial_scores(): pl.pallas_call(body, out_shape=[jax.ShapeDtypeStruct((2 * group, packed /...  3.03 us
  transfers between devices with their start and end apart: 14, of which 11 were waited for; matrix products, arithmetic and copies ran while one was open for 4% of the time, Pallas kernels for 8%

profile of v4, /device:TPU:1, one launch (start us, length us, event | category | flops | bytes accessed | tf_op | source)
XLA Modules:
  0.0 88.0 jit_solution(2794578435578672795)
XLA Ops:
  0.0 0.8 copy-done.3
  0.8 0.7 copy-done.4
  1.5 3.4 %collective-permute-start.26 = (bf16[4,3072]{1,0:T(4,128)(2,1)S(1)}, bf16[4,3072]{1,0:T(4,128)(2,1)S(1)}, u32[]{:S(2)}, u32[]{:S(2)}) collective-permute-start(bf16[4,3072]{1,0:T(4,128)(2,1)S(1)} %shard_map.91), channel_id=1, source_target_pairs={{0,24},{8,0},{16,8},{24,16},{4,28},{12,4},{20,12},{28,20},{32,56},... | collective-permute-start | bytes 73736 | tf_op jit(solution)/shard_map/ppermute | solution.py:22
  4.9 0.5 collective-permute-start.25
  5.4 0.6 collective-permute-start.24
  6.0 0.0 collective-permute-done.26
  6.0 3.0 %collective-permute-done.25 = bf16[4,3072]{1,0:T(4,128)(2,1)S(1)} collective-permute-done((bf16[4,3072]{1,0:T(4,128)(2,1)S(1)}, bf16[4,3072]{1,0:T(4,128)(2,1)S(1)}, u32[]{:S(2)}, u32[]{:S(2)}) %collective-permute-start.25) | collective-permute-done | bytes 24608 | tf_op jit(solution)/shard_map/ppermute | solution.py:22
  9.1 0.3 collective-permute-done.24
  9.3 0.1 pad_maximum_fusion.near_ref
  9.4 2.4 %collective-permute-start.27 = (bf16[16,3072]{1,0:T(8,128)(2,1)S(1)}, bf16[16,3072]{1,0:T(8,128)(2,1)S(1)}, u32[]{:S(2)}, u32[]{:S(2)}) collective-permute-start(bf16[16,3072]{1,0:T(8,128)(2,1)S(1)} %pad_maximum_fusion.near_ref), channel_id=1, source_target_pairs={{0,4},{4,0},{8,12},{12,8},{16,20},{20,16},{24,28},{28,24},{32,36},... | collective-permute-start | bytes 294920 | tf_op jit(solution)/shard_map/ppermute | solution.py:22
  11.8 0.9 select_reduce_fusion
  12.7 0.1 collective-permute-done.27.far_ref
  12.8 1.0 %shard_map.92.rest_0_ = bf16[8,4,3072]{2,1,0:T(4,128)(2,1)} custom-call(bf16[16,3072]{1,0:T(8,128)(2,1)S(1)} %pad_maximum_fusion.near_ref, bf16[16,3072]{1,0:T(8,128)(2,1)S(1)} %collective-permute-done.27.far_ref, s32[1,32]{1,0:T(1,128)S(1)} %bitcast.4), custom_call_target="tpu_custom_call" | custom-call | tf_op jit(solution)/shard_map/pallas_call | solution.py:98
  13.8 8.2 %all-to-all-start = ((bf16[8,4,3072]{2,1,0:T(4,128)(2,1)}), bf16[8,4,3072]{2,1,0:T(4,128)(2,1)S(1)}, u32[]{:S(2)}, u32[]{:S(2)}) async-start(bf16[8,4,3072]{2,1,0:T(4,128)(2,1)} %shard_map.92.rest_0_), calls=%async_computation | async-start | bytes 393216 | tf_op jit(solution)/shard_map/all_to_all | solution.py:414
  22.0 1.3 %fusion.10 = s32[]{:T(128)} fusion(s32[4]{0:T(128)} %len_ref.1), kind=kLoop, calls=%fused_computation.35 | loop fusion | flops 67 | bytes 20 | tf_op jit(solution)/shard_map/reduce_sum | solution.py:403
  23.9 0.8 dynamic-slice_bitcast_fusion
  24.7 0.7 copy.12.rest_1_.target_ref
  25.3 7.2 %shard_map.94 = (bf16[16384,128]{1,0:T(8,128)(2,1)}, bf16[16,16384]{1,0:T(8,128)(2,1)S(1)}, s32[16,128]{1,0:T(8,128)S(1)}) custom-call(s32[4]{0:T(128)} %len_ref.1, bf16[4,4096,128]{2,1,0:T(8,128)(2,1)} %cache_ref.1, bf16[4,16,4096]{2,1,0:T(8,128)(2,1)} %keys_ref.1, bf16[8,4,3072]{2,1,0:T(4,128)(2,1)} %shard_map.92.rest_0_, s32[4,1]{1,0:T(4,128)} %copy.12.rest_1_.target_ref, ...), custom_call_target="tpu_custom_call" | custom-call | tf_op jit(solution)/shard_map/pallas_call | solution.py:141
  32.6 0.0 all-to-all-done.arrived_ref
  32.6 0.0 copy-done.1
  32.6 0.4 shard_map.93
  33.1 0.0 copy-start
  33.1 0.0 copy-start.2
  33.1 23.2 %conditional.1 = (bf16[4,2048]{1,0:T(4,128)(2,1)S(1)}) conditional(s32[]{:T(128)} %clamp.3, (bf16[64,128]{1,0:T(8,128)(2,1)S(1)}, bf16[64,128]{1,0:T(8,128)(2,1)S(1)}, s32[16,128]{1,0:T(8,128)S(1)}, bf16[16384,128]{1,0:T(8,128)(2,1)}, bf16[16,16384]{1,0:T(8,128)(2,1)S(1)}, ...), branch_computations={%region_2.3_spmd, %region_3.4_spmd, %region_4.5_spmd, %region_5.6_... | conditional | bytes 4718840 | solution.py:429
  33.1 3.0 %branch_0_fun.3 = (f32[8,4608]{1,0:T(8,128)S(1)}, f32[8,4608]{1,0:T(8,128)S(1)}, f32[8,4608]{1,0:T(8,128)S(1)}, f32[8,4608]{1,0:T(8,128)S(1)}, bf16[9216,128]{1,0:T(8,128)(2,1)S(1)}) custom-call(bf16[64,128]{1,0:T(8,128)(2,1)S(1)} %get-tuple-element.56.lat_ref, bf16[64,128]{1,0:T(8,128)(2,1)S(1)} %get-tuple-element.58.rope_ref, ...), custom_call_target="tpu_custom_call" | custom-call | tf_op jit(solution)/shard_map/cond/branch_0_fun/pallas_call | solution.py:242
  36.1 1.4 %collective-permute-start = (f32[8,4608]{1,0:T(8,128)S(1)}, f32[8,4608]{1,0:T(8,128)S(1)}, u32[]{:S(2)}, u32[]{:S(2)}) collective-permute-start(f32[8,4608]{1,0:T(8,128)S(1)} %get-tuple-element.64), channel_id=1, source_target_pairs={{0,1},{1,2},{2,3},{3,0},{4,5},{5,6},{6,7},{7,4},{8,9},{9,10},{10,1... | collective-permute-start | bytes 442376 | tf_op jit(solution)/shard_map/cond/branch_0_fun/ppermute | solution.py:22
  37.5 2.6 %collective-permute-start.1 = (f32[8,4608]{1,0:T(8,128)S(1)}, f32[8,4608]{1,0:T(8,128)S(1)}, u32[]{:S(2)}, u32[]{:S(2)}) collective-permute-start(f32[8,4608]{1,0:T(8,128)S(1)} %get-tuple-element.65), channel_id=1, source_target_pairs={{0,2},{1,3},{2,0},{3,1},{4,6},{5,7},{6,4},{7,5},{8,10},{9,11},{10,... | collective-permute-start | bytes 442376 | tf_op jit(solution)/shard_map/cond/branch_0_fun/ppermute | solution.py:22
  40.1 1.1 %collective-permute-start.2 = (f32[8,4608]{1,0:T(8,128)S(1)}, f32[8,4608]{1,0:T(8,128)S(1)}, u32[]{:S(2)}, u32[]{:S(2)}) collective-permute-start(f32[8,4608]{1,0:T(8,128)S(1)} %get-tuple-element.66), channel_id=1, source_target_pairs={{0,3},{1,0},{2,1},{3,2},{4,7},{5,4},{6,5},{7,6},{8,11},{9,8},{10,9... | collective-permute-start | bytes 442376 | tf_op jit(solution)/shard_map/cond/branch_0_fun/ppermute | solution.py:22
  41.2 1.0 %collective-permute-done.refs_1_ = f32[8,4608]{1,0:T(8,128)S(1)} collective-permute-done((f32[8,4608]{1,0:T(8,128)S(1)}, f32[8,4608]{1,0:T(8,128)S(1)}, u32[]{:S(2)}, u32[]{:S(2)}) %collective-permute-start) | collective-permute-done | bytes 147488 | tf_op jit(solution)/shard_map/cond/branch_0_fun/ppermute | solution.py:22
  42.2 4.3 %collective-permute-done.1.refs_2_ = f32[8,4608]{1,0:T(8,128)S(1)} collective-permute-done((f32[8,4608]{1,0:T(8,128)S(1)}, f32[8,4608]{1,0:T(8,128)S(1)}, u32[]{:S(2)}, u32[]{:S(2)}) %collective-permute-start.1) | collective-permute-done | bytes 147488 | tf_op jit(solution)/shard_map/cond/branch_0_fun/ppermute | solution.py:22
  46.4 0.0 collective-permute-done.2.refs_3_
  46.4 0.7 branch_0_fun.4.refs_0_
  47.1 2.4 %collective-permute-start.5 = (bf16[8,4608]{1,0:T(8,128)(2,1)S(1)}, bf16[8,4608]{1,0:T(8,128)(2,1)S(1)}, u32[]{:S(2)}, u32[]{:S(2)}) collective-permute-start(bf16[8,4608]{1,0:T(8,128)(2,1)S(1)} %branch_0_fun.4.refs_0_), channel_id=1, source_target_pairs={{0,3},{1,0},{2,1},{3,2},{4,7},{5,4},{6,5},{7,6},{8,11},{9,8},{10,9... | collective-permute-start | bytes 221192 | tf_op jit(solution)/shard_map/cond/branch_0_fun/ppermute | solution.py:22
  49.5 0.9 %collective-permute-start.4 = (bf16[8,4608]{1,0:T(8,128)(2,1)S(1)}, bf16[8,4608]{1,0:T(8,128)(2,1)S(1)}, u32[]{:S(2)}, u32[]{:S(2)}) collective-permute-start(bf16[8,4608]{1,0:T(8,128)(2,1)S(1)} %branch_0_fun.4.refs_0_), channel_id=1, source_target_pairs={{0,2},{1,3},{2,0},{3,1},{4,6},{5,7},{6,4},{7,5},{8,10},{9,11},{10,... | collective-permute-start | bytes 221192 | tf_op jit(solution)/shard_map/cond/branch_0_fun/ppermute | solution.py:22
  50.4 0.0 collective-permute-start.3
  50.4 1.2 %collective-permute-done.5.refs_3_ = bf16[8,4608]{1,0:T(8,128)(2,1)S(1)} collective-permute-done((bf16[8,4608]{1,0:T(8,128)(2,1)S(1)}, bf16[8,4608]{1,0:T(8,128)(2,1)S(1)}, u32[]{:S(2)}, u32[]{:S(2)}) %collective-permute-start.5) | collective-permute-done | bytes 73760 | tf_op jit(solution)/shard_map/cond/branch_0_fun/ppermute | solution.py:22
  51.6 2.6 %collective-permute-done.4.refs_2_ = bf16[8,4608]{1,0:T(8,128)(2,1)S(1)} collective-permute-done((bf16[8,4608]{1,0:T(8,128)(2,1)S(1)}, bf16[8,4608]{1,0:T(8,128)(2,1)S(1)}, u32[]{:S(2)}, u32[]{:S(2)}) %collective-permute-start.4) | collective-permute-done | bytes 73760 | tf_op jit(solution)/shard_map/cond/branch_0_fun/ppermute | solution.py:22
  54.2 0.8 collective-permute-done.3.refs_1_
  55.0 0.8 branch_0_fun.5
  56.3 0.7 collective-permute-start.30
  56.9 0.8 collective-permute-start.29
  57.7 0.5 collective-permute-start.28
  58.1 0.8 collective-permute-done.30.refs_3_
  58.9 2.1 %collective-permute-done.29.refs_2_ = bf16[4,2048]{1,0:T(4,128)(2,1)S(1)} collective-permute-done((bf16[4,2048]{1,0:T(4,128)(2,1)S(1)}, bf16[4,2048]{1,0:T(4,128)(2,1)S(1)}, u32[]{:S(2)}, u32[]{:S(2)}) %collective-permute-start.29) | collective-permute-done | bytes 16416 | tf_op jit(solution)/shard_map/ppermute | solution.py:22
  61.0 0.5 collective-permute-done.28.refs_1_
  61.5 0.4 shard_map.95
  61.9 25.2 %all_to_all.10.all_ref = bf16[64,4,512]{2,1,0:T(4,128)(2,1)S(1)} all-to-all(bf16[64,4,512]{2,1,0:T(4,128)(2,1)S(1)} %shard_map.95), channel_id=1, replica_groups=mesh['dp'=64,'rank'=4] {'dp'}, dimensions={0} | all-to-all | bytes 524288 | tf_op jit(solution)/shard_map/all_to_all | solution.py:434
  87.1 0.9 shard_map.96
  (9 shorter events, 0.1 us)
Async XLA Ops:
  0.0 32.6 %copy-start.1 = (bf16[16,128,128]{2,1,0:T(8,128)(2,1)S(1)}, bf16[16,128,128]{2,1,0:T(8,128)(2,1)}, u32[]{:S(2)}) copy-start(bf16[16,128,128]{2,1,0:T(8,128)(2,1)} %w_ref.1) | copy-start | bytes 1572868
  0.0 0.8 copy-start.3
  0.8 0.7 copy-start.4
  1.5 4.5 %collective-permute-start.26 = (bf16[4,3072]{1,0:T(4,128)(2,1)S(1)}, bf16[4,3072]{1,0:T(4,128)(2,1)S(1)}, u32[]{:S(2)}, u32[]{:S(2)}) collective-permute-start(bf16[4,3072]{1,0:T(4,128)(2,1)S(1)} %shard_map.91), channel_id=1, source_target_pairs={{0,24},{8,0},{16,8},{24,16},{4,28},{12,4},{20,12},{28,20},{32,56},... | collective-permute-start | bytes 73736 | tf_op jit(solution)/shard_map/ppermute | solution.py:22
  4.9 4.2 %collective-permute-start.25 = (bf16[4,3072]{1,0:T(4,128)(2,1)S(1)}, bf16[4,3072]{1,0:T(4,128)(2,1)S(1)}, u32[]{:S(2)}, u32[]{:S(2)}) collective-permute-start(bf16[4,3072]{1,0:T(4,128)(2,1)S(1)} %shard_map.91), channel_id=1, source_target_pairs={{0,16},{8,24},{16,0},{24,8},{4,20},{12,28},{20,4},{28,12},{32,48},... | collective-permute-start | bytes 73736 | tf_op jit(solution)/shard_map/ppermute | solution.py:22
  5.4 3.9 %collective-permute-start.24 = (bf16[4,3072]{1,0:T(4,128)(2,1)S(1)}, bf16[4,3072]{1,0:T(4,128)(2,1)S(1)}, u32[]{:S(2)}, u32[]{:S(2)}) collective-permute-start(bf16[4,3072]{1,0:T(4,128)(2,1)S(1)} %shard_map.91), channel_id=1, source_target_pairs={{0,8},{8,16},{16,24},{24,0},{4,12},{12,20},{20,28},{28,4},{32,40},... | collective-permute-start | bytes 73736 | tf_op jit(solution)/shard_map/ppermute | solution.py:22
  9.4 3.4 %collective-permute-start.27 = (bf16[16,3072]{1,0:T(8,128)(2,1)S(1)}, bf16[16,3072]{1,0:T(8,128)(2,1)S(1)}, u32[]{:S(2)}, u32[]{:S(2)}) collective-permute-start(bf16[16,3072]{1,0:T(8,128)(2,1)S(1)} %pad_maximum_fusion.near_ref), channel_id=1, source_target_pairs={{0,4},{4,0},{8,12},{12,8},{16,20},{20,16},{24,28},{28,24},{32,36},... | collective-permute-start | bytes 294920 | tf_op jit(solution)/shard_map/ppermute | solution.py:22
  12.8 20.3 %copy-start.5 = (bf16[16,128,128]{2,1,0:T(8,128)(2,1)S(1)}, bf16[16,128,128]{2,1,0:T(8,128)(2,1)}, u32[]{:S(2)}) copy-start(bf16[16,128,128]{2,1,0:T(8,128)(2,1)} %param.20) | copy-start | bytes 1572868
  13.8 18.8 %all-to-all-start = ((bf16[8,4,3072]{2,1,0:T(4,128)(2,1)}), bf16[8,4,3072]{2,1,0:T(4,128)(2,1)S(1)}, u32[]{:S(2)}, u32[]{:S(2)}) async-start(bf16[8,4,3072]{2,1,0:T(4,128)(2,1)} %shard_map.92.rest_0_), calls=%async_computation | async-start | bytes 393216 | tf_op jit(solution)/shard_map/all_to_all | solution.py:414
  33.1 28.4 %copy-start = (bf16[2048,512]{1,0:T(8,128)(2,1)S(1)}, bf16[2048,512]{1,0:T(8,128)(2,1)}, u32[]{:S(2)}) copy-start(bf16[2048,512]{1,0:T(8,128)(2,1)} %refs_4_.1) | copy-start | bytes 6291460
  33.1 54.0 %copy-start.2 = (s32[4,1]{1,0:T(4,128)S(1)}, s32[4,1]{1,0:T(4,128)}, u32[]{:S(2)}) copy-start(s32[4,1]{1,0:T(4,128)} %copy.12.rest_1_.target_ref) | copy-start | bytes 52
  36.1 6.0 %collective-permute-start = (f32[8,4608]{1,0:T(8,128)S(1)}, f32[8,4608]{1,0:T(8,128)S(1)}, u32[]{:S(2)}, u32[]{:S(2)}) collective-permute-start(f32[8,4608]{1,0:T(8,128)S(1)} %get-tuple-element.64), channel_id=1, source_target_pairs={{0,1},{1,2},{2,3},{3,0},{4,5},{5,6},{6,7},{7,4},{8,9},{9,10},{10,1... | collective-permute-start | bytes 442376 | tf_op jit(solution)/shard_map/cond/branch_0_fun/ppermute | solution.py:22
  37.5 8.9 %collective-permute-start.1 = (f32[8,4608]{1,0:T(8,128)S(1)}, f32[8,4608]{1,0:T(8,128)S(1)}, u32[]{:S(2)}, u32[]{:S(2)}) collective-permute-start(f32[8,4608]{1,0:T(8,128)S(1)} %get-tuple-element.65), channel_id=1, source_target_pairs={{0,2},{1,3},{2,0},{3,1},{4,6},{5,7},{6,4},{7,5},{8,10},{9,11},{10,... | collective-permute-start | bytes 442376 | tf_op jit(solution)/shard_map/cond/branch_0_fun/ppermute | solution.py:22
  40.1 6.3 %collective-permute-start.2 = (f32[8,4608]{1,0:T(8,128)S(1)}, f32[8,4608]{1,0:T(8,128)S(1)}, u32[]{:S(2)}, u32[]{:S(2)}) collective-permute-start(f32[8,4608]{1,0:T(8,128)S(1)} %get-tuple-element.66), channel_id=1, source_target_pairs={{0,3},{1,0},{2,1},{3,2},{4,7},{5,4},{6,5},{7,6},{8,11},{9,8},{10,9... | collective-permute-start | bytes 442376 | tf_op jit(solution)/shard_map/cond/branch_0_fun/ppermute | solution.py:22
  47.1 4.5 %collective-permute-start.5 = (bf16[8,4608]{1,0:T(8,128)(2,1)S(1)}, bf16[8,4608]{1,0:T(8,128)(2,1)S(1)}, u32[]{:S(2)}, u32[]{:S(2)}) collective-permute-start(bf16[8,4608]{1,0:T(8,128)(2,1)S(1)} %branch_0_fun.4.refs_0_), channel_id=1, source_target_pairs={{0,3},{1,0},{2,1},{3,2},{4,7},{5,4},{6,5},{7,6},{8,11},{9,8},{10,9... | collective-permute-start | bytes 221192 | tf_op jit(solution)/shard_map/cond/branch_0_fun/ppermute | solution.py:22
  49.5 4.7 %collective-permute-start.4 = (bf16[8,4608]{1,0:T(8,128)(2,1)S(1)}, bf16[8,4608]{1,0:T(8,128)(2,1)S(1)}, u32[]{:S(2)}, u32[]{:S(2)}) collective-permute-start(bf16[8,4608]{1,0:T(8,128)(2,1)S(1)} %branch_0_fun.4.refs_0_), channel_id=1, source_target_pairs={{0,2},{1,3},{2,0},{3,1},{4,6},{5,7},{6,4},{7,5},{8,10},{9,11},{10,... | collective-permute-start | bytes 221192 | tf_op jit(solution)/shard_map/cond/branch_0_fun/ppermute | solution.py:22
  50.4 4.6 %collective-permute-start.3 = (bf16[8,4608]{1,0:T(8,128)(2,1)S(1)}, bf16[8,4608]{1,0:T(8,128)(2,1)S(1)}, u32[]{:S(2)}, u32[]{:S(2)}) collective-permute-start(bf16[8,4608]{1,0:T(8,128)(2,1)S(1)} %branch_0_fun.4.refs_0_), channel_id=1, source_target_pairs={{0,1},{1,2},{2,3},{3,0},{4,5},{5,6},{6,7},{7,4},{8,9},{9,10},{10,1... | collective-permute-start | bytes 221192 | tf_op jit(solution)/shard_map/cond/branch_0_fun/ppermute | solution.py:22
  56.3 2.7 %collective-permute-start.30 = (bf16[4,2048]{1,0:T(4,128)(2,1)S(1)}, bf16[4,2048]{1,0:T(4,128)(2,1)S(1)}, u32[]{:S(2)}, u32[]{:S(2)}) collective-permute-start(bf16[4,2048]{1,0:T(4,128)(2,1)S(1)} %get-tuple-element.112.refs_0_), channel_id=1, source_target_pairs={{0,3},{1,0},{2,1},{3,2},{4,7},{5,4},{6,5},{7,6},{8,11},{9,8},{10,9... | collective-permute-start | bytes 49160 | tf_op jit(solution)/shard_map/ppermute | solution.py:22
  56.9 4.1 %collective-permute-start.29 = (bf16[4,2048]{1,0:T(4,128)(2,1)S(1)}, bf16[4,2048]{1,0:T(4,128)(2,1)S(1)}, u32[]{:S(2)}, u32[]{:S(2)}) collective-permute-start(bf16[4,2048]{1,0:T(4,128)(2,1)S(1)} %get-tuple-element.112.refs_0_), channel_id=1, source_target_pairs={{0,2},{1,3},{2,0},{3,1},{4,6},{5,7},{6,4},{7,5},{8,10},{9,11},{10,... | collective-permute-start | bytes 49160 | tf_op jit(solution)/shard_map/ppermute | solution.py:22
  57.7 3.8 %collective-permute-start.28 = (bf16[4,2048]{1,0:T(4,128)(2,1)S(1)}, bf16[4,2048]{1,0:T(4,128)(2,1)S(1)}, u32[]{:S(2)}, u32[]{:S(2)}) collective-permute-start(bf16[4,2048]{1,0:T(4,128)(2,1)S(1)} %get-tuple-element.112.refs_0_), channel_id=1, source_target_pairs={{0,1},{1,2},{2,3},{3,0},{4,5},{5,6},{6,7},{7,4},{8,9},{9,10},{10,1... | collective-permute-start | bytes 49160 | tf_op jit(solution)/shard_map/ppermute | solution.py:22

commit v5 on v4

--- a/solution.py
+++ b/solution.py
@@ -31,11 +31,8 @@
 
 F32, BF16 = jnp.float32, jnp.bfloat16
 BLOCK = 512
-CHUNK = 4
 SIZES = (9216, 10240, 12288)
 SMALL = pltpu.CompilerParams(vmem_limit_bytes=8 << 20)
-LARGE = pltpu.CompilerParams(vmem_limit_bytes=60 << 20)
-HALF = pltpu.CompilerParams(vmem_limit_bytes=40 << 20)
 
 
 def vmem():
@@ -78,14 +75,15 @@
         in_specs=[hbm()] * 2,
         out_specs=vmem(),
         scratch_shapes=[pltpu.SemaphoreType.DMA((2,))],
-        compiler_params=HALF,
+        compiler_params=SMALL,
     )(q_nope, q_rope)
 
 
-def pick_rows(near, far, slot_here, seqs):
+def pick_rows(near, far, slot_here, seqs, ready):
     rows, width = near.shape
 
-    def body(near_ref, far_ref, slot_ref, out_ref):
+    def body(near_ref, far_ref, slot_ref, *rest):
+        out_ref = rest[-1]
         dp = lax.axis_index("dp")
         i = iota((NZ * seqs, 2 * rows), 0)
         wanted = (i // seqs * (NX * NC) + dp % (NX * NC)) * seqs + i % seqs
@@ -98,58 +96,23 @@
     return pl.pallas_call(
         body,
         out_shape=jax.ShapeDtypeStruct((NZ, seqs, width), BF16),
-        in_specs=[vmem()] * 3,
-        out_specs=vmem(),
-        compiler_params=SMALL,
-    )(near, far, slot_here)
-
-
-def pack_live(lengths, latent_cache, rope_keys, ready):
-    seqs, capacity, lat_part = latent_cache.shape
-    rope_part = rope_keys.shape[1]
-    packed = seqs * capacity
-    blocks = packed // BLOCK
-
-    def body(len_ref, cache_ref, keys_ref, *rest):
-        cache, keys, bounds_ref, sems = rest[-4:]
-        starts = [jnp.int32(0)]
-        for s in range(seqs):
-            starts.append(starts[-1] + (len_ref[s] + BLOCK - 1) // BLOCK)
-        copies = []
-        for b in range(blocks):
-            slot = jnp.int32(0)
-            start = jnp.int32(0)
-            for s in range(1, seqs):
-                slot = jnp.where(b >= starts[s], s, slot)
-                start = jnp.where(b >= starts[s], starts[s], start)
-            block = jnp.minimum(b - start, capacity // BLOCK - 1)
-            source = pl.ds(pl.multiple_of(block * BLOCK, BLOCK), BLOCK)
-            at = pl.ds(b * BLOCK, BLOCK)
-            copies += [
-                pltpu.make_async_copy(cache_ref.at[slot, source], cache.at[at], sems.at[0, b]),
-                pltpu.make_async_copy(keys_ref.at[slot, :, source], keys.at[:, at], sems.at[1, b]),
-            ]
-            copies[-2].start()
-            copies[-1].start()
-        for s in range(seqs):
-            first = starts[s] * BLOCK
-            bounds_ref[s : s + 1, :] = jnp.full((1, 128), first, jnp.int32)
-            bounds_ref[8 + s : 9 + s, :] = jnp.full((1, 128), first + len_ref[s], jnp.int32)
-        for copy in copies:
-            copy.wait()
-
-    return pl.pallas_call(
-        body,
-        out_shape=[
-            jax.ShapeDtypeStruct((packed, lat_part), BF16),
-            jax.ShapeDtypeStruct((rope_part, packed), BF16),
-            jax.ShapeDtypeStruct((16, 128), jnp.int32),
-        ],
-        in_specs=[smem(), hbm(), hbm()] + [hbm()] * len(ready),
-        out_specs=[vmem()] * 3,
-        compiler_params=LARGE,
-        scratch_shapes=[pltpu.SemaphoreType.DMA((2, blocks))],
-    )(lengths, latent_cache, rope_keys, *ready)
+        in_specs=[vmem()] * (3 + len(ready)),
+        out_specs=vmem(),
+        compiler_params=SMALL,
+    )(near, far, slot_here, *ready)
+
+
+def fetch(after, array):
+    def body(_, array_ref, out_ref):
+        out_ref[...] = array_ref[...]
+
+    return pl.pallas_call(
+        body,
+        out_shape=jax.ShapeDtypeStruct(array.shape, array.dtype),
+        in_specs=[hbm(), vmem()],
+        out_specs=vmem(),
+        compiler_params=SMALL,
+    )(after, array)
 
 
 def absorb(arrived, w_uk, rope_part):
@@ -200,40 +163,53 @@
     return (pos >= bounds_ref[slot : slot + 1, :1]) & (pos < bounds_ref[8 + slot : 9 + slot, :1])
 
 
-def partial_scores(query_lat, query_rope, bounds, cache, keys, packed, seqs, scale):
-    heads, lat_part = query_lat.shape[0] // seqs, query_lat.shape[1]
-    rope_part = keys.shape[0]
+def partial_scores(query_lat, query_rope, lengths, latent_cache, rope_keys, packed, scale):
+    seqs, capacity, lat_part = latent_cache.shape
+    heads = query_lat.shape[0] // seqs
+    rope_part = rope_keys.shape[1]
     ranks = lax.axis_size("rank")
     group = heads // ranks
     blocks, half = packed // BLOCK, packed // BLOCK // 2
-    chunks = [(b, min(b + CHUNK, blocks)) for b in range(0, blocks, CHUNK)]
-
-    def body(lat_ref, rope_ref, bounds_ref, cache_hbm, keys_hbm, *rest):
-        outs, (cache_ref, keys_ref, sems) = rest[:ranks], rest[ranks:]
+
+    def body(lat_ref, rope_ref, len_ref, cache_hbm, keys_hbm, *rest):
+        outs, (bounds_ref, cache_ref, keys_ref, sems) = rest[:ranks], rest[ranks:]
+        starts = [jnp.int32(0)]
+        for s in range(seqs):
+            starts.append(starts[-1] + (len_ref[s] + BLOCK - 1) // BLOCK)
         copies = []
-        for i, (first, end) in enumerate(chunks):
-            at = pl.ds(first * BLOCK, (end - first) * BLOCK)
+        for b in range(blocks):
+            slot = jnp.int32(0)
+            start = jnp.int32(0)
+            for s in range(1, seqs):
+                slot = jnp.where(b >= starts[s], s, slot)
+                start = jnp.where(b >= starts[s], starts[s], start)
+            block = jnp.minimum(b - start, capacity // BLOCK - 1)
+            source = pl.ds(pl.multiple_of(block * BLOCK, BLOCK), BLOCK)
+            at = pl.ds(b * BLOCK, BLOCK)
             copies += [
-                pltpu.make_async_copy(cache_hbm.at[at], cache_ref.at[at], sems.at[0, i]),
-                pltpu.make_async_copy(keys_hbm.at[:, at], keys_ref.at[:, at], sems.at[1, i]),
+                pltpu.make_async_copy(cache_hbm.at[slot, source], cache_ref.at[at], sems.at[0, b]),
+                pltpu.make_async_copy(
+                    keys_hbm.at[slot, :, source], keys_ref.at[:, at], sems.at[1, b]
+                ),
             ]
             copies[-2].start()
             copies[-1].start()
+        for s in range(seqs):
+            first = starts[s] * BLOCK
+            bounds_ref[s : s + 1, :] = jnp.full((1, 128), first, jnp.int32)
+            bounds_ref[8 + s : 9 + s, :] = jnp.full((1, 128), first + len_ref[s], jnp.int32)
         lat, rope = lat_ref[...], rope_ref[:, :rope_part]
         for b in range(blocks):
-            if b % CHUNK == 0:
-                copies[b // CHUNK * 2].wait()
-                copies[b // CHUNK * 2 + 1].wait()
+            copies[2 * b].wait()
+            copies[2 * b + 1].wait()
             at = pl.ds(b * BLOCK, BLOCK)
             every = lax.dot_general(
                 lat, cache_ref[at, :], (((1,), (1,)), ((), ())), preferred_element_type=F32
             )
             every = every + dot(rope, keys_ref[:, at])
-            pos = iota((heads, BLOCK), 1) + b * BLOCK
             part = every[:heads]
             for s in range(1, seqs):
-                rows = every[s * heads : (s + 1) * heads]
-                part = jnp.where(pos >= bounds_ref[s : s + 1, :1], rows, part)
+                part = jnp.where(b >= starts[s], every[s * heads : (s + 1) * heads], part)
             part = part * scale
             row, to = b // half * group, pl.ds(b % half * BLOCK, BLOCK)
             for k in range(ranks):
@@ -242,15 +218,18 @@
     return pl.pallas_call(
         body,
         out_shape=[jax.ShapeDtypeStruct((2 * group, packed // 2), F32)] * ranks
-        + [jax.ShapeDtypeStruct((packed, lat_part), BF16)],
-        in_specs=[vmem()] * 3 + [hbm()] * 2,
-        out_specs=[vmem()] * (ranks + 1),
+        + [
+            jax.ShapeDtypeStruct((16, 128), jnp.int32),
+            jax.ShapeDtypeStruct((packed, lat_part), BF16),
+        ],
+        in_specs=[vmem(), vmem(), smem(), hbm(), hbm()],
+        out_specs=[vmem()] * (ranks + 2),
         compiler_params=SMALL,
         scratch_shapes=[
             pltpu.VMEM((rope_part, packed), BF16),
-            pltpu.SemaphoreType.DMA((2, len(chunks))),
+            pltpu.SemaphoreType.DMA((2, blocks)),
         ],
-    )(query_lat, query_rope, bounds, cache, keys)
+    )(query_lat, query_rope, lengths, latent_cache, rope_keys)
 
 
 def softmax(parts, bounds, seqs):
@@ -407,18 +386,15 @@
     near = [rows] + [shifted(rows, "dp", x_groups, k) for k in range(1, NX)]
     near = jnp.concatenate(near, axis=0)
     far = shifted(near, "dp", c_groups, 1)
-    picked = pick_rows(near, far, slot_here, seqs)
-    cache, keys, bounds = pack_live(
-        lengths, latent_cache, rope_keys, (picked, targets, which.reshape(1, 1))
-    )
+    picked = pick_rows(near, far, slot_here, seqs, (targets, which.reshape(1, 1)))
     arrived = lax.all_to_all(picked, "dp", 0, 0, axis_index_groups=z_groups, tiled=True)
 
-    query_lat, query_rope = absorb(arrived, w_uk, rope_keys.shape[1])
+    query_lat, query_rope = absorb(arrived, fetch(picked, w_uk), rope_keys.shape[1])
 
     def attend(packed):
-        def branch(query_lat, query_rope, bounds, cache, keys, w_uv):
-            own, *others, held = partial_scores(
-                query_lat, query_rope, bounds, cache, keys, packed, seqs, scale
+        def branch(query_lat, query_rope, lengths, latent_cache, rope_keys, w_uv):
+            own, *others, bounds, held = partial_scores(
+                query_lat, query_rope, lengths, latent_cache, rope_keys, packed, scale
             )
             weights = softmax([own] + from_ranks(others), bounds, seqs)
             gathered = [weights] + from_ranks([weights] * (ranks - 1))
@@ -427,7 +403,14 @@
         return branch
 
     value_part = lax.switch(
-        which, [attend(n) for n in sizes], query_lat, query_rope, bounds, cache, keys, w_uv
+        which,
+        [attend(n) for n in sizes],
+        query_lat,
+        query_rope,
+        lengths,
+        latent_cache,
+        rope_keys,
+        w_uv,
     )
     parts = [value_part] + from_ranks([value_part] * (ranks - 1))
     copies = project(parts, w_out, lax.axis_size("dp"))

time: 88.3 us -> 88.4 us (level)
  Pallas kernels: 14.5 us -> 9.64 us
  waiting for transfers between devices: 16.5 us -> 20.8 us
    all_to_all x1, waiting for transfers between devices: 0.01 us -> 8.38 us  [per_device(): lax.all_to_all(picked, 'dp', 0, 0, axis_index_groups=z_groups, tiled=True)]
    pallas_call x1, Pallas kernels: 7.23 us -> 0.03 us  [fetch(): pl.pallas_call(body, out_shape=jax.ShapeDtypeStruct(array.shape, array.dt...]
    ppermute x13, waiting for transfers between devices: 16.5 us -> 12.4 us  [shifted(): return lax.ppermute(array, axis, pairs)]
    pallas_call x1, Pallas kernels: 3.03 us -> 5.39 us  [partial_scores(): pl.pallas_call(body, out_shape=[jax.ShapeDtypeStruct((2 * group, packed /...]
    unnamed x12 -> x8, local copies, waits for them, and re-layouts: 1.49 us -> 2.46 us
  transfers between devices with their start and end apart: 14 -> 14, of which waited for: 11 -> 13; matrix products, arithmetic and copies ran while one was open for 4% -> 3% of each run, Pallas kernels for 8% -> 0%
where the time goes in v5:
time: 88.4 us; the launch traced here: 87.4 us
  starting transfers between devices  25.3 us (29%)
  blocking collectives  24.9 us (28%)
  waiting for transfers between devices  20.8 us (24%)
  Pallas kernels  9.64 us (11%)
  local copies, waits for them, and re-layouts  3.31 us (4%)
  other arithmetic  2.24 us (3%)
    all_to_all x1, blocking collectives, per_device(): everyone = lax.all_to_all(copies, 'dp', 0, 0, tiled=True)  24.9 us
    ppermute x13, starting transfers between devices, shifted(): return lax.ppermute(array, axis, pairs)  17.1 us
    ppermute x13, waiting for transfers between devices, shifted(): return lax.ppermute(array, axis, pairs)  12.4 us
    all_to_all x1, waiting for transfers between devices, per_device(): lax.all_to_all(picked, 'dp', 0, 0, axis_index_groups=z_groups, tiled=True)  8.38 us
    all_to_all x1, starting transfers between devices, per_device(): lax.all_to_all(picked, 'dp', 0, 0, axis_index_groups=z_groups, tiled=True)  8.19 us
    pallas_call x1, Pallas kernels, partial_scores(): pl.pallas_call(body, out_shape=[jax.ShapeDtypeStruct((2 * group, packed /...  5.39 us
    unnamed x8, local copies, waits for them, and re-layouts  2.46 us
  transfers between devices with their start and end apart: 14, of which 13 were waited for; matrix products, arithmetic and copies ran while one was open for 3% of the time, Pallas kernels for 0%

profile of v5, /device:TPU:1, one launch (start us, length us, event | category | flops | bytes accessed | tf_op | source)
XLA Modules:
  0.0 87.4 jit_solution(1908599036881786056)
XLA Ops:
  0.0 0.7 copy-done.2
  0.7 0.7 copy-done.3
  1.5 3.4 %collective-permute-start.26 = (bf16[4,3072]{1,0:T(4,128)(2,1)S(1)}, bf16[4,3072]{1,0:T(4,128)(2,1)S(1)}, u32[]{:S(2)}, u32[]{:S(2)}) collective-permute-start(bf16[4,3072]{1,0:T(4,128)(2,1)S(1)} %shard_map.91), channel_id=1, source_target_pairs={{0,24},{8,0},{16,8},{24,16},{4,28},{12,4},{20,12},{28,20},{32,56},... | collective-permute-start | bytes 73736 | tf_op jit(solution)/shard_map/ppermute | solution.py:22
  4.8 0.5 collective-permute-start.25
  5.3 0.6 collective-permute-start.24
  6.0 1.3 %fusion.10 = s32[]{:T(128)} fusion(s32[4]{0:T(128)} %param.17), kind=kLoop, calls=%fused_computation.35 | loop fusion | flops 67 | bytes 20 | tf_op jit(solution)/shard_map/reduce_sum | solution.py:382
  7.3 0.8 dynamic-slice_bitcast_fusion
  8.7 0.1 copy.12.rest_0_.target_ref
  8.8 0.0 collective-permute-done.26
  8.8 0.2 collective-permute-done.25
  9.0 0.3 collective-permute-done.24
  9.3 0.1 pad_maximum_fusion.near_ref
  9.3 2.4 %collective-permute-start.27 = (bf16[16,3072]{1,0:T(8,128)(2,1)S(1)}, bf16[16,3072]{1,0:T(8,128)(2,1)S(1)}, u32[]{:S(2)}, u32[]{:S(2)}) collective-permute-start(bf16[16,3072]{1,0:T(8,128)(2,1)S(1)} %pad_maximum_fusion.near_ref), channel_id=1, source_target_pairs={{0,4},{4,0},{8,12},{12,8},{16,20},{20,16},{24,28},{28,24},{32,36},... | collective-permute-start | bytes 294920 | tf_op jit(solution)/shard_map/ppermute | solution.py:22
  11.8 0.9 select_reduce_fusion
  12.6 0.1 collective-permute-done.27.far_ref
  12.7 1.0 %shard_map.92._ = bf16[8,4,3072]{2,1,0:T(4,128)(2,1)} custom-call(bf16[16,3072]{1,0:T(8,128)(2,1)S(1)} %pad_maximum_fusion.near_ref, bf16[16,3072]{1,0:T(8,128)(2,1)S(1)} %collective-permute-done.27.far_ref, s32[1,32]{1,0:T(1,128)S(1)} %bitcast.4, s32[4,1]{1,0:T(4,128)S(1)} %copy.12.rest_0_.target_ref, s32[1,1]{1,0:T(1,128)} %bitcast.2.rest_1_), custom_call_target="tpu_custom_call" | custom-call | tf_op jit(solution)/shard_map/pallas_call | solution.py:96
  13.7 8.2 %all-to-all-start = ((bf16[8,4,3072]{2,1,0:T(4,128)(2,1)}), bf16[8,4,3072]{2,1,0:T(4,128)(2,1)S(1)}, u32[]{:S(2)}, u32[]{:S(2)}) async-start(bf16[8,4,3072]{2,1,0:T(4,128)(2,1)} %shard_map.92._), calls=%async_computation | async-start | bytes 393216 | tf_op jit(solution)/shard_map/all_to_all | solution.py:390
  21.9 1.0 %copy-done.1 = bf16[16,128,128]{2,1,0:T(8,128)(2,1)S(1)} copy-done((bf16[16,128,128]{2,1,0:T(8,128)(2,1)S(1)}, bf16[16,128,128]{2,1,0:T(8,128)(2,1)}, u32[]{:S(2)}) %copy-start.1) | copy-done | bytes 524312
  23.0 8.4 %all-to-all-done.arrived_ref = bf16[8,4,3072]{2,1,0:T(4,128)(2,1)S(1)} async-done(((bf16[8,4,3072]{2,1,0:T(4,128)(2,1)}), bf16[8,4,3072]{2,1,0:T(4,128)(2,1)S(1)}, u32[]{:S(2)}, u32[]{:S(2)}) %all-to-all-start) | async-done | bytes 196640 | tf_op jit(solution)/shard_map/all_to_all | solution.py:390
  31.4 0.4 shard_map.94
  31.8 24.3 %conditional.1 = (bf16[4,2048]{1,0:T(4,128)(2,1)S(1)}) conditional(s32[]{:T(128)} %clamp.3, (bf16[64,128]{1,0:T(8,128)(2,1)S(1)}, bf16[64,128]{1,0:T(8,128)(2,1)S(1)}, s32[4]{0:T(128)}, bf16[4,4096,128]{2,1,0:T(8,128)(2,1)}, bf16[4,16,4096]{2,1,0:T(8,128)(2,1)}, /*index=5*/bf16[16,128,128]{2,1,0:T(8,128)(2,1)}) %tuple.17, ...), branch_computations={%region_2.3_spmd, %region_3.4_spmd, %region_4.5_spmd, %region_5.6_... | conditional | bytes 6816020 | solution.py:405
  31.8 0.0 copy-start.4
  31.8 5.4 %branch_0_fun.3 = (f32[8,4608]{1,0:T(8,128)S(1)}, f32[8,4608]{1,0:T(8,128)S(1)}, f32[8,4608]{1,0:T(8,128)S(1)}, f32[8,4608]{1,0:T(8,128)S(1)}, s32[16,128]{1,0:T(8,128)S(1)}, /*index=5*/bf16[9216,128]{1,0:T(8,128)(2,1)S(1)}) custom-call(bf16[64,128]{1,0:T(8,128)(2,1)S(1)} %get-tuple-element.56.lat_ref, bf16[64,128]{1,0:T(8,128)(2,1)S(1)} %get-tuple-element.58.rope_ref, ...), custom_call_target="tpu_custom_call" | custom-call | tf_op jit(solution)/shard_map/cond/branch_0_fun/pallas_call | solution.py:218
  37.2 1.4 %collective-permute-start = (f32[8,4608]{1,0:T(8,128)S(1)}, f32[8,4608]{1,0:T(8,128)S(1)}, u32[]{:S(2)}, u32[]{:S(2)}) collective-permute-start(f32[8,4608]{1,0:T(8,128)S(1)} %get-tuple-element.64), channel_id=1, source_target_pairs={{0,1},{1,2},{2,3},{3,0},{4,5},{5,6},{6,7},{7,4},{8,9},{9,10},{10,1... | collective-permute-start | bytes 442376 | tf_op jit(solution)/shard_map/cond/branch_0_fun/ppermute | solution.py:22
  38.6 2.6 %collective-permute-start.1 = (f32[8,4608]{1,0:T(8,128)S(1)}, f32[8,4608]{1,0:T(8,128)S(1)}, u32[]{:S(2)}, u32[]{:S(2)}) collective-permute-start(f32[8,4608]{1,0:T(8,128)S(1)} %get-tuple-element.65), channel_id=1, source_target_pairs={{0,2},{1,3},{2,0},{3,1},{4,6},{5,7},{6,4},{7,5},{8,10},{9,11},{10,... | collective-permute-start | bytes 442376 | tf_op jit(solution)/shard_map/cond/branch_0_fun/ppermute | solution.py:22
  41.2 1.1 %collective-permute-start.2 = (f32[8,4608]{1,0:T(8,128)S(1)}, f32[8,4608]{1,0:T(8,128)S(1)}, u32[]{:S(2)}, u32[]{:S(2)}) collective-permute-start(f32[8,4608]{1,0:T(8,128)S(1)} %get-tuple-element.66), channel_id=1, source_target_pairs={{0,3},{1,0},{2,1},{3,2},{4,7},{5,4},{6,5},{7,6},{8,11},{9,8},{10,9... | collective-permute-start | bytes 442376 | tf_op jit(solution)/shard_map/cond/branch_0_fun/ppermute | solution.py:22
  42.3 0.3 collective-permute-done.refs_1_
  42.6 3.5 %collective-permute-done.1.refs_2_ = f32[8,4608]{1,0:T(8,128)S(1)} collective-permute-done((f32[8,4608]{1,0:T(8,128)S(1)}, f32[8,4608]{1,0:T(8,128)S(1)}, u32[]{:S(2)}, u32[]{:S(2)}) %collective-permute-start.1) | collective-permute-done | bytes 147488 | tf_op jit(solution)/shard_map/cond/branch_0_fun/ppermute | solution.py:22
  46.1 0.4 collective-permute-done.2.refs_3_
  46.5 0.7 branch_0_fun.4.refs_0_
  47.2 2.2 %collective-permute-start.5 = (bf16[8,4608]{1,0:T(8,128)(2,1)S(1)}, bf16[8,4608]{1,0:T(8,128)(2,1)S(1)}, u32[]{:S(2)}, u32[]{:S(2)}) collective-permute-start(bf16[8,4608]{1,0:T(8,128)(2,1)S(1)} %branch_0_fun.4.refs_0_), channel_id=1, source_target_pairs={{0,3},{1,0},{2,1},{3,2},{4,7},{5,4},{6,5},{7,6},{8,11},{9,8},{10,9... | collective-permute-start | bytes 221192 | tf_op jit(solution)/shard_map/cond/branch_0_fun/ppermute | solution.py:22
  49.5 0.1 collective-permute-start.4
  49.6 0.6 collective-permute-start.3
  50.2 0.6 collective-permute-done.5.refs_3_
  50.9 3.4 %collective-permute-done.4.refs_2_ = bf16[8,4608]{1,0:T(8,128)(2,1)S(1)} collective-permute-done((bf16[8,4608]{1,0:T(8,128)(2,1)S(1)}, bf16[8,4608]{1,0:T(8,128)(2,1)S(1)}, u32[]{:S(2)}, u32[]{:S(2)}) %collective-permute-start.4) | collective-permute-done | bytes 73760 | tf_op jit(solution)/shard_map/cond/branch_0_fun/ppermute | solution.py:22
  54.3 0.5 collective-permute-done.3.refs_1_
  54.8 0.0 copy-done.4
  54.8 0.8 branch_0_fun.5
  56.1 0.5 collective-permute-start.30
  56.6 0.8 collective-permute-start.29
  57.4 0.8 collective-permute-start.28
  58.2 0.6 collective-permute-done.30.refs_3_
  58.8 1.9 %collective-permute-done.29.refs_2_ = bf16[4,2048]{1,0:T(4,128)(2,1)S(1)} collective-permute-done((bf16[4,2048]{1,0:T(4,128)(2,1)S(1)}, bf16[4,2048]{1,0:T(4,128)(2,1)S(1)}, u32[]{:S(2)}, u32[]{:S(2)}) %collective-permute-start.29) | collective-permute-done | bytes 16416 | tf_op jit(solution)/shard_map/ppermute | solution.py:22
  60.7 0.5 collective-permute-done.28.refs_1_
  61.2 0.0 copy-done
  61.2 0.4 shard_map.95
  61.6 24.9 %all_to_all.10.all_ref = bf16[64,4,512]{2,1,0:T(4,128)(2,1)S(1)} all-to-all(bf16[64,4,512]{2,1,0:T(4,128)(2,1)S(1)} %shard_map.95), channel_id=1, replica_groups=mesh['dp'=64,'rank'=4] {'dp'}, dimensions={0} | all-to-all | bytes 524288 | tf_op jit(solution)/shard_map/all_to_all | solution.py:417
  86.5 0.9 %shard_map.96 = bf16[4,512]{1,0:T(4,128)(2,1)} custom-call(bf16[64,4,512]{2,1,0:T(4,128)(2,1)S(1)} %all_to_all.10.all_ref, s32[4,1]{1,0:T(4,128)S(1)} %copy.12.rest_0_.target_ref), custom_call_target="tpu_custom_call" | custom-call | tf_op jit(solution)/shard_map/pallas_call | solution.py:349
  (7 shorter events, 0.1 us)
Async XLA Ops:
  0.0 0.7 copy-start.2
  0.7 0.7 copy-start.3
  1.5 7.3 %collective-permute-start.26 = (bf16[4,3072]{1,0:T(4,128)(2,1)S(1)}, bf16[4,3072]{1,0:T(4,128)(2,1)S(1)}, u32[]{:S(2)}, u32[]{:S(2)}) collective-permute-start(bf16[4,3072]{1,0:T(4,128)(2,1)S(1)} %shard_map.91), channel_id=1, source_target_pairs={{0,24},{8,0},{16,8},{24,16},{4,28},{12,4},{20,12},{28,20},{32,56},... | collective-permute-start | bytes 73736 | tf_op jit(solution)/shard_map/ppermute | solution.py:22
  4.8 4.2 %collective-permute-start.25 = (bf16[4,3072]{1,0:T(4,128)(2,1)S(1)}, bf16[4,3072]{1,0:T(4,128)(2,1)S(1)}, u32[]{:S(2)}, u32[]{:S(2)}) collective-permute-start(bf16[4,3072]{1,0:T(4,128)(2,1)S(1)} %shard_map.91), channel_id=1, source_target_pairs={{0,16},{8,24},{16,0},{24,8},{4,20},{12,28},{20,4},{28,12},{32,48},... | collective-permute-start | bytes 73736 | tf_op jit(solution)/shard_map/ppermute | solution.py:22
  5.3 3.9 %collective-permute-start.24 = (bf16[4,3072]{1,0:T(4,128)(2,1)S(1)}, bf16[4,3072]{1,0:T(4,128)(2,1)S(1)}, u32[]{:S(2)}, u32[]{:S(2)}) collective-permute-start(bf16[4,3072]{1,0:T(4,128)(2,1)S(1)} %shard_map.91), channel_id=1, source_target_pairs={{0,8},{8,16},{16,24},{24,0},{4,12},{12,20},{20,28},{28,4},{32,40},... | collective-permute-start | bytes 73736 | tf_op jit(solution)/shard_map/ppermute | solution.py:22
  9.3 3.4 %collective-permute-start.27 = (bf16[16,3072]{1,0:T(8,128)(2,1)S(1)}, bf16[16,3072]{1,0:T(8,128)(2,1)S(1)}, u32[]{:S(2)}, u32[]{:S(2)}) collective-permute-start(bf16[16,3072]{1,0:T(8,128)(2,1)S(1)} %pad_maximum_fusion.near_ref), channel_id=1, source_target_pairs={{0,4},{4,0},{8,12},{12,8},{16,20},{20,16},{24,28},{28,24},{32,36},... | collective-permute-start | bytes 294920 | tf_op jit(solution)/shard_map/ppermute | solution.py:22
  13.7 17.7 %all-to-all-start = ((bf16[8,4,3072]{2,1,0:T(4,128)(2,1)}), bf16[8,4,3072]{2,1,0:T(4,128)(2,1)S(1)}, u32[]{:S(2)}, u32[]{:S(2)}) async-start(bf16[8,4,3072]{2,1,0:T(4,128)(2,1)} %shard_map.92._), calls=%async_computation | async-start | bytes 393216 | tf_op jit(solution)/shard_map/all_to_all | solution.py:390
  21.9 1.0 %copy-start.1 = (bf16[16,128,128]{2,1,0:T(8,128)(2,1)S(1)}, bf16[16,128,128]{2,1,0:T(8,128)(2,1)}, u32[]{:S(2)}) copy-start(bf16[16,128,128]{2,1,0:T(8,128)(2,1)} %array_ref.1) | copy-start | bytes 1572868
  31.8 29.4 %copy-start = (bf16[2048,512]{1,0:T(8,128)(2,1)S(1)}, bf16[2048,512]{1,0:T(8,128)(2,1)}, u32[]{:S(2)}) copy-start(bf16[2048,512]{1,0:T(8,128)(2,1)} %refs_4_.1) | copy-start | bytes 6291460
  31.8 23.0 %copy-start.4 = (bf16[16,128,128]{2,1,0:T(8,128)(2,1)S(1)}, bf16[16,128,128]{2,1,0:T(8,128)(2,1)}, u32[]{:S(2)}) copy-start(bf16[16,128,128]{2,1,0:T(8,128)(2,1)} %get-tuple-element.69.refs_6_) | copy-start | bytes 1572868 | tf_op jit(solution)/shard_map/cond
  37.2 5.4 %collective-permute-start = (f32[8,4608]{1,0:T(8,128)S(1)}, f32[8,4608]{1,0:T(8,128)S(1)}, u32[]{:S(2)}, u32[]{:S(2)}) collective-permute-start(f32[8,4608]{1,0:T(8,128)S(1)} %get-tuple-element.64), channel_id=1, source_target_pairs={{0,1},{1,2},{2,3},{3,0},{4,5},{5,6},{6,7},{7,4},{8,9},{9,10},{10,1... | collective-permute-start | bytes 442376 | tf_op jit(solution)/shard_map/cond/branch_0_fun/ppermute | solution.py:22
  38.6 7.5 %collective-permute-start.1 = (f32[8,4608]{1,0:T(8,128)S(1)}, f32[8,4608]{1,0:T(8,128)S(1)}, u32[]{:S(2)}, u32[]{:S(2)}) collective-permute-start(f32[8,4608]{1,0:T(8,128)S(1)} %get-tuple-element.65), channel_id=1, source_target_pairs={{0,2},{1,3},{2,0},{3,1},{4,6},{5,7},{6,4},{7,5},{8,10},{9,11},{10,... | collective-permute-start | bytes 442376 | tf_op jit(solution)/shard_map/cond/branch_0_fun/ppermute | solution.py:22
  41.2 5.3 %collective-permute-start.2 = (f32[8,4608]{1,0:T(8,128)S(1)}, f32[8,4608]{1,0:T(8,128)S(1)}, u32[]{:S(2)}, u32[]{:S(2)}) collective-permute-start(f32[8,4608]{1,0:T(8,128)S(1)} %get-tuple-element.66), channel_id=1, source_target_pairs={{0,3},{1,0},{2,1},{3,2},{4,7},{5,4},{6,5},{7,6},{8,11},{9,8},{10,9... | collective-permute-start | bytes 442376 | tf_op jit(solution)/shard_map/cond/branch_0_fun/ppermute | solution.py:22
  47.2 3.7 %collective-permute-start.5 = (bf16[8,4608]{1,0:T(8,128)(2,1)S(1)}, bf16[8,4608]{1,0:T(8,128)(2,1)S(1)}, u32[]{:S(2)}, u32[]{:S(2)}) collective-permute-start(bf16[8,4608]{1,0:T(8,128)(2,1)S(1)} %branch_0_fun.4.refs_0_), channel_id=1, source_target_pairs={{0,3},{1,0},{2,1},{3,2},{4,7},{5,4},{6,5},{7,6},{8,11},{9,8},{10,9... | collective-permute-start | bytes 221192 | tf_op jit(solution)/shard_map/cond/branch_0_fun/ppermute | solution.py:22
  49.5 4.8 %collective-permute-start.4 = (bf16[8,4608]{1,0:T(8,128)(2,1)S(1)}, bf16[8,4608]{1,0:T(8,128)(2,1)S(1)}, u32[]{:S(2)}, u32[]{:S(2)}) collective-permute-start(bf16[8,4608]{1,0:T(8,128)(2,1)S(1)} %branch_0_fun.4.refs_0_), channel_id=1, source_target_pairs={{0,2},{1,3},{2,0},{3,1},{4,6},{5,7},{6,4},{7,5},{8,10},{9,11},{10,... | collective-permute-start | bytes 221192 | tf_op jit(solution)/shard_map/cond/branch_0_fun/ppermute | solution.py:22
  49.6 5.2 %collective-permute-start.3 = (bf16[8,4608]{1,0:T(8,128)(2,1)S(1)}, bf16[8,4608]{1,0:T(8,128)(2,1)S(1)}, u32[]{:S(2)}, u32[]{:S(2)}) collective-permute-start(bf16[8,4608]{1,0:T(8,128)(2,1)S(1)} %branch_0_fun.4.refs_0_), channel_id=1, source_target_pairs={{0,1},{1,2},{2,3},{3,0},{4,5},{5,6},{6,7},{7,4},{8,9},{9,10},{10,1... | collective-permute-start | bytes 221192 | tf_op jit(solution)/shard_map/cond/branch_0_fun/ppermute | solution.py:22
  56.1 2.7 %collective-permute-start.30 = (bf16[4,2048]{1,0:T(4,128)(2,1)S(1)}, bf16[4,2048]{1,0:T(4,128)(2,1)S(1)}, u32[]{:S(2)}, u32[]{:S(2)}) collective-permute-start(bf16[4,2048]{1,0:T(4,128)(2,1)S(1)} %get-tuple-element.110.refs_0_), channel_id=1, source_target_pairs={{0,3},{1,0},{2,1},{3,2},{4,7},{5,4},{6,5},{7,6},{8,11},{9,8},{10,9... | collective-permute-start | bytes 49160 | tf_op jit(solution)/shard_map/ppermute | solution.py:22
  56.6 4.1 %collective-permute-start.29 = (bf16[4,2048]{1,0:T(4,128)(2,1)S(1)}, bf16[4,2048]{1,0:T(4,128)(2,1)S(1)}, u32[]{:S(2)}, u32[]{:S(2)}) collective-permute-start(bf16[4,2048]{1,0:T(4,128)(2,1)S(1)} %get-tuple-element.110.refs_0_), channel_id=1, source_target_pairs={{0,2},{1,3},{2,0},{3,1},{4,6},{5,7},{6,4},{7,5},{8,10},{9,11},{10,... | collective-permute-start | bytes 49160 | tf_op jit(solution)/shard_map/ppermute | solution.py:22
  57.4 3.8 %collective-permute-start.28 = (bf16[4,2048]{1,0:T(4,128)(2,1)S(1)}, bf16[4,2048]{1,0:T(4,128)(2,1)S(1)}, u32[]{:S(2)}, u32[]{:S(2)}) collective-permute-start(bf16[4,2048]{1,0:T(4,128)(2,1)S(1)} %get-tuple-element.110.refs_0_), channel_id=1, source_target_pairs={{0,1},{1,2},{2,3},{3,0},{4,5},{5,6},{6,7},{7,4},{8,9},{9,10},{10,1... | collective-permute-start | bytes 49160 | tf_op jit(solution)/shard_map/ppermute | solution.py:22

commit v6 on v5

--- a/solution.py
+++ b/solution.py
@@ -23,16 +23,20 @@
 
 
 def from_ranks(arrays):
-    count = lax.axis_size("rank")
-    return [
-        shifted(a, "rank", [list(range(count))], k) for k, a in enumerate(arrays, start=1)
-    ]
+    ring = [list(range(lax.axis_size("rank")))]
+    return [shifted(a, "rank", ring, k) for k, a in enumerate(arrays, start=1)]
+
+
+def placed_as(order, arrays):
+    return [arrays[k] for k in order]
 
 
 F32, BF16 = jnp.float32, jnp.bfloat16
 BLOCK = 512
+FIRST_FAR, LAST_FAR = (0, 2, 1, 3), (0, 3, 1, 2)
 SIZES = (9216, 10240, 12288)
 SMALL = pltpu.CompilerParams(vmem_limit_bytes=8 << 20)
+SCORES = pltpu.CompilerParams(vmem_limit_bytes=16 << 20)
 
 
 def vmem():
@@ -172,11 +176,22 @@
     blocks, half = packed // BLOCK, packed // BLOCK // 2
 
     def body(lat_ref, rope_ref, len_ref, cache_hbm, keys_hbm, *rest):
-        outs, (bounds_ref, cache_ref, keys_ref, sems) = rest[:ranks], rest[ranks:]
+        outs, (bounds_ref, packed_ref, cache_ref, keys_ref, sems) = rest[:ranks], rest[ranks:]
+        copies = [pltpu.make_async_copy(keys_hbm, keys_ref, sems.at[seqs])]
+        for s in range(seqs):
+            copies.append(pltpu.make_async_copy(cache_hbm.at[s], cache_ref.at[s], sems.at[s]))
+        for copy in copies:
+            copy.start()
         starts = [jnp.int32(0)]
         for s in range(seqs):
             starts.append(starts[-1] + (len_ref[s] + BLOCK - 1) // BLOCK)
-        copies = []
+        for s in range(seqs):
+            first = starts[s] * BLOCK
+            bounds_ref[s : s + 1, :] = jnp.full((1, 128), first, jnp.int32)
+            bounds_ref[8 + s : 9 + s, :] = jnp.full((1, 128), first + len_ref[s], jnp.int32)
+        lat, rope = lat_ref[...], rope_ref[:, :rope_part]
+        for copy in copies:
+            copy.wait()
         for b in range(blocks):
             slot = jnp.int32(0)
             start = jnp.int32(0)
@@ -185,28 +200,12 @@
                 start = jnp.where(b >= starts[s], starts[s], start)
             block = jnp.minimum(b - start, capacity // BLOCK - 1)
             source = pl.ds(pl.multiple_of(block * BLOCK, BLOCK), BLOCK)
-            at = pl.ds(b * BLOCK, BLOCK)
-            copies += [
-                pltpu.make_async_copy(cache_hbm.at[slot, source], cache_ref.at[at], sems.at[0, b]),
-                pltpu.make_async_copy(
-                    keys_hbm.at[slot, :, source], keys_ref.at[:, at], sems.at[1, b]
-                ),
-            ]
-            copies[-2].start()
-            copies[-1].start()
-        for s in range(seqs):
-            first = starts[s] * BLOCK
-            bounds_ref[s : s + 1, :] = jnp.full((1, 128), first, jnp.int32)
-            bounds_ref[8 + s : 9 + s, :] = jnp.full((1, 128), first + len_ref[s], jnp.int32)
-        lat, rope = lat_ref[...], rope_ref[:, :rope_part]
-        for b in range(blocks):
-            copies[2 * b].wait()
-            copies[2 * b + 1].wait()
-            at = pl.ds(b * BLOCK, BLOCK)
+            rows = cache_ref[slot, source, :]
+            packed_ref[b * BLOCK : (b + 1) * BLOCK, :] = rows
             every = lax.dot_general(
-                lat, cache_ref[at, :], (((1,), (1,)), ((), ())), preferred_element_type=F32
+                lat, rows, (((1,), (1,)), ((), ())), preferred_element_type=F32
             )
-            every = every + dot(rope, keys_ref[:, at])
+            every = every + dot(rope, keys_ref[slot, :, source])
             part = every[:heads]
             for s in range(1, seqs):
                 part = jnp.where(b >= starts[s], every[s * heads : (s + 1) * heads], part)
@@ -224,10 +223,11 @@
         ],
         in_specs=[vmem(), vmem(), smem(), hbm(), hbm()],
         out_specs=[vmem()] * (ranks + 2),
-        compiler_params=SMALL,
+        compiler_params=SCORES,
         scratch_shapes=[
-            pltpu.VMEM((rope_part, packed), BF16),
-            pltpu.SemaphoreType.DMA((2, blocks)),
+            pltpu.VMEM(latent_cache.shape, BF16),
+            pltpu.VMEM(rope_keys.shape, BF16),
+            pltpu.SemaphoreType.DMA((seqs + 1,)),
         ],
     )(query_lat, query_rope, lengths, latent_cache, rope_keys)
 
@@ -271,7 +271,7 @@
     blocks, half = packed // BLOCK, packed // BLOCK // 2
 
     def body(*refs):
-        weight_refs = refs[:ranks]
+        weight_refs = [refs[LAST_FAR.index(k)] for k in range(ranks)]
         bounds_ref, cache_ref, w_ref, out_ref, lat_rows = refs[ranks:]
         rank = lax.axis_index("rank")
         total = jnp.zeros((seqs * heads, lat_part), F32)
@@ -305,7 +305,7 @@
         out_specs=vmem(),
         compiler_params=SMALL,
         scratch_shapes=[pltpu.VMEM((seqs * heads, lat_part), F32)],
-    )(*weights, bounds, cache, w_uv)
+    )(*placed_as(LAST_FAR, weights), bounds, cache, w_uv)
 
 
 def project(parts, w_out, copies):
@@ -396,7 +396,8 @@
             own, *others, bounds, held = partial_scores(
                 query_lat, query_rope, lengths, latent_cache, rope_keys, packed, scale
             )
-            weights = softmax([own] + from_ranks(others), bounds, seqs)
+            parts = placed_as(FIRST_FAR, [own] + from_ranks(others))
+            weights = softmax(parts, bounds, seqs)
             gathered = [weights] + from_ranks([weights] * (ranks - 1))
             return head_part(gathered, bounds, held, w_uv, packed, seqs)
 
@@ -413,7 +414,7 @@
         w_uv,
     )
     parts = [value_part] + from_ranks([value_part] * (ranks - 1))
-    copies = project(parts, w_out, lax.axis_size("dp"))
+    copies = project(placed_as(LAST_FAR, parts), w_out, lax.axis_size("dp"))
     everyone = lax.all_to_all(copies, "dp", 0, 0, tiled=True)
     return bring_back(everyone, targets)
 

time: 88.4 us -> 85.7 us (0.969)
  waiting for transfers between devices: 20.8 us -> 18.4 us
  starting transfers between devices: 25.3 us -> 27.3 us
    ppermute x13, waiting for transfers between devices: 12.4 us -> 9.99 us  [shifted(): return lax.ppermute(array, axis, pairs)]
    ppermute x13, starting transfers between devices: 17.1 us -> 19.1 us  [shifted(): return lax.ppermute(array, axis, pairs)]
  transfers between devices with their start and end apart: 14 -> 14, of which waited for: 13 -> 11; matrix products, arithmetic and copies ran while one was open for 3% -> 4% of each run, Pallas kernels for 0% -> 0%
where the time goes in v6:
time: 85.7 us; the launch traced here: 85.5 us
  starting transfers between devices  27.3 us (32%)
  blocking collectives  24.1 us (28%)
  waiting for transfers between devices  18.4 us (21%)
  Pallas kernels  8.85 us (10%)
  local copies, waits for them, and re-layouts  3.31 us (4%)
  other arithmetic  2.24 us (3%)
    all_to_all x1, blocking collectives, per_device(): everyone = lax.all_to_all(copies, 'dp', 0, 0, tiled=True)  24.1 us
    ppermute x13, starting transfers between devices, shifted(): return lax.ppermute(array, axis, pairs)  19.1 us
    ppermute x13, waiting for transfers between devices, shifted(): return lax.ppermute(array, axis, pairs)  9.99 us
    all_to_all x1, waiting for transfers between devices, per_device(): lax.all_to_all(picked, 'dp', 0, 0, axis_index_groups=z_groups, tiled=True)  8.38 us
    all_to_all x1, starting transfers between devices, per_device(): lax.all_to_all(picked, 'dp', 0, 0, axis_index_groups=z_groups, tiled=True)  8.19 us
    pallas_call x1, Pallas kernels, partial_scores(): pl.pallas_call(body, out_shape=[jax.ShapeDtypeStruct((2 * group, packed /...  4.6 us
    unnamed x8, local copies, waits for them, and re-layouts  2.46 us
  transfers between devices with their start and end apart: 14, of which 11 were waited for; matrix products, arithmetic and copies ran while one was open for 4% of the time, Pallas kernels for 0%

profile of v6, /device:TPU:1, one launch (start us, length us, event | category | flops | bytes accessed | tf_op | source)
XLA Modules:
  0.0 85.5 jit_solution(7500466449031143522)
XLA Ops:
  0.0 0.7 copy-done.2
  0.7 0.7 copy-done.3
  1.5 3.4 %collective-permute-start.26 = (bf16[4,3072]{1,0:T(4,128)(2,1)S(1)}, bf16[4,3072]{1,0:T(4,128)(2,1)S(1)}, u32[]{:S(2)}, u32[]{:S(2)}) collective-permute-start(bf16[4,3072]{1,0:T(4,128)(2,1)S(1)} %shard_map.91), channel_id=1, source_target_pairs={{0,24},{8,0},{16,8},{24,16},{4,28},{12,4},{20,12},{28,20},{32,56},... | collective-permute-start | bytes 73736 | tf_op jit(solution)/shard_map/ppermute | solution.py:22
  4.8 0.5 collective-permute-start.25
  5.3 0.6 collective-permute-start.24
  6.0 1.3 %fusion.10 = s32[]{:T(128)} fusion(s32[4]{0:T(128)} %param.17), kind=kLoop, calls=%fused_computation.35 | loop fusion | flops 67 | bytes 20 | tf_op jit(solution)/shard_map/reduce_sum | solution.py:382
  7.3 0.8 dynamic-slice_bitcast_fusion
  8.7 0.1 copy.12.rest_0_.target_ref
  8.8 0.0 collective-permute-done.26
  8.8 0.2 collective-permute-done.25
  9.0 0.3 collective-permute-done.24
  9.3 0.1 pad_maximum_fusion.near_ref
  9.3 2.4 %collective-permute-start.27 = (bf16[16,3072]{1,0:T(8,128)(2,1)S(1)}, bf16[16,3072]{1,0:T(8,128)(2,1)S(1)}, u32[]{:S(2)}, u32[]{:S(2)}) collective-permute-start(bf16[16,3072]{1,0:T(8,128)(2,1)S(1)} %pad_maximum_fusion.near_ref), channel_id=1, source_target_pairs={{0,4},{4,0},{8,12},{12,8},{16,20},{20,16},{24,28},{28,24},{32,36},... | collective-permute-start | bytes 294920 | tf_op jit(solution)/shard_map/ppermute | solution.py:22
  11.8 0.9 %select_reduce_fusion = s32[32]{0:T(128)S(1)} fusion(s32[256]{0:T(256)} %param.18, s32[32]{0:T(128)S(1)} %fusion), kind=kLoop, calls=%fused_computation.1 | loop fusion | flops 24544 | bytes 1280 | tf_op jit(solution)/shard_map/reduce_sum | solution.py:372
  12.6 0.1 collective-permute-done.27.far_ref
  12.7 1.0 %shard_map.92._ = bf16[8,4,3072]{2,1,0:T(4,128)(2,1)} custom-call(bf16[16,3072]{1,0:T(8,128)(2,1)S(1)} %pad_maximum_fusion.near_ref, bf16[16,3072]{1,0:T(8,128)(2,1)S(1)} %collective-permute-done.27.far_ref, s32[1,32]{1,0:T(1,128)S(1)} %bitcast.4, s32[4,1]{1,0:T(4,128)S(1)} %copy.12.rest_0_.target_ref, s32[1,1]{1,0:T(1,128)} %bitcast.2.rest_1_), custom_call_target="tpu_custom_call" | custom-call | tf_op jit(solution)/shard_map/pallas_call | solution.py:100
  13.7 8.2 %all-to-all-start = ((bf16[8,4,3072]{2,1,0:T(4,128)(2,1)}), bf16[8,4,3072]{2,1,0:T(4,128)(2,1)S(1)}, u32[]{:S(2)}, u32[]{:S(2)}) async-start(bf16[8,4,3072]{2,1,0:T(4,128)(2,1)} %shard_map.92._), calls=%async_computation | async-start | bytes 393216 | tf_op jit(solution)/shard_map/all_to_all | solution.py:390
  21.9 1.0 %copy-done.1 = bf16[16,128,128]{2,1,0:T(8,128)(2,1)S(1)} copy-done((bf16[16,128,128]{2,1,0:T(8,128)(2,1)S(1)}, bf16[16,128,128]{2,1,0:T(8,128)(2,1)}, u32[]{:S(2)}) %copy-start.1) | copy-done | bytes 524312
  23.0 8.4 %all-to-all-done.arrived_ref = bf16[8,4,3072]{2,1,0:T(4,128)(2,1)S(1)} async-done(((bf16[8,4,3072]{2,1,0:T(4,128)(2,1)}), bf16[8,4,3072]{2,1,0:T(4,128)(2,1)S(1)}, u32[]{:S(2)}, u32[]{:S(2)}) %all-to-all-start) | async-done | bytes 196640 | tf_op jit(solution)/shard_map/all_to_all | solution.py:390
  31.4 0.4 shard_map.94
  31.8 23.5 %conditional.1 = (bf16[4,2048]{1,0:T(4,128)(2,1)S(1)}) conditional(s32[]{:T(128)} %clamp.3, (bf16[64,128]{1,0:T(8,128)(2,1)S(1)}, bf16[64,128]{1,0:T(8,128)(2,1)S(1)}, s32[4]{0:T(128)}, bf16[4,4096,128]{2,1,0:T(8,128)(2,1)}, bf16[4,16,4096]{2,1,0:T(8,128)(2,1)}, /*index=5*/bf16[16,128,128]{2,1,0:T(8,128)(2,1)}) %tuple.17, ...), branch_computations={%region_2.3_spmd, %region_3.4_spmd, %region_4.5_spmd, %region_5.6_... | conditional | bytes 6816020 | solution.py:406
  31.8 0.0 copy-start.4
  31.8 4.6 %branch_0_fun.3 = (f32[8,4608]{1,0:T(8,128)S(1)}, f32[8,4608]{1,0:T(8,128)S(1)}, f32[8,4608]{1,0:T(8,128)S(1)}, f32[8,4608]{1,0:T(8,128)S(1)}, s32[16,128]{1,0:T(8,128)S(1)}, /*index=5*/bf16[9216,128]{1,0:T(8,128)(2,1)S(1)}) custom-call(bf16[64,128]{1,0:T(8,128)(2,1)S(1)} %get-tuple-element.56.lat_ref, bf16[64,128]{1,0:T(8,128)(2,1)S(1)} %get-tuple-element.58.rope_ref, ...), custom_call_target="tpu_custom_call" | custom-call | tf_op jit(solution)/shard_map/cond/branch_0_fun/pallas_call | solution.py:217
  36.4 3.0 %collective-permute-start = (f32[8,4608]{1,0:T(8,128)S(1)}, f32[8,4608]{1,0:T(8,128)S(1)}, u32[]{:S(2)}, u32[]{:S(2)}) collective-permute-start(f32[8,4608]{1,0:T(8,128)S(1)} %get-tuple-element.64), channel_id=1, source_target_pairs={{0,2},{1,3},{2,0},{3,1},{4,6},{5,7},{6,4},{7,5},{8,10},{9,11},{10,... | collective-permute-start | bytes 442376 | tf_op jit(solution)/shard_map/cond/branch_0_fun/ppermute | solution.py:22
  39.4 0.4 collective-permute-start.1
  39.8 2.3 %collective-permute-start.2 = (f32[8,4608]{1,0:T(8,128)S(1)}, f32[8,4608]{1,0:T(8,128)S(1)}, u32[]{:S(2)}, u32[]{:S(2)}) collective-permute-start(f32[8,4608]{1,0:T(8,128)S(1)} %get-tuple-element.66), channel_id=1, source_target_pairs={{0,3},{1,0},{2,1},{3,2},{4,7},{5,4},{6,5},{7,6},{8,11},{9,8},{10,9... | collective-permute-start | bytes 442376 | tf_op jit(solution)/shard_map/cond/branch_0_fun/ppermute | solution.py:22
  42.1 0.0 collective-permute-done.refs_1_
  42.1 4.6 %collective-permute-done.1.refs_2_ = f32[8,4608]{1,0:T(8,128)S(1)} collective-permute-done((f32[8,4608]{1,0:T(8,128)S(1)}, f32[8,4608]{1,0:T(8,128)S(1)}, u32[]{:S(2)}, u32[]{:S(2)}) %collective-permute-start.1) | collective-permute-done | bytes 147488 | tf_op jit(solution)/shard_map/cond/branch_0_fun/ppermute | solution.py:22
  46.7 0.0 collective-permute-done.2.refs_3_
  46.7 0.7 branch_0_fun.4.refs_0_
  47.4 0.7 collective-permute-start.5
  48.1 2.5 %collective-permute-start.4 = (bf16[8,4608]{1,0:T(8,128)(2,1)S(1)}, bf16[8,4608]{1,0:T(8,128)(2,1)S(1)}, u32[]{:S(2)}, u32[]{:S(2)}) collective-permute-start(bf16[8,4608]{1,0:T(8,128)(2,1)S(1)} %branch_0_fun.4.refs_0_), channel_id=1, source_target_pairs={{0,1},{1,2},{2,3},{3,0},{4,5},{5,6},{6,7},{7,4},{8,9},{9,10},{10,1... | collective-permute-start | bytes 221192 | tf_op jit(solution)/shard_map/cond/branch_0_fun/ppermute | solution.py:22
  50.6 0.2 collective-permute-start.3
  50.8 1.5 %collective-permute-done.5.refs_3_ = bf16[8,4608]{1,0:T(8,128)(2,1)S(1)} collective-permute-done((bf16[8,4608]{1,0:T(8,128)(2,1)S(1)}, bf16[8,4608]{1,0:T(8,128)(2,1)S(1)}, u32[]{:S(2)}, u32[]{:S(2)}) %collective-permute-start.5) | collective-permute-done | bytes 73760 | tf_op jit(solution)/shard_map/cond/branch_0_fun/ppermute | solution.py:22
  52.3 0.7 collective-permute-done.4.refs_2_
  53.0 1.1 %collective-permute-done.3.refs_1_ = bf16[8,4608]{1,0:T(8,128)(2,1)S(1)} collective-permute-done((bf16[8,4608]{1,0:T(8,128)(2,1)S(1)}, bf16[8,4608]{1,0:T(8,128)(2,1)S(1)}, u32[]{:S(2)}, u32[]{:S(2)}) %collective-permute-start.3) | collective-permute-done | bytes 73760 | tf_op jit(solution)/shard_map/cond/branch_0_fun/ppermute | solution.py:22
  54.1 0.0 copy-done.4
  54.1 0.8 branch_0_fun.5
  55.4 0.5 collective-permute-start.30
  55.9 1.6 %collective-permute-start.29 = (bf16[4,2048]{1,0:T(4,128)(2,1)S(1)}, bf16[4,2048]{1,0:T(4,128)(2,1)S(1)}, u32[]{:S(2)}, u32[]{:S(2)}) collective-permute-start(bf16[4,2048]{1,0:T(4,128)(2,1)S(1)} %get-tuple-element.110.refs_0_), channel_id=1, source_target_pairs={{0,1},{1,2},{2,3},{3,0},{4,5},{5,6},{6,7},{7,4},{8,9},{9,10},{10,1... | collective-permute-start | bytes 49160 | tf_op jit(solution)/shard_map/ppermute | solution.py:22
  57.5 1.1 %collective-permute-start.28 = (bf16[4,2048]{1,0:T(4,128)(2,1)S(1)}, bf16[4,2048]{1,0:T(4,128)(2,1)S(1)}, u32[]{:S(2)}, u32[]{:S(2)}) collective-permute-start(bf16[4,2048]{1,0:T(4,128)(2,1)S(1)} %get-tuple-element.110.refs_0_), channel_id=1, source_target_pairs={{0,3},{1,0},{2,1},{3,2},{4,7},{5,4},{6,5},{7,6},{8,11},{9,8},{10,9... | collective-permute-start | bytes 49160 | tf_op jit(solution)/shard_map/ppermute | solution.py:22
  58.5 1.0 %collective-permute-done.30.refs_3_ = bf16[4,2048]{1,0:T(4,128)(2,1)S(1)} collective-permute-done((bf16[4,2048]{1,0:T(4,128)(2,1)S(1)}, bf16[4,2048]{1,0:T(4,128)(2,1)S(1)}, u32[]{:S(2)}, u32[]{:S(2)}) %collective-permute-start.30) | collective-permute-done | bytes 16416 | tf_op jit(solution)/shard_map/ppermute | solution.py:22
  59.5 0.2 collective-permute-done.29.refs_2_
  59.7 0.3 collective-permute-done.28.refs_1_
  60.0 0.0 copy-done
  60.0 0.4 shard_map.95
  60.5 24.1 %all_to_all.10.all_ref = bf16[64,4,512]{2,1,0:T(4,128)(2,1)S(1)} all-to-all(bf16[64,4,512]{2,1,0:T(4,128)(2,1)S(1)} %shard_map.95), channel_id=1, replica_groups=mesh['dp'=64,'rank'=4] {'dp'}, dimensions={0} | all-to-all | bytes 524288 | tf_op jit(solution)/shard_map/all_to_all | solution.py:418
  84.6 0.9 %shard_map.96 = bf16[4,512]{1,0:T(4,128)(2,1)} custom-call(bf16[64,4,512]{2,1,0:T(4,128)(2,1)S(1)} %all_to_all.10.all_ref, s32[4,1]{1,0:T(4,128)S(1)} %copy.12.rest_0_.target_ref), custom_call_target="tpu_custom_call" | custom-call | tf_op jit(solution)/shard_map/pallas_call | solution.py:349
  (7 shorter events, 0.1 us)
Async XLA Ops:
  0.0 0.7 copy-start.2
  0.7 0.7 copy-start.3
  1.5 7.3 %collective-permute-start.26 = (bf16[4,3072]{1,0:T(4,128)(2,1)S(1)}, bf16[4,3072]{1,0:T(4,128)(2,1)S(1)}, u32[]{:S(2)}, u32[]{:S(2)}) collective-permute-start(bf16[4,3072]{1,0:T(4,128)(2,1)S(1)} %shard_map.91), channel_id=1, source_target_pairs={{0,24},{8,0},{16,8},{24,16},{4,28},{12,4},{20,12},{28,20},{32,56},... | collective-permute-start | bytes 73736 | tf_op jit(solution)/shard_map/ppermute | solution.py:22
  4.8 4.2 %collective-permute-start.25 = (bf16[4,3072]{1,0:T(4,128)(2,1)S(1)}, bf16[4,3072]{1,0:T(4,128)(2,1)S(1)}, u32[]{:S(2)}, u32[]{:S(2)}) collective-permute-start(bf16[4,3072]{1,0:T(4,128)(2,1)S(1)} %shard_map.91), channel_id=1, source_target_pairs={{0,16},{8,24},{16,0},{24,8},{4,20},{12,28},{20,4},{28,12},{32,48},... | collective-permute-start | bytes 73736 | tf_op jit(solution)/shard_map/ppermute | solution.py:22
  5.3 3.9 %collective-permute-start.24 = (bf16[4,3072]{1,0:T(4,128)(2,1)S(1)}, bf16[4,3072]{1,0:T(4,128)(2,1)S(1)}, u32[]{:S(2)}, u32[]{:S(2)}) collective-permute-start(bf16[4,3072]{1,0:T(4,128)(2,1)S(1)} %shard_map.91), channel_id=1, source_target_pairs={{0,8},{8,16},{16,24},{24,0},{4,12},{12,20},{20,28},{28,4},{32,40},... | collective-permute-start | bytes 73736 | tf_op jit(solution)/shard_map/ppermute | solution.py:22
  9.3 3.4 %collective-permute-start.27 = (bf16[16,3072]{1,0:T(8,128)(2,1)S(1)}, bf16[16,3072]{1,0:T(8,128)(2,1)S(1)}, u32[]{:S(2)}, u32[]{:S(2)}) collective-permute-start(bf16[16,3072]{1,0:T(8,128)(2,1)S(1)} %pad_maximum_fusion.near_ref), channel_id=1, source_target_pairs={{0,4},{4,0},{8,12},{12,8},{16,20},{20,16},{24,28},{28,24},{32,36},... | collective-permute-start | bytes 294920 | tf_op jit(solution)/shard_map/ppermute | solution.py:22
  13.7 17.7 %all-to-all-start = ((bf16[8,4,3072]{2,1,0:T(4,128)(2,1)}), bf16[8,4,3072]{2,1,0:T(4,128)(2,1)S(1)}, u32[]{:S(2)}, u32[]{:S(2)}) async-start(bf16[8,4,3072]{2,1,0:T(4,128)(2,1)} %shard_map.92._), calls=%async_computation | async-start | bytes 393216 | tf_op jit(solution)/shard_map/all_to_all | solution.py:390
  21.9 1.0 %copy-start.1 = (bf16[16,128,128]{2,1,0:T(8,128)(2,1)S(1)}, bf16[16,128,128]{2,1,0:T(8,128)(2,1)}, u32[]{:S(2)}) copy-start(bf16[16,128,128]{2,1,0:T(8,128)(2,1)} %array_ref.1) | copy-start | bytes 1572868
  31.8 28.2 %copy-start = (bf16[2048,512]{1,0:T(8,128)(2,1)S(1)}, bf16[2048,512]{1,0:T(8,128)(2,1)}, u32[]{:S(2)}) copy-start(bf16[2048,512]{1,0:T(8,128)(2,1)} %refs_4_.1) | copy-start | bytes 6291460
  31.8 22.3 %copy-start.4 = (bf16[16,128,128]{2,1,0:T(8,128)(2,1)S(1)}, bf16[16,128,128]{2,1,0:T(8,128)(2,1)}, u32[]{:S(2)}) copy-start(bf16[16,128,128]{2,1,0:T(8,128)(2,1)} %get-tuple-element.69.refs_6_) | copy-start | bytes 1572868 | tf_op jit(solution)/shard_map/cond
  36.4 5.7 %collective-permute-start = (f32[8,4608]{1,0:T(8,128)S(1)}, f32[8,4608]{1,0:T(8,128)S(1)}, u32[]{:S(2)}, u32[]{:S(2)}) collective-permute-start(f32[8,4608]{1,0:T(8,128)S(1)} %get-tuple-element.64), channel_id=1, source_target_pairs={{0,2},{1,3},{2,0},{3,1},{4,6},{5,7},{6,4},{7,5},{8,10},{9,11},{10,... | collective-permute-start | bytes 442376 | tf_op jit(solution)/shard_map/cond/branch_0_fun/ppermute | solution.py:22
  39.4 7.3 %collective-permute-start.1 = (f32[8,4608]{1,0:T(8,128)S(1)}, f32[8,4608]{1,0:T(8,128)S(1)}, u32[]{:S(2)}, u32[]{:S(2)}) collective-permute-start(f32[8,4608]{1,0:T(8,128)S(1)} %get-tuple-element.65), channel_id=1, source_target_pairs={{0,1},{1,2},{2,3},{3,0},{4,5},{5,6},{6,7},{7,4},{8,9},{9,10},{10,1... | collective-permute-start | bytes 442376 | tf_op jit(solution)/shard_map/cond/branch_0_fun/ppermute | solution.py:22
  39.8 6.9 %collective-permute-start.2 = (f32[8,4608]{1,0:T(8,128)S(1)}, f32[8,4608]{1,0:T(8,128)S(1)}, u32[]{:S(2)}, u32[]{:S(2)}) collective-permute-start(f32[8,4608]{1,0:T(8,128)S(1)} %get-tuple-element.66), channel_id=1, source_target_pairs={{0,3},{1,0},{2,1},{3,2},{4,7},{5,4},{6,5},{7,6},{8,11},{9,8},{10,9... | collective-permute-start | bytes 442376 | tf_op jit(solution)/shard_map/cond/branch_0_fun/ppermute | solution.py:22
  47.4 4.8 %collective-permute-start.5 = (bf16[8,4608]{1,0:T(8,128)(2,1)S(1)}, bf16[8,4608]{1,0:T(8,128)(2,1)S(1)}, u32[]{:S(2)}, u32[]{:S(2)}) collective-permute-start(bf16[8,4608]{1,0:T(8,128)(2,1)S(1)} %branch_0_fun.4.refs_0_), channel_id=1, source_target_pairs={{0,2},{1,3},{2,0},{3,1},{4,6},{5,7},{6,4},{7,5},{8,10},{9,11},{10,... | collective-permute-start | bytes 221192 | tf_op jit(solution)/shard_map/cond/branch_0_fun/ppermute | solution.py:22
  48.1 4.9 %collective-permute-start.4 = (bf16[8,4608]{1,0:T(8,128)(2,1)S(1)}, bf16[8,4608]{1,0:T(8,128)(2,1)S(1)}, u32[]{:S(2)}, u32[]{:S(2)}) collective-permute-start(bf16[8,4608]{1,0:T(8,128)(2,1)S(1)} %branch_0_fun.4.refs_0_), channel_id=1, source_target_pairs={{0,1},{1,2},{2,3},{3,0},{4,5},{5,6},{6,7},{7,4},{8,9},{9,10},{10,1... | collective-permute-start | bytes 221192 | tf_op jit(solution)/shard_map/cond/branch_0_fun/ppermute | solution.py:22
  50.6 3.5 %collective-permute-start.3 = (bf16[8,4608]{1,0:T(8,128)(2,1)S(1)}, bf16[8,4608]{1,0:T(8,128)(2,1)S(1)}, u32[]{:S(2)}, u32[]{:S(2)}) collective-permute-start(bf16[8,4608]{1,0:T(8,128)(2,1)S(1)} %branch_0_fun.4.refs_0_), channel_id=1, source_target_pairs={{0,3},{1,0},{2,1},{3,2},{4,7},{5,4},{6,5},{7,6},{8,11},{9,8},{10,9... | collective-permute-start | bytes 221192 | tf_op jit(solution)/shard_map/cond/branch_0_fun/ppermute | solution.py:22
  55.4 4.2 %collective-permute-start.30 = (bf16[4,2048]{1,0:T(4,128)(2,1)S(1)}, bf16[4,2048]{1,0:T(4,128)(2,1)S(1)}, u32[]{:S(2)}, u32[]{:S(2)}) collective-permute-start(bf16[4,2048]{1,0:T(4,128)(2,1)S(1)} %get-tuple-element.110.refs_0_), channel_id=1, source_target_pairs={{0,2},{1,3},{2,0},{3,1},{4,6},{5,7},{6,4},{7,5},{8,10},{9,11},{10,... | collective-permute-start | bytes 49160 | tf_op jit(solution)/shard_map/ppermute | solution.py:22
  55.9 3.9 %collective-permute-start.29 = (bf16[4,2048]{1,0:T(4,128)(2,1)S(1)}, bf16[4,2048]{1,0:T(4,128)(2,1)S(1)}, u32[]{:S(2)}, u32[]{:S(2)}) collective-permute-start(bf16[4,2048]{1,0:T(4,128)(2,1)S(1)} %get-tuple-element.110.refs_0_), channel_id=1, source_target_pairs={{0,1},{1,2},{2,3},{3,0},{4,5},{5,6},{6,7},{7,4},{8,9},{9,10},{10,1... | collective-permute-start | bytes 49160 | tf_op jit(solution)/shard_map/ppermute | solution.py:22
  57.5 2.6 %collective-permute-start.28 = (bf16[4,2048]{1,0:T(4,128)(2,1)S(1)}, bf16[4,2048]{1,0:T(4,128)(2,1)S(1)}, u32[]{:S(2)}, u32[]{:S(2)}) collective-permute-start(bf16[4,2048]{1,0:T(4,128)(2,1)S(1)} %get-tuple-element.110.refs_0_), channel_id=1, source_target_pairs={{0,3},{1,0},{2,1},{3,2},{4,7},{5,4},{6,5},{7,6},{8,11},{9,8},{10,9... | collective-permute-start | bytes 49160 | tf_op jit(solution)/shard_map/ppermute | solution.py:22

commit v7 on v6

--- a/solution.py
+++ b/solution.py
@@ -41,10 +41,6 @@
 
 def vmem():
     return pl.BlockSpec(memory_space=pltpu.VMEM)
-
-
-def smem():
-    return pl.BlockSpec(memory_space=pltpu.SMEM)
 
 
 def hbm():
@@ -175,13 +171,17 @@
     group = heads // ranks
     blocks, half = packed // BLOCK, packed // BLOCK // 2
 
-    def body(lat_ref, rope_ref, len_ref, cache_hbm, keys_hbm, *rest):
-        outs, (bounds_ref, packed_ref, cache_ref, keys_ref, sems) = rest[:ranks], rest[ranks:]
+    def body(lat_ref, rope_ref, len_hbm, cache_hbm, keys_hbm, *rest):
+        outs, rest = rest[:ranks], rest[ranks:]
+        bounds_ref, packed_ref, cache_ref, keys_ref, len_ref, sems = rest
         copies = [pltpu.make_async_copy(keys_hbm, keys_ref, sems.at[seqs])]
         for s in range(seqs):
             copies.append(pltpu.make_async_copy(cache_hbm.at[s], cache_ref.at[s], sems.at[s]))
         for copy in copies:
             copy.start()
+        lengths_copy = pltpu.make_async_copy(len_hbm, len_ref, sems.at[seqs + 1])
+        lengths_copy.start()
+        lengths_copy.wait()
         starts = [jnp.int32(0)]
         for s in range(seqs):
             starts.append(starts[-1] + (len_ref[s] + BLOCK - 1) // BLOCK)
@@ -221,13 +221,14 @@
             jax.ShapeDtypeStruct((16, 128), jnp.int32),
             jax.ShapeDtypeStruct((packed, lat_part), BF16),
         ],
-        in_specs=[vmem(), vmem(), smem(), hbm(), hbm()],
+        in_specs=[vmem()] * 2 + [hbm()] * 3,
         out_specs=[vmem()] * (ranks + 2),
         compiler_params=SCORES,
         scratch_shapes=[
             pltpu.VMEM(latent_cache.shape, BF16),
             pltpu.VMEM(rope_keys.shape, BF16),
-            pltpu.SemaphoreType.DMA((seqs + 1,)),
+            pltpu.SMEM((seqs,), jnp.int32),
+            pltpu.SemaphoreType.DMA((seqs + 2,)),
         ],
     )(query_lat, query_rope, lengths, latent_cache, rope_keys)
 
@@ -367,7 +368,9 @@
     plane_rows = 2 * NX * seqs
     at = jnp.arange(plane_rows, dtype=jnp.int32)
     from_c = (dp_pos % NC + at // (NX * seqs)) % NC
-    from_x = (dp_pos // NC % NX + NX - at // seqs % NX) % NX
+    place = at // seqs % NX
+    step = jnp.where(place == 0, 0, (place + 1) % (NX - 1) + 1)
+    from_x = (dp_pos // NC % NX + NX - step) % NX
     row_of = ((dp_pos // (NC * NX) * NX + from_x) * NC + from_c) * seqs + at % seqs
     slot_here = jnp.sum(
         jnp.where(
@@ -384,7 +387,7 @@
 
     rows = join(q_nope, q_rope)
     near = [rows] + [shifted(rows, "dp", x_groups, k) for k in range(1, NX)]
-    near = jnp.concatenate(near, axis=0)
+    near = jnp.concatenate(placed_as(LAST_FAR, near), axis=0)
     far = shifted(near, "dp", c_groups, 1)
     picked = pick_rows(near, far, slot_here, seqs, (targets, which.reshape(1, 1)))
     arrived = lax.all_to_all(picked, "dp", 0, 0, axis_index_groups=z_groups, tiled=True)

time: 85.7 us -> 86.1 us (level); the launches traced: 85.5 us -> 84.8 us
  starting transfers between devices: 27.3 us -> 28.3 us
    ppermute x13, starting transfers between devices: 19.1 us -> 20.1 us  [shifted(): return lax.ppermute(array, axis, pairs)]
  transfers between devices with their start and end apart: 14 -> 14, of which waited for: 11 -> 9; matrix products, arithmetic and copies ran while one was open for 4% -> 4% of each run, Pallas kernels for 0% -> 0%
where the time goes in v7:
time: 86.1 us; the launch traced here: 84.8 us
  starting transfers between devices  28.3 us (33%)
  blocking collectives  23.6 us (27%)
  waiting for transfers between devices  17.9 us (21%)
  Pallas kernels  8.25 us (10%)
  local copies, waits for them, and re-layouts  3.31 us (4%)
  other arithmetic  2.25 us (3%)
    all_to_all x1, blocking collectives, per_device(): everyone = lax.all_to_all(copies, 'dp', 0, 0, tiled=True)  23.6 us
    ppermute x13, starting transfers between devices, shifted(): return lax.ppermute(array, axis, pairs)  20.1 us
    ppermute x13, waiting for transfers between devices, shifted(): return lax.ppermute(array, axis, pairs)  9.54 us
    all_to_all x1, waiting for transfers between devices, per_device(): lax.all_to_all(picked, 'dp', 0, 0, axis_index_groups=z_groups, tiled=True)  8.38 us
    all_to_all x1, starting transfers between devices, per_device(): lax.all_to_all(picked, 'dp', 0, 0, axis_index_groups=z_groups, tiled=True)  8.19 us
    pallas_call x1, Pallas kernels, partial_scores(): pl.pallas_call(body, out_shape=[jax.ShapeDtypeStruct((2 * group, packed /...  3.99 us
    unnamed x8, local copies, waits for them, and re-layouts  2.46 us
  transfers between devices with their start and end apart: 14, of which 9 were waited for; matrix products, arithmetic and copies ran while one was open for 4% of the time, Pallas kernels for 0%

profile of v7, /device:TPU:1, one launch (start us, length us, event | category | flops | bytes accessed | tf_op | source)
XLA Modules:
  0.0 84.8 jit_solution(284676062606837279)
XLA Ops:
  0.0 0.7 copy-done.2
  0.7 0.7 copy-done.3
  1.5 3.6 %collective-permute-start.26 = (bf16[4,3072]{1,0:T(4,128)(2,1)S(1)}, bf16[4,3072]{1,0:T(4,128)(2,1)S(1)}, u32[]{:S(2)}, u32[]{:S(2)}) collective-permute-start(bf16[4,3072]{1,0:T(4,128)(2,1)S(1)} %shard_map.91), channel_id=1, source_target_pairs={{0,16},{8,24},{16,0},{24,8},{4,20},{12,28},{20,4},{28,12},{32,48},... | collective-permute-start | bytes 73736 | tf_op jit(solution)/shard_map/ppermute | solution.py:22
  5.1 0.3 collective-permute-start.25
  5.4 2.4 %collective-permute-start.24 = (bf16[4,3072]{1,0:T(4,128)(2,1)S(1)}, bf16[4,3072]{1,0:T(4,128)(2,1)S(1)}, u32[]{:S(2)}, u32[]{:S(2)}) collective-permute-start(bf16[4,3072]{1,0:T(4,128)(2,1)S(1)} %shard_map.91), channel_id=1, source_target_pairs={{0,24},{8,0},{16,8},{24,16},{4,28},{12,4},{20,12},{28,20},{32,56},... | collective-permute-start | bytes 73736 | tf_op jit(solution)/shard_map/ppermute | solution.py:22
  7.8 1.3 %fusion.11 = s32[]{:T(128)} fusion(s32[4]{0:T(128)} %param.17), kind=kLoop, calls=%fused_computation.38 | loop fusion | flops 67 | bytes 20 | tf_op jit(solution)/shard_map/reduce_sum | solution.py:385
  9.1 0.8 dynamic-slice_bitcast_fusion
  10.5 0.1 copy.12.rest_0_.target_ref
  10.6 0.0 collective-permute-done.26
  10.6 0.0 collective-permute-done.25
  10.6 0.0 collective-permute-done.24
  10.6 0.1 pad_maximum_fusion.near_ref
  10.7 1.6 %collective-permute-start.27 = (bf16[16,3072]{1,0:T(8,128)(2,1)S(1)}, bf16[16,3072]{1,0:T(8,128)(2,1)S(1)}, u32[]{:S(2)}, u32[]{:S(2)}) collective-permute-start(bf16[16,3072]{1,0:T(8,128)(2,1)S(1)} %pad_maximum_fusion.near_ref), channel_id=1, source_target_pairs={{0,4},{4,0},{8,12},{12,8},{16,20},{20,16},{24,28},{28,24},{32,36},... | collective-permute-start | bytes 294920 | tf_op jit(solution)/shard_map/ppermute | solution.py:22
  12.3 0.9 %select_reduce_fusion = s32[32]{0:T(128)S(1)} fusion(s32[256]{0:T(256)} %param.18, s32[32]{0:T(128)S(1)} %fusion), kind=kLoop, calls=%fused_computation.1 | loop fusion | flops 24544 | bytes 1280 | tf_op jit(solution)/shard_map/reduce_sum | solution.py:375
  13.2 0.1 collective-permute-done.27.far_ref
  13.2 1.0 %shard_map.92._ = bf16[8,4,3072]{2,1,0:T(4,128)(2,1)} custom-call(bf16[16,3072]{1,0:T(8,128)(2,1)S(1)} %pad_maximum_fusion.near_ref, bf16[16,3072]{1,0:T(8,128)(2,1)S(1)} %collective-permute-done.27.far_ref, s32[1,32]{1,0:T(1,128)S(1)} %bitcast.4, s32[4,1]{1,0:T(4,128)S(1)} %copy.12.rest_0_.target_ref, s32[1,1]{1,0:T(1,128)} %bitcast.2.rest_1_), custom_call_target="tpu_custom_call" | custom-call | tf_op jit(solution)/shard_map/pallas_call | solution.py:96
  14.2 8.2 %all-to-all-start = ((bf16[8,4,3072]{2,1,0:T(4,128)(2,1)}), bf16[8,4,3072]{2,1,0:T(4,128)(2,1)S(1)}, u32[]{:S(2)}, u32[]{:S(2)}) async-start(bf16[8,4,3072]{2,1,0:T(4,128)(2,1)} %shard_map.92._), calls=%async_computation | async-start | bytes 393216 | tf_op jit(solution)/shard_map/all_to_all | solution.py:393
  22.4 1.0 %copy-done.1 = bf16[16,128,128]{2,1,0:T(8,128)(2,1)S(1)} copy-done((bf16[16,128,128]{2,1,0:T(8,128)(2,1)S(1)}, bf16[16,128,128]{2,1,0:T(8,128)(2,1)}, u32[]{:S(2)}) %copy-start.1) | copy-done | bytes 524312
  23.5 8.4 %all-to-all-done.arrived_ref = bf16[8,4,3072]{2,1,0:T(4,128)(2,1)S(1)} async-done(((bf16[8,4,3072]{2,1,0:T(4,128)(2,1)}), bf16[8,4,3072]{2,1,0:T(4,128)(2,1)S(1)}, u32[]{:S(2)}, u32[]{:S(2)}) %all-to-all-start) | async-done | bytes 196640 | tf_op jit(solution)/shard_map/all_to_all | solution.py:393
  31.9 0.4 shard_map.94
  32.3 22.9 %conditional.1 = (bf16[4,2048]{1,0:T(4,128)(2,1)S(1)}) conditional(s32[]{:T(128)} %clamp.3, (bf16[64,128]{1,0:T(8,128)(2,1)S(1)}, bf16[64,128]{1,0:T(8,128)(2,1)S(1)}, s32[4]{0:T(128)}, bf16[4,4096,128]{2,1,0:T(8,128)(2,1)}, bf16[4,16,4096]{2,1,0:T(8,128)(2,1)}, /*index=5*/bf16[16,128,128]{2,1,0:T(8,128)(2,1)}) %tuple.17, ...), branch_computations={%region_2.3_spmd, %region_3.4_spmd, %region_4.5_spmd, %region_5.6_... | conditional | bytes 6816020 | solution.py:409
  32.3 0.0 copy-start.4
  32.4 4.0 %branch_0_fun.3 = (f32[8,4608]{1,0:T(8,128)S(1)}, f32[8,4608]{1,0:T(8,128)S(1)}, f32[8,4608]{1,0:T(8,128)S(1)}, f32[8,4608]{1,0:T(8,128)S(1)}, s32[16,128]{1,0:T(8,128)S(1)}, /*index=5*/bf16[9216,128]{1,0:T(8,128)(2,1)S(1)}) custom-call(bf16[64,128]{1,0:T(8,128)(2,1)S(1)} %get-tuple-element.56.lat_ref, bf16[64,128]{1,0:T(8,128)(2,1)S(1)} %get-tuple-element.58.rope_ref, ...), custom_call_target="tpu_custom_call" | custom-call | tf_op jit(solution)/shard_map/cond/branch_0_fun/pallas_call | solution.py:217
  36.4 3.0 %collective-permute-start = (f32[8,4608]{1,0:T(8,128)S(1)}, f32[8,4608]{1,0:T(8,128)S(1)}, u32[]{:S(2)}, u32[]{:S(2)}) collective-permute-start(f32[8,4608]{1,0:T(8,128)S(1)} %get-tuple-element.64), channel_id=1, source_target_pairs={{0,2},{1,3},{2,0},{3,1},{4,6},{5,7},{6,4},{7,5},{8,10},{9,11},{10,... | collective-permute-start | bytes 442376 | tf_op jit(solution)/shard_map/cond/branch_0_fun/ppermute | solution.py:22
  39.3 0.4 collective-permute-start.1
  39.7 2.3 %collective-permute-start.2 = (f32[8,4608]{1,0:T(8,128)S(1)}, f32[8,4608]{1,0:T(8,128)S(1)}, u32[]{:S(2)}, u32[]{:S(2)}) collective-permute-start(f32[8,4608]{1,0:T(8,128)S(1)} %get-tuple-element.66), channel_id=1, source_target_pairs={{0,3},{1,0},{2,1},{3,2},{4,7},{5,4},{6,5},{7,6},{8,11},{9,8},{10,9... | collective-permute-start | bytes 442376 | tf_op jit(solution)/shard_map/cond/branch_0_fun/ppermute | solution.py:22
  42.0 0.0 collective-permute-done.refs_1_
  42.0 4.7 %collective-permute-done.1.refs_2_ = f32[8,4608]{1,0:T(8,128)S(1)} collective-permute-done((f32[8,4608]{1,0:T(8,128)S(1)}, f32[8,4608]{1,0:T(8,128)S(1)}, u32[]{:S(2)}, u32[]{:S(2)}) %collective-permute-start.1) | collective-permute-done | bytes 147488 | tf_op jit(solution)/shard_map/cond/branch_0_fun/ppermute | solution.py:22
  46.7 0.0 collective-permute-done.2.refs_3_
  46.7 0.7 branch_0_fun.4.refs_0_
  47.4 0.7 collective-permute-start.5
  48.0 2.4 %collective-permute-start.4 = (bf16[8,4608]{1,0:T(8,128)(2,1)S(1)}, bf16[8,4608]{1,0:T(8,128)(2,1)S(1)}, u32[]{:S(2)}, u32[]{:S(2)}) collective-permute-start(bf16[8,4608]{1,0:T(8,128)(2,1)S(1)} %branch_0_fun.4.refs_0_), channel_id=1, source_target_pairs={{0,1},{1,2},{2,3},{3,0},{4,5},{5,6},{6,7},{7,4},{8,9},{9,10},{10,1... | collective-permute-start | bytes 221192 | tf_op jit(solution)/shard_map/cond/branch_0_fun/ppermute | solution.py:22
  50.5 0.2 collective-permute-start.3
  50.7 1.5 %collective-permute-done.5.refs_3_ = bf16[8,4608]{1,0:T(8,128)(2,1)S(1)} collective-permute-done((bf16[8,4608]{1,0:T(8,128)(2,1)S(1)}, bf16[8,4608]{1,0:T(8,128)(2,1)S(1)}, u32[]{:S(2)}, u32[]{:S(2)}) %collective-permute-start.5) | collective-permute-done | bytes 73760 | tf_op jit(solution)/shard_map/cond/branch_0_fun/ppermute | solution.py:22
  52.2 0.7 collective-permute-done.4.refs_2_
  53.0 1.0 %collective-permute-done.3.refs_1_ = bf16[8,4608]{1,0:T(8,128)(2,1)S(1)} collective-permute-done((bf16[8,4608]{1,0:T(8,128)(2,1)S(1)}, bf16[8,4608]{1,0:T(8,128)(2,1)S(1)}, u32[]{:S(2)}, u32[]{:S(2)}) %collective-permute-start.3) | collective-permute-done | bytes 73760 | tf_op jit(solution)/shard_map/cond/branch_0_fun/ppermute | solution.py:22
  54.0 0.0 copy-done.4
  54.0 0.8 branch_0_fun.5
  55.3 0.5 collective-permute-start.30
  55.8 1.6 %collective-permute-start.29 = (bf16[4,2048]{1,0:T(4,128)(2,1)S(1)}, bf16[4,2048]{1,0:T(4,128)(2,1)S(1)}, u32[]{:S(2)}, u32[]{:S(2)}) collective-permute-start(bf16[4,2048]{1,0:T(4,128)(2,1)S(1)} %get-tuple-element.110.refs_0_), channel_id=1, source_target_pairs={{0,1},{1,2},{2,3},{3,0},{4,5},{5,6},{6,7},{7,4},{8,9},{9,10},{10,1... | collective-permute-start | bytes 49160 | tf_op jit(solution)/shard_map/ppermute | solution.py:22
  57.4 1.1 %collective-permute-start.28 = (bf16[4,2048]{1,0:T(4,128)(2,1)S(1)}, bf16[4,2048]{1,0:T(4,128)(2,1)S(1)}, u32[]{:S(2)}, u32[]{:S(2)}) collective-permute-start(bf16[4,2048]{1,0:T(4,128)(2,1)S(1)} %get-tuple-element.110.refs_0_), channel_id=1, source_target_pairs={{0,3},{1,0},{2,1},{3,2},{4,7},{5,4},{6,5},{7,6},{8,11},{9,8},{10,9... | collective-permute-start | bytes 49160 | tf_op jit(solution)/shard_map/ppermute | solution.py:22
  58.4 1.0 %collective-permute-done.30.refs_3_ = bf16[4,2048]{1,0:T(4,128)(2,1)S(1)} collective-permute-done((bf16[4,2048]{1,0:T(4,128)(2,1)S(1)}, bf16[4,2048]{1,0:T(4,128)(2,1)S(1)}, u32[]{:S(2)}, u32[]{:S(2)}) %collective-permute-start.30) | collective-permute-done | bytes 16416 | tf_op jit(solution)/shard_map/ppermute | solution.py:22
  59.4 0.2 collective-permute-done.29.refs_2_
  59.6 0.3 collective-permute-done.28.refs_1_
  59.9 0.0 copy-done
  59.9 0.4 shard_map.95
  60.4 23.6 %all_to_all.10.all_ref = bf16[64,4,512]{2,1,0:T(4,128)(2,1)S(1)} all-to-all(bf16[64,4,512]{2,1,0:T(4,128)(2,1)S(1)} %shard_map.95), channel_id=1, replica_groups=mesh['dp'=64,'rank'=4] {'dp'}, dimensions={0} | all-to-all | bytes 524288 | tf_op jit(solution)/shard_map/all_to_all | solution.py:421
  84.0 0.9 %shard_map.96 = bf16[4,512]{1,0:T(4,128)(2,1)} custom-call(bf16[64,4,512]{2,1,0:T(4,128)(2,1)S(1)} %all_to_all.10.all_ref, s32[4,1]{1,0:T(4,128)S(1)} %copy.12.rest_0_.target_ref), custom_call_target="tpu_custom_call" | custom-call | tf_op jit(solution)/shard_map/pallas_call | solution.py:350
  (7 shorter events, 0.1 us)
Async XLA Ops:
  0.0 0.7 copy-start.2
  0.7 0.7 copy-start.3
  1.5 9.2 %collective-permute-start.26 = (bf16[4,3072]{1,0:T(4,128)(2,1)S(1)}, bf16[4,3072]{1,0:T(4,128)(2,1)S(1)}, u32[]{:S(2)}, u32[]{:S(2)}) collective-permute-start(bf16[4,3072]{1,0:T(4,128)(2,1)S(1)} %shard_map.91), channel_id=1, source_target_pairs={{0,16},{8,24},{16,0},{24,8},{4,20},{12,28},{20,4},{28,12},{32,48},... | collective-permute-start | bytes 73736 | tf_op jit(solution)/shard_map/ppermute | solution.py:22
  5.1 5.5 %collective-permute-start.25 = (bf16[4,3072]{1,0:T(4,128)(2,1)S(1)}, bf16[4,3072]{1,0:T(4,128)(2,1)S(1)}, u32[]{:S(2)}, u32[]{:S(2)}) collective-permute-start(bf16[4,3072]{1,0:T(4,128)(2,1)S(1)} %shard_map.91), channel_id=1, source_target_pairs={{0,8},{8,16},{16,24},{24,0},{4,12},{12,20},{20,28},{28,4},{32,40},... | collective-permute-start | bytes 73736 | tf_op jit(solution)/shard_map/ppermute | solution.py:22
  5.4 5.2 %collective-permute-start.24 = (bf16[4,3072]{1,0:T(4,128)(2,1)S(1)}, bf16[4,3072]{1,0:T(4,128)(2,1)S(1)}, u32[]{:S(2)}, u32[]{:S(2)}) collective-permute-start(bf16[4,3072]{1,0:T(4,128)(2,1)S(1)} %shard_map.91), channel_id=1, source_target_pairs={{0,24},{8,0},{16,8},{24,16},{4,28},{12,4},{20,12},{28,20},{32,56},... | collective-permute-start | bytes 73736 | tf_op jit(solution)/shard_map/ppermute | solution.py:22
  10.7 2.5 %collective-permute-start.27 = (bf16[16,3072]{1,0:T(8,128)(2,1)S(1)}, bf16[16,3072]{1,0:T(8,128)(2,1)S(1)}, u32[]{:S(2)}, u32[]{:S(2)}) collective-permute-start(bf16[16,3072]{1,0:T(8,128)(2,1)S(1)} %pad_maximum_fusion.near_ref), channel_id=1, source_target_pairs={{0,4},{4,0},{8,12},{12,8},{16,20},{20,16},{24,28},{28,24},{32,36},... | collective-permute-start | bytes 294920 | tf_op jit(solution)/shard_map/ppermute | solution.py:22
  14.2 17.7 %all-to-all-start = ((bf16[8,4,3072]{2,1,0:T(4,128)(2,1)}), bf16[8,4,3072]{2,1,0:T(4,128)(2,1)S(1)}, u32[]{:S(2)}, u32[]{:S(2)}) async-start(bf16[8,4,3072]{2,1,0:T(4,128)(2,1)} %shard_map.92._), calls=%async_computation | async-start | bytes 393216 | tf_op jit(solution)/shard_map/all_to_all | solution.py:393
  22.4 1.0 %copy-start.1 = (bf16[16,128,128]{2,1,0:T(8,128)(2,1)S(1)}, bf16[16,128,128]{2,1,0:T(8,128)(2,1)}, u32[]{:S(2)}) copy-start(bf16[16,128,128]{2,1,0:T(8,128)(2,1)} %array_ref.1) | copy-start | bytes 1572868
  32.3 27.6 %copy-start = (bf16[2048,512]{1,0:T(8,128)(2,1)S(1)}, bf16[2048,512]{1,0:T(8,128)(2,1)}, u32[]{:S(2)}) copy-start(bf16[2048,512]{1,0:T(8,128)(2,1)} %refs_4_.1) | copy-start | bytes 6291460
  32.3 21.6 %copy-start.4 = (bf16[16,128,128]{2,1,0:T(8,128)(2,1)S(1)}, bf16[16,128,128]{2,1,0:T(8,128)(2,1)}, u32[]{:S(2)}) copy-start(bf16[16,128,128]{2,1,0:T(8,128)(2,1)} %get-tuple-element.69.refs_6_) | copy-start | bytes 1572868 | tf_op jit(solution)/shard_map/cond
  36.4 5.7 %collective-permute-start = (f32[8,4608]{1,0:T(8,128)S(1)}, f32[8,4608]{1,0:T(8,128)S(1)}, u32[]{:S(2)}, u32[]{:S(2)}) collective-permute-start(f32[8,4608]{1,0:T(8,128)S(1)} %get-tuple-element.64), channel_id=1, source_target_pairs={{0,2},{1,3},{2,0},{3,1},{4,6},{5,7},{6,4},{7,5},{8,10},{9,11},{10,... | collective-permute-start | bytes 442376 | tf_op jit(solution)/shard_map/cond/branch_0_fun/ppermute | solution.py:22
  39.3 7.3 %collective-permute-start.1 = (f32[8,4608]{1,0:T(8,128)S(1)}, f32[8,4608]{1,0:T(8,128)S(1)}, u32[]{:S(2)}, u32[]{:S(2)}) collective-permute-start(f32[8,4608]{1,0:T(8,128)S(1)} %get-tuple-element.65), channel_id=1, source_target_pairs={{0,1},{1,2},{2,3},{3,0},{4,5},{5,6},{6,7},{7,4},{8,9},{9,10},{10,1... | collective-permute-start | bytes 442376 | tf_op jit(solution)/shard_map/cond/branch_0_fun/ppermute | solution.py:22
  39.7 6.9 %collective-permute-start.2 = (f32[8,4608]{1,0:T(8,128)S(1)}, f32[8,4608]{1,0:T(8,128)S(1)}, u32[]{:S(2)}, u32[]{:S(2)}) collective-permute-start(f32[8,4608]{1,0:T(8,128)S(1)} %get-tuple-element.66), channel_id=1, source_target_pairs={{0,3},{1,0},{2,1},{3,2},{4,7},{5,4},{6,5},{7,6},{8,11},{9,8},{10,9... | collective-permute-start | bytes 442376 | tf_op jit(solution)/shard_map/cond/branch_0_fun/ppermute | solution.py:22
  47.4 4.8 %collective-permute-start.5 = (bf16[8,4608]{1,0:T(8,128)(2,1)S(1)}, bf16[8,4608]{1,0:T(8,128)(2,1)S(1)}, u32[]{:S(2)}, u32[]{:S(2)}) collective-permute-start(bf16[8,4608]{1,0:T(8,128)(2,1)S(1)} %branch_0_fun.4.refs_0_), channel_id=1, source_target_pairs={{0,2},{1,3},{2,0},{3,1},{4,6},{5,7},{6,4},{7,5},{8,10},{9,11},{10,... | collective-permute-start | bytes 221192 | tf_op jit(solution)/shard_map/cond/branch_0_fun/ppermute | solution.py:22
  48.0 4.9 %collective-permute-start.4 = (bf16[8,4608]{1,0:T(8,128)(2,1)S(1)}, bf16[8,4608]{1,0:T(8,128)(2,1)S(1)}, u32[]{:S(2)}, u32[]{:S(2)}) collective-permute-start(bf16[8,4608]{1,0:T(8,128)(2,1)S(1)} %branch_0_fun.4.refs_0_), channel_id=1, source_target_pairs={{0,1},{1,2},{2,3},{3,0},{4,5},{5,6},{6,7},{7,4},{8,9},{9,10},{10,1... | collective-permute-start | bytes 221192 | tf_op jit(solution)/shard_map/cond/branch_0_fun/ppermute | solution.py:22
  50.5 3.5 %collective-permute-start.3 = (bf16[8,4608]{1,0:T(8,128)(2,1)S(1)}, bf16[8,4608]{1,0:T(8,128)(2,1)S(1)}, u32[]{:S(2)}, u32[]{:S(2)}) collective-permute-start(bf16[8,4608]{1,0:T(8,128)(2,1)S(1)} %branch_0_fun.4.refs_0_), channel_id=1, source_target_pairs={{0,3},{1,0},{2,1},{3,2},{4,7},{5,4},{6,5},{7,6},{8,11},{9,8},{10,9... | collective-permute-start | bytes 221192 | tf_op jit(solution)/shard_map/cond/branch_0_fun/ppermute | solution.py:22
  55.3 4.2 %collective-permute-start.30 = (bf16[4,2048]{1,0:T(4,128)(2,1)S(1)}, bf16[4,2048]{1,0:T(4,128)(2,1)S(1)}, u32[]{:S(2)}, u32[]{:S(2)}) collective-permute-start(bf16[4,2048]{1,0:T(4,128)(2,1)S(1)} %get-tuple-element.110.refs_0_), channel_id=1, source_target_pairs={{0,2},{1,3},{2,0},{3,1},{4,6},{5,7},{6,4},{7,5},{8,10},{9,11},{10,... | collective-permute-start | bytes 49160 | tf_op jit(solution)/shard_map/ppermute | solution.py:22
  55.8 3.9 %collective-permute-start.29 = (bf16[4,2048]{1,0:T(4,128)(2,1)S(1)}, bf16[4,2048]{1,0:T(4,128)(2,1)S(1)}, u32[]{:S(2)}, u32[]{:S(2)}) collective-permute-start(bf16[4,2048]{1,0:T(4,128)(2,1)S(1)} %get-tuple-element.110.refs_0_), channel_id=1, source_target_pairs={{0,1},{1,2},{2,3},{3,0},{4,5},{5,6},{6,7},{7,4},{8,9},{9,10},{10,1... | collective-permute-start | bytes 49160 | tf_op jit(solution)/shard_map/ppermute | solution.py:22
  57.4 2.6 %collective-permute-start.28 = (bf16[4,2048]{1,0:T(4,128)(2,1)S(1)}, bf16[4,2048]{1,0:T(4,128)(2,1)S(1)}, u32[]{:S(2)}, u32[]{:S(2)}) collective-permute-start(bf16[4,2048]{1,0:T(4,128)(2,1)S(1)} %get-tuple-element.110.refs_0_), channel_id=1, source_target_pairs={{0,3},{1,0},{2,1},{3,2},{4,7},{5,4},{6,5},{7,6},{8,11},{9,8},{10,9... | collective-permute-start | bytes 49160 | tf_op jit(solution)/shard_map/ppermute | solution.py:22
